TPU v7x, 256 devices: a whole 4x4x8 slice. The times are simulated.
256 devices in a mesh: mem: 4 (over z_hi, core), lat: 64 (over z_lo, x, y).
Axes of the slice: x: 4, y: 4, z: 8 (z_hi: 2, z_lo: 4; z = z_hi * 4 + z_lo), core: 2. Of those that a mesh axis runs over, the one named last changes fastest.
Arguments:
- control: float32 [128, 128, 1024], P('mem', 'lat'), may hold values from -6 to 6
- ensemble: float32 [128, 4, 128, 1024], P('mem', None, 'lat'), may hold values from -0.72 to 0.72
- widths: int32 [128], P('lat'), may hold values from 0 to 4
- interp_source: int32 [4, 256, 2048], P(None, 'lat'), may hold values from 0 to 4095, as said below
- interp_weight: float32 [4, 256, 2048], P(None, 'lat'), may hold values from 0.1 to 0.5
- obs_mask: int32 [4, 256, 2048], P(None, 'lat'), may hold values 0 or 1
- innovation: float32 [4, 256, 2048], P(None, 'lat'), may hold values from -12 to 12
Outputs:
- control_next: float32 [128, 128, 1024], P('mem', 'lat')
Inputs may be any that keep to these rules, and one draw needn't show every extreme that they name: `interp_source`: for a fine point (j, i) in band b = j // 4 each value is (row - b * 2 + 1) * 1024 + column of a coarse cell inside the grid whose row differs from j // 2 by at most 1 and whose column differs from i // 2 by at most 2, cyclically modulo 1024.
All inputs are finite; a program needn't handle non-finite values. No bound on the sum of `obs_mask` on one device may be relied on, other than what follows from the above.
Results may differ from a plain program's by a relative error of at most 0.0001.
Values sent between devices are 32-bit elements; how exact they have to be, the bound alone decides.
No kernel may reach another device: no remote copies, remote signals or barrier semaphores. Data moves between devices by JAX's collectives and lax.ppermute only.
A program may use at most 128 MiB of HBM per device.

v0:
```python
import jax
import jax.numpy as jnp
from jax import lax
from jax.sharding import PartitionSpec as P

WIDEST = 4
GRAD_STEPS = 2


C_MID = 0.5
C_SIDE = 0.25
STEP_SIZE = 0.5
HIGHEST_PRECISION = lax.Precision.HIGHEST


def padded_2(cells, sides, width):
    for axis, dim in sides:
        count = lax.axis_size(axis)
        ends = count - 1
        head = lax.slice_in_dim(cells, 0, width, axis=dim)
        tail = lax.slice_in_dim(cells, cells.shape[dim] - width, cells.shape[dim], axis=dim)
        cells = jnp.concatenate(
            [
                lax.ppermute(tail, axis, [(i, (i + 1) % count) for i in range(ends)]),
                cells,
                lax.ppermute(head, axis, [((i + 1) % count, i) for i in range(ends)]),
            ],
            axis=dim,
        )
    return cells


def in_blocks(value, dim, devices):
    lengths = value.shape
    parts = value.reshape(*lengths[:dim], devices, lengths[dim] // devices, *lengths[dim + 1 :])
    return jnp.moveaxis(parts, dim, 0)


def summed_on_arrival(value, axis, dim):
    devices = lax.axis_size(axis)
    parts = lax.all_to_all(in_blocks(value, dim, devices), axis, 0, 0, tiled=True)
    return jnp.sum(parts, axis=0)


def in_order(parts, dim):
    parts = jnp.moveaxis(parts, 0, dim)
    lengths = parts.shape
    return parts.reshape(*lengths[:dim], lengths[dim] * lengths[dim + 1], *lengths[dim + 2 :])


def copy_for_each(value, axis):
    devices = lax.axis_size(axis)
    return lax.all_to_all(
        jnp.broadcast_to(value[None], (devices, *value.shape)), axis, 0, 0, tiled=True
    )


def gather_directly(value, axis, dim):
    return in_order(copy_for_each(value, axis), dim)


def lon_filter(source_field, widths):
    scaled = 1.0 / (2.0 * widths.astype(jnp.float32) + 1.0)
    summed = jnp.zeros_like(source_field)
    for offset in range(-WIDEST, WIDEST + 1):
        weight_row = jnp.where(abs(offset) <= widths, scaled, 0.0 * scaled)
        summed = summed + jnp.roll(source_field, offset, axis=-1) * weight_row[:, None]
    return summed


def lat_filter(source_field):
    padded = padded_2(source_field, (("lat", 1),), 1)
    return C_MID * source_field + C_SIDE * (padded[:, :-2] + padded[:, 2:])


def obs_stencil(fine_field):
    return (
        0.25 * jnp.roll(fine_field, 1, axis=-1)
        + 0.5 * fine_field
        + 0.25 * jnp.roll(fine_field, -1, axis=-1)
    )


def refine_field(coarse_part):
    slots, rows, cols = coarse_part.shape
    spread = jnp.broadcast_to(coarse_part[:, :, None, :, None], (slots, rows, 2, cols, 2))
    return spread.reshape(slots, 2 * rows, 2 * cols)


def coarsen_field(fine_portion):
    slots, rows, cols = fine_portion.shape
    return fine_portion.reshape(slots, rows // 2, 2, cols // 2, 2).sum(axis=(2, 4))


def offset_planes(interp_source, interp_weight, lon_count):
    fine_rows = interp_source.shape[1]
    fine_cols = interp_source.shape[2]
    input_row_index = interp_source // lon_count
    source_col = interp_source % lon_count
    parent_row = (jnp.arange(fine_rows, dtype=jnp.int32) // 2 + 1)[None, :, None]
    parent_col = (jnp.arange(fine_cols, dtype=jnp.int32) // 2)[None, None, :]
    row_shift = input_row_index - parent_row
    col_shift = (source_col - parent_col + 2) % lon_count - 2
    code = (row_shift + 1) * 5 + (col_shift + 2)
    planes = []
    for number in range(15):
        planes.append(jnp.sum(jnp.where(code == number, interp_weight, 0.0), axis=0))
    return planes


def local(control, ensemble, widths, interp_source, interp_weight, obs_mask, innovation):
    slot_count = ensemble.shape[1]
    count_of_rows = control.shape[1]
    lon_count = control.shape[2]
    obs_weight = obs_mask.astype(jnp.float32)
    slot_share = slot_count // lax.axis_size("mem")
    first_slot = lax.axis_index("mem") * slot_share
    obs_weight = lax.dynamic_slice_in_dim(obs_weight, first_slot, slot_share, 0)
    target = lax.dynamic_slice_in_dim(innovation, first_slot, slot_share, 0)
    planes = offset_planes(interp_source, interp_weight, lon_count)
    control_now = control
    for iteration in range(GRAD_STEPS):
        forward = lat_filter(lon_filter(control_now, widths))
        partial_sum = jnp.einsum("mtri,mri->tri", ensemble, forward, precision=HIGHEST_PRECISION)
        coarse = summed_on_arrival(partial_sum, "mem", 0)
        window = padded_2(coarse, (("lat", 1),), 1)
        fine_field = jnp.zeros((slot_share, 2 * count_of_rows, 2 * lon_count), jnp.float32)
        for row_shift in range(-1, 2):
            band_rows = window[:, 1 + row_shift : 1 + row_shift + count_of_rows]
            for col_shift in range(-2, 3):
                shifted = jnp.roll(band_rows, -col_shift, axis=-1)
                fine_field = fine_field + planes[(row_shift + 1) * 5 + col_shift + 2][
                    None
                ] * refine_field(shifted)
        misfit = obs_weight * (obs_stencil(fine_field) - target)
        fine_grid_return = obs_stencil(misfit)
        landed = jnp.zeros((slot_share, count_of_rows + 2, lon_count), jnp.float32)
        for row_shift in range(-1, 2):
            for col_shift in range(-2, 3):
                collected_return = coarsen_field(
                    planes[(row_shift + 1) * 5 + col_shift + 2][None] * fine_grid_return
                )
                rolled = jnp.roll(collected_return, col_shift, axis=-1)
                landed = landed + jnp.pad(rolled, ((0, 0), (1 + row_shift, 1 - row_shift), (0, 0)))
        rim_rows = jnp.concatenate([landed[:, :1], landed[:, -1:]], axis=1)
        arrived = padded_2(rim_rows, (("lat", 1),), 1)
        coarse_back = landed[:, 1:-1]
        coarse_back = coarse_back.at[:, 0].add(arrived[:, 0]).at[:, -1].add(arrived[:, 3])
        coarse_back = gather_directly(coarse_back, "mem", 0)
        member_back = jnp.einsum(
            "mtri,tri->mri", ensemble, coarse_back, precision=HIGHEST_PRECISION
        )
        gradient = control_now + lon_filter(lat_filter(member_back), widths)
        control_now = control_now - STEP_SIZE * gradient
    return control_now


def solution(mesh):
    in_specs = (
        P("mem", "lat", None),
        P("mem", None, "lat", None),
        P("lat"),
        P(None, "lat", None),
        P(None, "lat", None),
        P(None, "lat", None),
        P(None, "lat", None),
    )
    out_specs = P("mem", "lat", None)
    return jax.shard_map(local, mesh=mesh, in_specs=in_specs, out_specs=out_specs, check_vma=False)
```

profile of v0, /device:TPU:30, one launch (start us, length us, event | category | flops | bytes accessed | tf_op | source)
XLA Modules:
  0.0 437.2 jit_solution(13958686309939112678)
XLA Ops:
  8.8 3.4 collective-permute-start
  15.9 7.4 %collective-permute-done.1 = f32[32,1,1024]{2,1,0:T(1,128)S(1)} collective-permute-done((f32[32,1,1024]{2,1,0:T(1,128)S(1)}, f32[32,1,1024]{2,1,0:T(1,128)S(1)}, u32[]{:S(2)}, u32[]{:S(2)}) %collective-permute-start.1) | collective-permute-done | bytes 131104 | tf_op jit(solution)/shard_map/ppermute | solution.py:26
  25.0 7.6 %all-to-all-start = ((f32[4,1,2,1024]{3,2,1,0:T(2,128)}), f32[4,1,2,1024]{3,2,1,0:T(2,128)S(1)}, u32[]{:S(2)}, u32[]{:S(2)}) async-start(f32[4,1,2,1024]{3,2,1,0:T(2,128)} %bitcast.10), calls=%async_computation | async-start | bytes 65536 | tf_op jit(solution)/shard_map/all_to_all | solution.py:41
  34.2 6.2 %all-to-all-done = f32[4,1,2,1024]{3,2,1,0:T(2,128)S(1)} async-done(((f32[4,1,2,1024]{3,2,1,0:T(2,128)}), f32[4,1,2,1024]{3,2,1,0:T(2,128)S(1)}, u32[]{:S(2)}, u32[]{:S(2)}) %all-to-all-start) | async-done | bytes 32800 | tf_op jit(solution)/shard_map/all_to_all | solution.py:41
  42.9 4.1 collective-permute-start.3
  49.8 3.0 collective-permute-done.3
  95.3 3.2 reshape.1694
  100.1 2.8 reshape.1693
  104.6 2.8 reshape.1689
  109.0 2.8 reshape.1688
  113.5 2.8 reshape.1684
  117.9 2.8 reshape.1683
  122.4 2.8 reshape.1690
  126.2 2.8 reshape.1685
  130.2 2.8 reshape.1696
  137.9 2.8 reshape.1692
  152.0 2.8 reshape.1686
  162.7 3.1 collective-permute-start.4
  168.6 6.9 %collective-permute-done.5 = f32[1,1,1024]{2,1,0:T(1,128)S(1)} collective-permute-done((f32[1,1,1024]{2,1,0:T(1,128)S(1)}, f32[1,1,1024]{2,1,0:T(1,128)S(1)}, u32[]{:S(2)}, u32[]{:S(2)}) %collective-permute-start.5) | collective-permute-done | bytes 4128 | tf_op jit(solution)/shard_map/ppermute | solution.py:26
  175.6 10.4 %all_to_all.20 = f32[4,1,2,1024]{3,2,1,0:T(2,128)S(1)} all-to-all(f32[4,1,2,1024]{3,2,1,0:T(2,128)S(1)} %broadcast_in_dim.446), channel_id=1, replica_groups=mesh['mem'=4,'lat'=64] {'mem'}, dimensions={0} | all-to-all | bytes 65536 | tf_op jit(solution)/shard_map/all_to_all | solution.py:53
  188.7 3.9 collective-permute-start.7
  193.8 6.1 %collective-permute-done.7 = f32[32,1,1024]{2,1,0:T(1,128)S(1)} collective-permute-done((f32[32,1,1024]{2,1,0:T(1,128)S(1)}, f32[32,1,1024]{2,1,0:T(1,128)S(1)}, u32[]{:S(2)}, u32[]{:S(2)}) %collective-permute-start.7) | collective-permute-done | bytes 131104 | tf_op jit(solution)/shard_map/ppermute | solution.py:26
  210.1 3.9 collective-permute-start.9
  215.0 6.1 %collective-permute-done.9 = f32[32,1,1024]{2,1,0:T(1,128)S(1)} collective-permute-done((f32[32,1,1024]{2,1,0:T(1,128)S(1)}, f32[32,1,1024]{2,1,0:T(1,128)S(1)}, u32[]{:S(2)}, u32[]{:S(2)}) %collective-permute-start.9) | collective-permute-done | bytes 131104 | tf_op jit(solution)/shard_map/ppermute | solution.py:26
  222.2 10.2 %all_to_all.21 = f32[4,1,2,1024]{3,2,1,0:T(2,128)S(1)} all-to-all(f32[4,1,2,1024]{3,2,1,0:T(2,128)S(1)} %bitcast.398), channel_id=1, replica_groups=mesh['mem'=4,'lat'=64] {'mem'}, dimensions={0} | all-to-all | bytes 65536 | tf_op jit(solution)/shard_map/all_to_all | solution.py:41
  234.4 4.3 collective-permute-start.11
  273.5 3.0 broadcast_in_dim.449
  309.7 3.6 reshape.1711
  315.4 3.5 reshape.1710
  320.9 3.5 reshape.1706
  326.4 3.5 reshape.1705
  331.9 3.5 reshape.1701
  337.4 3.5 reshape.1700
  342.8 3.5 reshape.1707
  348.2 3.5 reshape.1702
  353.6 3.8 reshape.1713
  359.5 3.5 reshape.1712
  364.9 3.5 reshape.1709
  370.4 3.5 reshape.1708
  375.8 3.5 reshape.1704
  381.3 3.5 reshape.1703
  386.8 3.5 reshape.1714
  392.4 5.3 %collective-permute-start.12 = (f32[1,1,1024]{2,1,0:T(1,128)S(1)}, f32[1,1,1024]{2,1,0:T(1,128)S(1)}, u32[]{:S(2)}, u32[]{:S(2)}) collective-permute-start(f32[1,1,1024]{2,1,0:T(1,128)S(1)} %get-tuple-element.191), channel_id=1, source_target_pairs={{0,1},{1,2},{2,3},{3,4},{4,5},{5,6},{6,7},{7,8},{8,9},{9,10},{10,1... | collective-permute-start | bytes 12296 | tf_op jit(solution)/shard_map/ppermute | solution.py:24
  399.8 7.7 %collective-permute-done.13 = f32[1,1,1024]{2,1,0:T(1,128)S(1)} collective-permute-done((f32[1,1,1024]{2,1,0:T(1,128)S(1)}, f32[1,1,1024]{2,1,0:T(1,128)S(1)}, u32[]{:S(2)}, u32[]{:S(2)}) %collective-permute-start.13) | collective-permute-done | bytes 4128 | tf_op jit(solution)/shard_map/ppermute | solution.py:26
  407.6 10.2 %all_to_all.22 = f32[4,1,2,1024]{3,2,1,0:T(2,128)S(1)} all-to-all(f32[4,1,2,1024]{3,2,1,0:T(2,128)S(1)} %broadcast_in_dim.493), channel_id=1, replica_groups=mesh['mem'=4,'lat'=64] {'mem'}, dimensions={0} | all-to-all | bytes 65536 | tf_op jit(solution)/shard_map/all_to_all | solution.py:53
  420.4 4.1 collective-permute-start.15
  425.5 6.1 %collective-permute-done.15 = f32[32,1,1024]{2,1,0:T(1,128)S(1)} collective-permute-done((f32[32,1,1024]{2,1,0:T(1,128)S(1)}, f32[32,1,1024]{2,1,0:T(1,128)S(1)}, u32[]{:S(2)}, u32[]{:S(2)}) %collective-permute-start.15) | collective-permute-done | bytes 131104 | tf_op jit(solution)/shard_map/ppermute | solution.py:26
  434.0 3.0 multiply_subtract_fusion
  (330 shorter events, 225.3 us)
Async XLA Ops:
  0.0 6.3 %copy-start = (f32[32,2,1024]{2,1,0:T(2,128)S(1)}, f32[32,2,1024]{2,1,0:T(2,128)}, u32[]{:S(2)}) copy-start(f32[32,2,1024]{2,1,0:T(2,128)} %param.15) | copy-start | bytes 786436
  3.6 3.4 copy-start.36
  7.0 16.8 %copy-start.33 = (f32[2]{0:T(128)}, f32[2]{0:T(128)S(1)}, u32[]{:S(2)}) copy-start(f32[2]{0:T(128)S(1)} %get-tuple-element.72) | copy-start | bytes 28
  7.1 16.8 %copy-start.25 = (f32[2]{0:T(128)}, f32[2]{0:T(128)S(1)}, u32[]{:S(2)}) copy-start(f32[2]{0:T(128)S(1)} %get-tuple-element.268) | copy-start | bytes 28
  7.1 16.8 %copy-start.27 = (f32[2]{0:T(128)}, f32[2]{0:T(128)S(1)}, u32[]{:S(2)}) copy-start(f32[2]{0:T(128)S(1)} %get-tuple-element.269) | copy-start | bytes 28
  7.1 16.8 %copy-start.29 = (f32[2]{0:T(128)}, f32[2]{0:T(128)S(1)}, u32[]{:S(2)}) copy-start(f32[2]{0:T(128)S(1)} %get-tuple-element.270) | copy-start | bytes 28
  7.1 16.8 %copy-start.31 = (f32[2]{0:T(128)}, f32[2]{0:T(128)S(1)}, u32[]{:S(2)}) copy-start(f32[2]{0:T(128)S(1)} %get-tuple-element.271) | copy-start | bytes 28
  7.1 16.8 %copy-start.1 = (f32[32,4,2,1024]{3,2,1,0:T(2,128)S(1)}, f32[32,4,2,1024]{3,2,1,0:T(2,128)}, u32[]{:S(2)}) copy-start(f32[32,4,2,1024]{3,2,1,0:T(2,128)} %param.16) | copy-start | bytes 3145732
  7.1 25.4 %copy-start.13 = (f32[4,4,2048]{2,1,0:T(4,128)S(1)}, f32[4,4,2048]{2,1,0:T(4,128)}, u32[]{:S(2)}) copy-start(f32[4,4,2048]{2,1,0:T(4,128)} %param.19) | copy-start | bytes 393220
  7.1 25.4 %copy-start.14 = (s32[4,4,2048]{2,1,0:T(4,128)S(1)}, s32[4,4,2048]{2,1,0:T(4,128)}, u32[]{:S(2)}) copy-start(s32[4,4,2048]{2,1,0:T(4,128)} %param.18) | copy-start | bytes 393220
  8.8 7.1 %collective-permute-start = (f32[32,1,1024]{2,1,0:T(1,128)S(1)}, f32[32,1,1024]{2,1,0:T(1,128)S(1)}, u32[]{:S(2)}, u32[]{:S(2)}) collective-permute-start(f32[32,1,1024]{2,1,0:T(1,128)S(1)} %get-tuple-element.128), channel_id=1, source_target_pairs={{0,1},{1,2},{2,3},{3,4},{4,5},{5,6},{6,7},{7,8},{8,9},{9,10},{10,1... | collective-permute-start | bytes 393224 | tf_op jit(solution)/shard_map/ppermute | solution.py:24
  12.2 11.1 %collective-permute-start.1 = (f32[32,1,1024]{2,1,0:T(1,128)S(1)}, f32[32,1,1024]{2,1,0:T(1,128)S(1)}, u32[]{:S(2)}, u32[]{:S(2)}) collective-permute-start(f32[32,1,1024]{2,1,0:T(1,128)S(1)} %get-tuple-element.129), channel_id=1, source_target_pairs={{1,0},{2,1},{3,2},{4,3},{5,4},{6,5},{7,6},{8,7},{9,8},{10,9},{11,1... | collective-permute-start | bytes 393224 | tf_op jit(solution)/shard_map/ppermute | solution.py:26
  25.0 15.4 %all-to-all-start = ((f32[4,1,2,1024]{3,2,1,0:T(2,128)}), f32[4,1,2,1024]{3,2,1,0:T(2,128)S(1)}, u32[]{:S(2)}, u32[]{:S(2)}) async-start(f32[4,1,2,1024]{3,2,1,0:T(2,128)} %bitcast.10), calls=%async_computation | async-start | bytes 65536 | tf_op jit(solution)/shard_map/all_to_all | solution.py:41
  41.0 8.8 %collective-permute-start.2 = (f32[1,1,1024]{2,1,0:T(1,128)}, f32[1,1,1024]{2,1,0:T(1,128)S(1)}, u32[]{:S(2)}, u32[]{:S(2)}) collective-permute-start(f32[1,1,1024]{2,1,0:T(1,128)} %get-tuple-element.264), channel_id=1, source_target_pairs={{0,1},{1,2},{2,3},{3,4},{4,5},{5,6},{6,7},{7,8},{8,9},{9,10},{10,1... | collective-permute-start | bytes 12296 | tf_op jit(solution)/shard_map/ppermute | solution.py:24
  42.9 9.9 %collective-permute-start.3 = (f32[1,1,1024]{2,1,0:T(1,128)}, f32[1,1,1024]{2,1,0:T(1,128)S(1)}, u32[]{:S(2)}, u32[]{:S(2)}) collective-permute-start(f32[1,1,1024]{2,1,0:T(1,128)} %get-tuple-element.265), channel_id=1, source_target_pairs={{1,0},{2,1},{3,2},{4,3},{5,4},{6,5},{7,6},{8,7},{9,8},{10,9},{11,1... | collective-permute-start | bytes 12296 | tf_op jit(solution)/shard_map/ppermute | solution.py:26
  66.2 2.2 copy-start.24
  66.2 2.2 copy-start.35
  68.5 2.2 copy-start.21
  70.7 2.2 copy-start.22
  72.8 2.4 copy-start.23
  77.4 2.2 copy-start.19
  79.6 2.2 copy-start.18
  81.8 2.2 copy-start.17
  83.9 2.2 copy-start.16
  86.1 2.2 copy-start.15
  162.7 5.9 %collective-permute-start.4 = (f32[1,1,1024]{2,1,0:T(1,128)S(1)}, f32[1,1,1024]{2,1,0:T(1,128)S(1)}, u32[]{:S(2)}, u32[]{:S(2)}) collective-permute-start(f32[1,1,1024]{2,1,0:T(1,128)S(1)} %get-tuple-element.193), channel_id=1, source_target_pairs={{0,1},{1,2},{2,3},{3,4},{4,5},{5,6},{6,7},{7,8},{8,9},{9,10},{10,1... | collective-permute-start | bytes 12296 | tf_op jit(solution)/shard_map/ppermute | solution.py:24
  165.8 9.7 %collective-permute-start.5 = (f32[1,1,1024]{2,1,0:T(1,128)S(1)}, f32[1,1,1024]{2,1,0:T(1,128)S(1)}, u32[]{:S(2)}, u32[]{:S(2)}) collective-permute-start(f32[1,1,1024]{2,1,0:T(1,128)S(1)} %get-tuple-element.192), channel_id=1, source_target_pairs={{1,0},{2,1},{3,2},{4,3},{5,4},{6,5},{7,6},{8,7},{9,8},{10,9},{11,1... | collective-permute-start | bytes 12296 | tf_op jit(solution)/shard_map/ppermute | solution.py:26
  186.8 7.0 %collective-permute-start.6 = (f32[32,1,1024]{2,1,0:T(1,128)S(1)}, f32[32,1,1024]{2,1,0:T(1,128)S(1)}, u32[]{:S(2)}, u32[]{:S(2)}) collective-permute-start(f32[32,1,1024]{2,1,0:T(1,128)S(1)} %get-tuple-element.126), channel_id=1, source_target_pairs={{0,1},{1,2},{2,3},{3,4},{4,5},{5,6},{6,7},{7,8},{8,9},{9,10},{10,1... | collective-permute-start | bytes 393224 | tf_op jit(solution)/shard_map/ppermute | solution.py:24
  188.7 11.2 %collective-permute-start.7 = (f32[32,1,1024]{2,1,0:T(1,128)S(1)}, f32[32,1,1024]{2,1,0:T(1,128)S(1)}, u32[]{:S(2)}, u32[]{:S(2)}) collective-permute-start(f32[32,1,1024]{2,1,0:T(1,128)S(1)} %get-tuple-element.127), channel_id=1, source_target_pairs={{1,0},{2,1},{3,2},{4,3},{5,4},{6,5},{7,6},{8,7},{9,8},{10,9},{11,1... | collective-permute-start | bytes 393224 | tf_op jit(solution)/shard_map/ppermute | solution.py:26
  208.1 6.9 %collective-permute-start.8 = (f32[32,1,1024]{2,1,0:T(1,128)S(1)}, f32[32,1,1024]{2,1,0:T(1,128)S(1)}, u32[]{:S(2)}, u32[]{:S(2)}) collective-permute-start(f32[32,1,1024]{2,1,0:T(1,128)S(1)} %get-tuple-element.92), channel_id=1, source_target_pairs={{0,1},{1,2},{2,3},{3,4},{4,5},{5,6},{6,7},{7,8},{8,9},{9,10},{10,1... | collective-permute-start | bytes 393224 | tf_op jit(solution)/shard_map/ppermute | solution.py:24
  210.1 11.1 %collective-permute-start.9 = (f32[32,1,1024]{2,1,0:T(1,128)S(1)}, f32[32,1,1024]{2,1,0:T(1,128)S(1)}, u32[]{:S(2)}, u32[]{:S(2)}) collective-permute-start(f32[32,1,1024]{2,1,0:T(1,128)S(1)} %get-tuple-element.93), channel_id=1, source_target_pairs={{1,0},{2,1},{3,2},{4,3},{5,4},{6,5},{7,6},{8,7},{9,8},{10,9},{11,1... | collective-permute-start | bytes 393224 | tf_op jit(solution)/shard_map/ppermute | solution.py:26
  232.4 10.8 %collective-permute-start.10 = (f32[1,1,1024]{2,1,0:T(1,128)S(1)}, f32[1,1,1024]{2,1,0:T(1,128)S(1)}, u32[]{:S(2)}, u32[]{:S(2)}) collective-permute-start(f32[1,1,1024]{2,1,0:T(1,128)S(1)} %get-tuple-element.245), channel_id=1, source_target_pairs={{0,1},{1,2},{2,3},{3,4},{4,5},{5,6},{6,7},{7,8},{8,9},{9,10},{10,1... | collective-permute-start | bytes 12296 | tf_op jit(solution)/shard_map/ppermute | solution.py:24
  234.4 9.7 %collective-permute-start.11 = (f32[1,1,1024]{2,1,0:T(1,128)S(1)}, f32[1,1,1024]{2,1,0:T(1,128)S(1)}, u32[]{:S(2)}, u32[]{:S(2)}) collective-permute-start(f32[1,1,1024]{2,1,0:T(1,128)S(1)} %get-tuple-element.246), channel_id=1, source_target_pairs={{1,0},{2,1},{3,2},{4,3},{5,4},{6,5},{7,6},{8,7},{9,8},{10,9},{11,1... | collective-permute-start | bytes 12296 | tf_op jit(solution)/shard_map/ppermute | solution.py:26
  303.5 4.6 %copy-start.2 = (f32[4,2048]{1,0:T(4,128)S(1)}, f32[4,2048]{1,0:T(4,128)}, u32[]{:S(2)}) copy-start(f32[4,2048]{1,0:T(4,128)} %get-tuple-element.56) | copy-start | bytes 98308
  303.5 4.6 %copy-start.3 = (f32[4,2048]{1,0:T(4,128)S(1)}, f32[4,2048]{1,0:T(4,128)}, u32[]{:S(2)}) copy-start(f32[4,2048]{1,0:T(4,128)} %get-tuple-element.57) | copy-start | bytes 98308
  303.5 4.6 %copy-start.4 = (f32[4,2048]{1,0:T(4,128)S(1)}, f32[4,2048]{1,0:T(4,128)}, u32[]{:S(2)}) copy-start(f32[4,2048]{1,0:T(4,128)} %get-tuple-element.58) | copy-start | bytes 98308
  303.6 4.6 %copy-start.5 = (f32[4,2048]{1,0:T(4,128)S(1)}, f32[4,2048]{1,0:T(4,128)}, u32[]{:S(2)}) copy-start(f32[4,2048]{1,0:T(4,128)} %get-tuple-element.59) | copy-start | bytes 98308
  303.6 4.6 %copy-start.6 = (f32[4,2048]{1,0:T(4,128)S(1)}, f32[4,2048]{1,0:T(4,128)}, u32[]{:S(2)}) copy-start(f32[4,2048]{1,0:T(4,128)} %get-tuple-element.60) | copy-start | bytes 98308
  303.6 4.6 %copy-start.7 = (f32[4,2048]{1,0:T(4,128)S(1)}, f32[4,2048]{1,0:T(4,128)}, u32[]{:S(2)}) copy-start(f32[4,2048]{1,0:T(4,128)} %get-tuple-element.61) | copy-start | bytes 98308
  303.6 4.6 %copy-start.8 = (f32[4,2048]{1,0:T(4,128)S(1)}, f32[4,2048]{1,0:T(4,128)}, u32[]{:S(2)}) copy-start(f32[4,2048]{1,0:T(4,128)} %get-tuple-element.62) | copy-start | bytes 98308
  303.6 4.6 %copy-start.9 = (f32[4,2048]{1,0:T(4,128)S(1)}, f32[4,2048]{1,0:T(4,128)}, u32[]{:S(2)}) copy-start(f32[4,2048]{1,0:T(4,128)} %get-tuple-element.63) | copy-start | bytes 98308
  303.6 4.6 %copy-start.10 = (f32[4,2048]{1,0:T(4,128)S(1)}, f32[4,2048]{1,0:T(4,128)}, u32[]{:S(2)}) copy-start(f32[4,2048]{1,0:T(4,128)} %get-tuple-element.65) | copy-start | bytes 98308
  303.6 4.6 %copy-start.11 = (f32[4,2048]{1,0:T(4,128)S(1)}, f32[4,2048]{1,0:T(4,128)}, u32[]{:S(2)}) copy-start(f32[4,2048]{1,0:T(4,128)} %get-tuple-element.66) | copy-start | bytes 98308
  303.6 4.6 %copy-start.12 = (f32[4,2048]{1,0:T(4,128)S(1)}, f32[4,2048]{1,0:T(4,128)}, u32[]{:S(2)}) copy-start(f32[4,2048]{1,0:T(4,128)} %get-tuple-element.67) | copy-start | bytes 98308
  392.4 7.3 %collective-permute-start.12 = (f32[1,1,1024]{2,1,0:T(1,128)S(1)}, f32[1,1,1024]{2,1,0:T(1,128)S(1)}, u32[]{:S(2)}, u32[]{:S(2)}) collective-permute-start(f32[1,1,1024]{2,1,0:T(1,128)S(1)} %get-tuple-element.191), channel_id=1, source_target_pairs={{0,1},{1,2},{2,3},{3,4},{4,5},{5,6},{6,7},{7,8},{8,9},{9,10},{10,1... | collective-permute-start | bytes 12296 | tf_op jit(solution)/shard_map/ppermute | solution.py:24
  397.7 9.7 %collective-permute-start.13 = (f32[1,1,1024]{2,1,0:T(1,128)S(1)}, f32[1,1,1024]{2,1,0:T(1,128)S(1)}, u32[]{:S(2)}, u32[]{:S(2)}) collective-permute-start(f32[1,1,1024]{2,1,0:T(1,128)S(1)} %get-tuple-element.190), channel_id=1, source_target_pairs={{1,0},{2,1},{3,2},{4,3},{5,4},{6,5},{7,6},{8,7},{9,8},{10,9},{11,1... | collective-permute-start | bytes 12296 | tf_op jit(solution)/shard_map/ppermute | solution.py:26
  418.5 7.0 %collective-permute-start.14 = (f32[32,1,1024]{2,1,0:T(1,128)S(1)}, f32[32,1,1024]{2,1,0:T(1,128)S(1)}, u32[]{:S(2)}, u32[]{:S(2)}) collective-permute-start(f32[32,1,1024]{2,1,0:T(1,128)S(1)} %get-tuple-element.90), channel_id=1, source_target_pairs={{0,1},{1,2},{2,3},{3,4},{4,5},{5,6},{6,7},{7,8},{8,9},{9,10},{10,1... | collective-permute-start | bytes 393224 | tf_op jit(solution)/shard_map/ppermute | solution.py:24
  420.4 11.2 %collective-permute-start.15 = (f32[32,1,1024]{2,1,0:T(1,128)S(1)}, f32[32,1,1024]{2,1,0:T(1,128)S(1)}, u32[]{:S(2)}, u32[]{:S(2)}) collective-permute-start(f32[32,1,1024]{2,1,0:T(1,128)S(1)} %get-tuple-element.91), channel_id=1, source_target_pairs={{1,0},{2,1},{3,2},{4,3},{5,4},{6,5},{7,6},{8,7},{9,8},{10,9},{11,1... | collective-permute-start | bytes 393224 | tf_op jit(solution)/shard_map/ppermute | solution.py:26
  (6 other events, 9.3 us)
where the time goes:
time: 445 us; the launch traced here: 437 us
  local copies, waits for them, and re-layouts  225 us (51%)
  other arithmetic  68.3 us (15%)
  starting transfers between devices  56.4 us (13%)
  waiting for transfers between devices  54.9 us (12%)
  blocking collectives  30.8 us (7%)
    broadcast_in_dim x60, local copies, waits for them, and re-layouts, refine_field(): jnp.broadcast_to(coarse_part[:, :, None, :, None], (slots, rows, 2, cols,...  100 us
    reshape x30, local copies, waits for them, and re-layouts, coarsen_field(): fine_portion.reshape(slots, rows // 2, 2, cols // 2, 2).sum(axis=(2, 4))  95.4 us
    ppermute x8, waiting for transfers between devices, padded_2(): lax.ppermute(head, axis, [((i + 1) % count, i) for i in range(ends)])  44.3 us
    reduce_sum x30, other arithmetic, coarsen_field(): fine_portion.reshape(slots, rows // 2, 2, cols // 2, 2).sum(axis=(2, 4))  38.8 us
    ppermute x8, starting transfers between devices, padded_2(): lax.ppermute(head, axis, [((i + 1) % count, i) for i in range(ends)])  27.5 us
    ppermute x8, starting transfers between devices, padded_2(): lax.ppermute(tail, axis, [(i, (i + 1) % count) for i in range(ends)])  21.4 us
    all_to_all x2, blocking collectives, copy_for_each(): lax.all_to_all(jnp.broadcast_to(value[None], (devices, *value.shape)), ax...  20.6 us
    slice x36, local copies, waits for them, and re-layouts, local(): rolled = jnp.roll(collected_return, col_shift, axis=-1)  14.3 us
  transfers between devices with their start and end apart: 17, of which 13 were waited for; matrix products, arithmetic and copies ran while one was open for 2% of the time, Pallas kernels for 0%

commit v1 on v0

v1 whole, which is shorter than its diff:
```python
import jax
import jax.numpy as jnp
from jax import lax
from jax.experimental import pallas as pl
from jax.experimental.pallas import tpu as pltpu
from jax.sharding import PartitionSpec as P

WIDEST = 4
STEP_SIZE = 0.5
C_MID = 0.5
C_SIDE = 0.25

F32 = jnp.float32
LIMIT = 40 * 1024 * 1024


def shape(*dims):
    return jax.ShapeDtypeStruct(dims, F32)


def call(kernel, outs, args, scalars=(), flops=1_000_000):
    in_specs = [pl.BlockSpec(memory_space=pltpu.SMEM)] * len(scalars)
    in_specs += [pl.BlockSpec(memory_space=pltpu.VMEM)] * len(args)
    args = tuple(scalars) + tuple(args)
    return pl.pallas_call(
        kernel,
        out_shape=outs,
        in_specs=in_specs,
        out_specs=jax.tree.map(lambda _: pl.BlockSpec(memory_space=pltpu.VMEM), outs),
        compiler_params=pltpu.CompilerParams(vmem_limit_bytes=LIMIT),
        cost_estimate=pl.CostEstimate(flops=flops, transcendentals=0, bytes_accessed=1_000_000),
    )(*args)


def iota(shape_, dim):
    return lax.broadcasted_iota(jnp.int32, shape_, dim)


def shifted(x, k):
    nd = x.ndim
    turned = pltpu.roll(x, k % 128, nd - 1)
    lane = iota(x.shape, nd - 1)
    if k > 0:
        return jnp.where(lane < k, pltpu.roll(turned, 1, nd - 2), turned)
    return jnp.where(lane >= 128 + k, pltpu.roll(turned, 7, nd - 2), turned)


def tap_weights(widths_ref, r):
    width = jnp.full((8, 128), widths_ref[r], jnp.int32)
    scaled = 1.0 / (2.0 * width.astype(F32) + 1.0)
    return [jnp.where(k <= width, scaled, 0.0) for k in range(WIDEST + 1)]


def if_inside(place_ref, above, below):
    band = jnp.full((8, 128), place_ref[0], jnp.int32)
    last = jnp.full((8, 128), place_ref[1], jnp.int32)
    return jnp.where(band > 0, above, 0.0), jnp.where(band < last, below, 0.0)


def lon_filter(x, taps):
    total = x * taps[0]
    for k in range(1, WIDEST + 1):
        total = total + (shifted(x, k) + shifted(x, -k)) * taps[k]
    return total


def filter_kernel(widths_ref, v_ref, w0_ref, w1_ref):
    for r, out in ((0, w0_ref), (1, w1_ref)):
        taps = tap_weights(widths_ref, r)

        def body(b, carry, r=r, out=out, taps=taps):
            x = v_ref[pl.ds(b * 4, 4), pl.ds(r, 8, stride=2), :]
            out[pl.ds(b * 4, 4)] = lon_filter(x, taps)
            return carry

        lax.fori_loop(0, 8, body, 0)


def split_kernel(e_ref, e0_ref, e1_ref):
    def body(b, carry):
        at = pl.ds(b * 8, 8)
        e0_ref[at] = e_ref[at, pl.ds(0, 8, stride=2), :]
        e1_ref[at] = e_ref[at, pl.ds(1, 8, stride=2), :]
        return carry

    lax.fori_loop(0, 16, body, 0)


def planes_kernel(src_ref, wgt_ref, msk_ref, inn_ref, planes_ref, mask_ref, target_ref):
    parent = iota((8, 128), 0) * 128 + iota((8, 128), 1) // 2
    for j in range(8):
        half, fr = j // 4, j % 4
        at = pl.ds(j, 8, stride=8)
        codes, weights = [], []
        for s in range(4):
            src = src_ref[s, at, :]
            row_shift = lax.shift_right_logical(src, 10) - (fr // 2 + 1)
            col = jnp.bitwise_and(src, 1023)
            col_shift = jnp.bitwise_and(col - parent - half * 64 + 2, 1023) - 2
            codes.append((row_shift + 1) * 5 + col_shift + 2)
            weights.append(wgt_ref[s, at, :])
        for n in range(15):
            total = jnp.where(codes[0] == n, weights[0], 0.0)
            for s in range(1, 4):
                total = total + jnp.where(codes[s] == n, weights[s], 0.0)
            planes_ref[n, j] = total
        for t in range(4):
            mask_ref[t, j] = msk_ref[t, at, :].astype(F32)
            target_ref[t, j] = inn_ref[t, at, :]


def first_kernel(place_ref, w0_ref, w1_ref, above_ref, below_ref, e0_ref, e1_ref, part_ref):
    def body(m, sums):
        a, b = w0_ref[m], w1_ref[m]
        above, below = if_inside(place_ref, above_ref[m], below_ref[m])
        f0 = C_MID * a + C_SIDE * (above + b)
        f1 = C_MID * b + C_SIDE * (a + below)
        sums = list(sums)
        for t in range(4):
            sums[t] = sums[t] + e0_ref[m * 4 + t] * f0
            sums[4 + t] = sums[4 + t] + e1_ref[m * 4 + t] * f1
        return tuple(sums)

    sums = lax.fori_loop(0, 32, body, (jnp.zeros((8, 128), F32),) * 8, unroll=4)
    for n in range(8):
        part_ref[n] = sums[n]


def sum_kernel(parts_ref, a_ref, b_ref):
    count = a_ref.shape[0]
    for n in range(2 * count):
        total = (parts_ref[0, n] + parts_ref[1, n]) + (parts_ref[2, n] + parts_ref[3, n])
        if n < count:
            a_ref[n] = total
        else:
            b_ref[n - count] = total


def lanes(x, index):
    return jnp.take_along_axis(x, index, axis=1)


def stencil(a, b):
    lane = iota((8, 128), 1)
    a1, b1 = pltpu.roll(a, 1, 1), pltpu.roll(b, 1, 1)
    left_a = jnp.where(lane == 0, pltpu.roll(b1, 1, 0), a1)
    left_b = jnp.where(lane == 0, a1, b1)
    a2, b2 = pltpu.roll(a, 127, 1), pltpu.roll(b, 127, 1)
    right_a = jnp.where(lane == 127, b2, a2)
    right_b = jnp.where(lane == 127, pltpu.roll(a2, 7, 0), b2)
    return 0.5 * a + 0.25 * (left_a + right_a), 0.5 * b + 0.25 * (left_b + right_b)


def observe_slot(t, rows, planes_ref, mask_ref, target_ref):
    lane = iota((8, 128), 1)
    up = [lane // 2, lane // 2 + 64]
    down = jnp.bitwise_and(lane * 2, 127)
    fine = [None] * 8
    for q in range(4):
        for d in range(-2, 3):
            x = rows[q] if d == 0 else shifted(rows[q], -d)
            for half in range(2):
                u = lanes(x, up[half])
                for fr in range(4):
                    rs = q - 1 - fr // 2
                    if -1 <= rs <= 1:
                        j = half * 4 + fr
                        term = planes_ref[(rs + 1) * 5 + d + 2, j] * u
                        fine[j] = term if fine[j] is None else fine[j] + term
    back = [None] * 8
    for fr in range(4):
        a, b = stencil(fine[fr], fine[4 + fr])
        a = mask_ref[t, fr] * (a - target_ref[t, fr])
        b = mask_ref[t, 4 + fr] * (b - target_ref[t, 4 + fr])
        back[fr], back[4 + fr] = stencil(a, b)
    landed = []
    for q in range(4):
        total = None
        for d in range(-2, 3):
            halves = []
            for half in range(2):
                z = None
                for fr in range(4):
                    rs = q - 1 - fr // 2
                    if -1 <= rs <= 1:
                        j = half * 4 + fr
                        term = planes_ref[(rs + 1) * 5 + d + 2, j] * back[j]
                        z = term if z is None else z + term
                z = z + pltpu.roll(z, 127, 1)
                halves.append(lanes(z, down))
            w = jnp.where(lane < 64, halves[0], halves[1])
            w = w if d == 0 else shifted(w, d)
            total = w if total is None else total + w
        landed.append(total)
    return landed


def first_observe_kernel(above_ref, c0_ref, c1_ref, below_ref, planes_ref, mask_ref, target_ref, la_ref, lb_ref):
    for t in range(4):
        rows = [above_ref[t], c0_ref[t], c1_ref[t], below_ref[t]]
        landed = observe_slot(t, rows, planes_ref, mask_ref, target_ref)
        la_ref[t], la_ref[4 + t], lb_ref[t], lb_ref[4 + t] = landed


def second_observe_kernel(ca_ref, cb_ref, da_ref, db_ref, planes_ref, mask_ref, target_ref, la_ref, lb_ref):
    for t in range(4):
        rows = [
            ca_ref[t] + da_ref[t],
            ca_ref[4 + t] + da_ref[4 + t],
            cb_ref[t] + db_ref[t],
            cb_ref[4 + t] + db_ref[4 + t],
        ]
        landed = observe_slot(t, rows, planes_ref, mask_ref, target_ref)
        la_ref[t], la_ref[4 + t], lb_ref[t], lb_ref[4 + t] = landed


def member_back(e_ref, at, weights):
    x = e_ref[pl.ds(at * 16, 16)].reshape(4, 4, 8, 128)
    total = x[:, 0] * weights[0]
    for t in range(1, 4):
        total = total + x[:, t] * weights[t]
    return total


def adjoint_rows(place_ref, la_ref, lb_ref, ra_ref, rb_ref):
    rows = []
    for mine, theirs in ((la_ref, ra_ref), (lb_ref, rb_ref)):
        for half in range(2):
            rows.append([mine[half * 4 + t] + theirs[half * 4 + t] for t in range(4)])
    for t in range(4):
        rows[0][t], rows[3][t] = if_inside(place_ref, rows[0][t], rows[3][t])
    return rows


def descend(b, e_refs, rows, old, taps):
    back = [member_back(e_refs[q], b, rows[q]) for q in range(4)]
    fresh = []
    for r in range(2):
        smooth = C_MID * back[r + 1] + C_SIDE * (back[r] + back[r + 2])
        gradient = old[r] + lon_filter(smooth, taps[r])
        fresh.append(old[r] - STEP_SIZE * gradient)
    return fresh


def middle_kernel(widths_ref, place_ref, la_ref, lb_ref, ra_ref, rb_ref, em_ref, e0_ref, e1_ref, ep_ref, v_ref, new_ref, part_ref):
    rows = adjoint_rows(place_ref, la_ref, lb_ref, ra_ref, rb_ref)
    taps = [tap_weights(widths_ref, r) for r in range(2)]
    e_refs = (em_ref, e0_ref, e1_ref, ep_ref)
    part_ref[...] = jnp.zeros_like(part_ref)

    def body(b, carry):
        at = pl.ds(b * 4, 4)
        old = [v_ref[at, pl.ds(r, 8, stride=2), :] for r in range(2)]
        fresh = descend(b, e_refs, rows, old, taps)
        for r in range(2):
            new_ref[r, at] = fresh[r]
        w = [lon_filter(fresh[r], taps[r]) for r in range(2)]
        forward = [
            C_SIDE * w[0],
            C_MID * w[0] + C_SIDE * w[1],
            C_MID * w[1] + C_SIDE * w[0],
            C_SIDE * w[1],
        ]
        forward[0], forward[3] = if_inside(place_ref, forward[0], forward[3])
        for q in range(4):
            x = e_refs[q][pl.ds(b * 16, 16)].reshape(4, 4, 8, 128)
            for t in range(4):
                part_ref[q * 4 + t] += jnp.sum(x[:, t] * forward[q], axis=0)
        return carry

    lax.fori_loop(0, 8, body, 0)


def last_kernel(widths_ref, place_ref, la_ref, lb_ref, ra_ref, rb_ref, em_ref, e0_ref, e1_ref, ep_ref, v_ref, out_ref):
    rows = adjoint_rows(place_ref, la_ref, lb_ref, ra_ref, rb_ref)
    taps = [tap_weights(widths_ref, r) for r in range(2)]
    e_refs = (em_ref, e0_ref, e1_ref, ep_ref)

    def body(b, carry):
        at = pl.ds(b * 4, 4)
        old = [v_ref[r, at] for r in range(2)]
        fresh = descend(b, e_refs, rows, old, taps)
        for r in range(2):
            out_ref[at, pl.ds(r, 8, stride=2), :] = fresh[r]
        return carry

    lax.fori_loop(0, 8, body, 0)


def to_next(x):
    count = lax.axis_size("lat")
    return lax.ppermute(x, "lat", [(i, (i + 1) % count) for i in range(count)])


def to_previous(x):
    count = lax.axis_size("lat")
    return lax.ppermute(x, "lat", [((i + 1) % count, i) for i in range(count)])


def tiles(x):
    lead, (rows, cols) = x.shape[:-2], x.shape[-2:]
    x = x.reshape(-1, rows, cols // 128, 128).transpose(0, 2, 1, 3)
    return x.reshape(-1, cols // 128 * rows, 128)


def local(control, ensemble, widths, interp_source, interp_weight, obs_mask, innovation):
    v = tiles(control)
    e = tiles(ensemble)
    place = jnp.stack([lax.axis_index("lat"), lax.axis_size("lat") - 1]).astype(jnp.int32)
    row = shape(32, 8, 128)
    w0, w1 = call(filter_kernel, (row, row), (v,), (widths,))
    above, below = to_next(w1), to_previous(w0)
    e0, e1 = call(split_kernel, (shape(128, 8, 128),) * 2, (e,))
    e_above, e_below = to_next(e1), to_previous(e0)
    fields = call(
        planes_kernel,
        (shape(15, 8, 8, 128), shape(4, 8, 8, 128), shape(4, 8, 8, 128)),
        tuple(tiles(x) for x in (interp_source, interp_weight, obs_mask, innovation)),
    )
    part = call(first_kernel, shape(8, 8, 128), (w0, w1, above, below, e0, e1), (place,))
    four, eight = shape(4, 8, 128), shape(8, 8, 128)
    c0, c1 = call(sum_kernel, (four, four), (lax.all_gather(part, "mem"),))
    la, lb = call(
        first_observe_kernel, (eight, eight), (to_next(c1), c0, c1, to_previous(c0)) + tuple(fields)
    )
    ra, rb = to_next(lb), to_previous(la)
    new, part = call(
        middle_kernel,
        (shape(2, 32, 8, 128), shape(16, 8, 128)),
        (la, lb, ra, rb, e_above, e0, e1, e_below, v),
        (widths, place),
    )
    ca, cb = call(sum_kernel, (eight, eight), (lax.all_gather(part, "mem"),))
    la, lb = call(
        second_observe_kernel, (eight, eight), (ca, cb, to_next(cb), to_previous(ca)) + tuple(fields)
    )
    ra, rb = to_next(lb), to_previous(la)
    out = call(
        last_kernel,
        shape(32, 16, 128),
        (la, lb, ra, rb, e_above, e0, e1, e_below, new),
        (widths, place),
    )
    return out.reshape(32, 8, 2, 128).transpose(0, 2, 1, 3).reshape(control.shape)


def solution(mesh):
    in_specs = (
        P("mem", "lat", None),
        P("mem", None, "lat", None),
        P("lat"),
        P(None, "lat", None),
        P(None, "lat", None),
        P(None, "lat", None),
        P(None, "lat", None),
    )
    out_specs = P("mem", "lat", None)
    return jax.shard_map(local, mesh=mesh, in_specs=in_specs, out_specs=out_specs, check_vma=False)
```

time: 445 us -> 116 us (0.26)
  the two profiles are of different devices: /device:TPU:30 before, /device:TPU:1 now
where the time goes in v1:
time: 116 us; the launch traced here: 115 us
  waiting for transfers between devices  36 us (31%)
  starting transfers between devices  35 us (30%)
  blocking collectives  23.7 us (20%)
  Pallas kernels  18.6 us (16%)
  local copies, waits for them, and re-layouts  1.9 us (2%)
    ppermute x6, starting transfers between devices, to_previous(): return lax.ppermute(x, 'lat', [((i + 1) % count, i) for i in range(count)])  32.2 us
    ppermute x6, waiting for transfers between devices, to_next(): return lax.ppermute(x, 'lat', [(i, (i + 1) % count) for i in range(count)])  28.9 us
    pallas_call x10, Pallas kernels, call(): pl.pallas_call(kernel, out_shape=outs, in_specs=in_specs, out_specs=jax.t...  18.6 us
    all_gather x1, blocking collectives, local(): ca, cb = call(sum_kernel, (eight, eight), (lax.all_gather(part, 'mem'),))  12.5 us
    all_gather x1, blocking collectives, local(): c0, c1 = call(sum_kernel, (four, four), (lax.all_gather(part, 'mem'),))  11.1 us
    ppermute x6, waiting for transfers between devices, to_previous(): return lax.ppermute(x, 'lat', [((i + 1) % count, i) for i in range(count)])  7.15 us
    ppermute x6, starting transfers between devices, to_next(): return lax.ppermute(x, 'lat', [(i, (i + 1) % count) for i in range(count)])  2.79 us
  transfers between devices with their start and end apart: 12, of which 9 were waited for; matrix products, arithmetic and copies ran while one was open for 0% of the time, Pallas kernels for 7%

profile of v1, /device:TPU:1, one launch (start us, length us, event | category | flops | bytes accessed | tf_op | source)
XLA Modules:
  0.0 115.4 jit_solution(5246661126978842045)
XLA Ops:
  0.0 1.2 %copy-done.1 = f32[32,4,2,1024]{3,2,1,0:T(2,128)S(1)} copy-done((f32[32,4,2,1024]{3,2,1,0:T(2,128)S(1)}, f32[32,4,2,1024]{3,2,1,0:T(2,128)}, u32[]{:S(2)}) %copy-start.1) | copy-done | bytes 1048600
  1.2 0.0 copy-start
  1.2 0.1 shard_map.74
  1.4 9.9 %collective-permute-start.7 = (f32[128,8,128]{2,1,0:T(8,128)S(1)}, f32[128,8,128]{2,1,0:T(8,128)S(1)}, u32[]{:S(2)}, u32[]{:S(2)}) collective-permute-start(f32[128,8,128]{2,1,0:T(8,128)S(1)} %get-tuple-element.24.e0_ref), channel_id=1, source_target_pairs={{1,0},{2,1},{3,2},{4,3},{5,4},{6,5},{7,6},{8,7},{9,8},{10,9},{11,1... | collective-permute-start | bytes 1572872 | tf_op jit(solution)/shard_map/ppermute | solution.py:297
  11.2 0.0 copy-start.6
  11.2 0.0 collective-permute-start.6
  11.3 0.0 copy-done
  11.3 0.6 copy-done.6
  11.9 2.2 %shard_map.73 = (f32[32,8,128]{2,1,0:T(8,128)S(1)}, f32[32,8,128]{2,1,0:T(8,128)S(1)}) custom-call(s32[2]{0:T(128)S(1)} %copy-done.6, f32[32,16,128]{2,1,0:T(8,128)S(1)} %bitcast.38), custom_call_target="tpu_custom_call" | custom-call | flops 1000000 | bytes 1000000 | tf_op jit(solution)/shard_map/pallas_call | solution.py:25
  14.1 6.9 %collective-permute-start.1 = (f32[32,8,128]{2,1,0:T(8,128)S(1)}, f32[32,8,128]{2,1,0:T(8,128)S(1)}, u32[]{:S(2)}, u32[]{:S(2)}) collective-permute-start(f32[32,8,128]{2,1,0:T(8,128)S(1)} %get-tuple-element.22.w0_ref), channel_id=1, source_target_pairs={{1,0},{2,1},{3,2},{4,3},{5,4},{6,5},{7,6},{8,7},{9,8},{10,9},{11,1... | collective-permute-start | bytes 393224 | tf_op jit(solution)/shard_map/ppermute | solution.py:297
  21.1 0.0 collective-permute-start
  21.1 0.1 pad_add_fusion.place_ref
  21.1 3.5 %collective-permute-done.1.below_ref = f32[32,8,128]{2,1,0:T(8,128)S(1)} collective-permute-done((f32[32,8,128]{2,1,0:T(8,128)S(1)}, f32[32,8,128]{2,1,0:T(8,128)S(1)}, u32[]{:S(2)}, u32[]{:S(2)}) %collective-permute-start.1) | collective-permute-done | bytes 131104 | tf_op jit(solution)/shard_map/ppermute | solution.py:297
  24.7 7.9 %collective-permute-done.above_ref = f32[32,8,128]{2,1,0:T(8,128)S(1)} collective-permute-done((f32[32,8,128]{2,1,0:T(8,128)S(1)}, f32[32,8,128]{2,1,0:T(8,128)S(1)}, u32[]{:S(2)}, u32[]{:S(2)}) %collective-permute-start) | collective-permute-done | bytes 131104 | tf_op jit(solution)/shard_map/ppermute | solution.py:292
  32.6 0.0 copy-start.4
  32.6 0.0 copy-start.5
  32.6 0.7 shard_map.75
  33.3 0.0 copy-start.2
  33.3 0.0 copy-start.3
  33.3 11.1 %all-gather = f32[32,8,128]{2,1,0:T(8,128)S(1)} all-gather(f32[8,8,128]{2,1,0:T(8,128)S(1)} %shard_map.75), channel_id=2, replica_groups=mesh['mem'=4,'lat'=64] {'mem'}, dimensions={0}, use_global_device_ids=true | all-gather | bytes 163840 | tf_op jit(solution)/shard_map/all_gather | solution.py:322
  44.5 0.1 collective-permute-start.2
  44.6 7.5 %collective-permute-start.3 = (f32[4,8,128]{2,1,0:T(8,128)S(1)}, f32[4,8,128]{2,1,0:T(8,128)S(1)}, u32[]{:S(2)}, u32[]{:S(2)}) collective-permute-start(f32[4,8,128]{2,1,0:T(8,128)S(1)} %get-tuple-element.27.c0_ref), channel_id=1, source_target_pairs={{1,0},{2,1},{3,2},{4,3},{5,4},{6,5},{7,6},{8,7},{9,8},{10,9},{11,1... | collective-permute-start | bytes 49160 | tf_op jit(solution)/shard_map/ppermute | solution.py:297
  52.0 0.0 copy-done.4
  52.0 0.0 copy-done.5
  52.0 0.0 copy-done.2
  52.0 0.0 copy-done.3
  52.0 0.3 shard_map.77
  52.3 0.8 collective-permute-done.2.above_ref
  53.1 0.0 collective-permute-done.3.below_ref
  53.2 4.9 %shard_map.78 = (f32[8,8,128]{2,1,0:T(8,128)S(1)}, f32[8,8,128]{2,1,0:T(8,128)S(1)}) custom-call(f32[4,8,128]{2,1,0:T(8,128)S(1)} %collective-permute-done.2.above_ref, f32[4,8,128]{2,1,0:T(8,128)S(1)} %get-tuple-element.27.c0_ref, f32[4,8,128]{2,1,0:T(8,128)S(1)} %get-tuple-element.26.c1_ref, f32[4,8,128]{2,1,0:T(8,128)S(1)} %collective-permute-done.3.below_ref, ...), custom_call_target="tpu_custom_call" | custom-call | flops 1000000 | bytes 1000000 | tf_op jit(solution)/shard_map/pallas_call | solution.py:25
  58.1 7.6 %collective-permute-start.5 = (f32[8,8,128]{2,1,0:T(8,128)S(1)}, f32[8,8,128]{2,1,0:T(8,128)S(1)}, u32[]{:S(2)}, u32[]{:S(2)}) collective-permute-start(f32[8,8,128]{2,1,0:T(8,128)S(1)} %get-tuple-element.31.la_ref), channel_id=1, source_target_pairs={{1,0},{2,1},{3,2},{4,3},{5,4},{6,5},{7,6},{8,7},{9,8},{10,9},{11,1... | collective-permute-start | bytes 98312 | tf_op jit(solution)/shard_map/ppermute | solution.py:297
  65.6 0.0 collective-permute-start.4
  65.7 1.0 collective-permute-done.5.rb_ref
  66.7 7.8 %collective-permute-done.4.ra_ref = f32[8,8,128]{2,1,0:T(8,128)S(1)} collective-permute-done((f32[8,8,128]{2,1,0:T(8,128)S(1)}, f32[8,8,128]{2,1,0:T(8,128)S(1)}, u32[]{:S(2)}, u32[]{:S(2)}) %collective-permute-start.4) | collective-permute-done | bytes 32800 | tf_op jit(solution)/shard_map/ppermute | solution.py:292
  74.4 0.0 collective-permute-done.7.ep_ref
  74.4 0.0 collective-permute-done.6.em_ref
  74.4 2.9 %shard_map.79 = (f32[2,32,8,128]{3,2,1,0:T(8,128)S(1)}, f32[16,8,128]{2,1,0:T(8,128)S(1)}) custom-call(s32[2]{0:T(128)S(1)} %copy-done.6, s32[2]{0:T(128)S(1)} %pad_add_fusion.place_ref, f32[8,8,128]{2,1,0:T(8,128)S(1)} %get-tuple-element.31.la_ref, f32[8,8,128]{2,1,0:T(8,128)S(1)} %get-tuple-element.32.lb_ref, ...), custom_call_target="tpu_custom_call" | custom-call | flops 1000000 | bytes 1000000 | tf_op jit(solution)/shard_map/pallas_call | solution.py:25
  77.3 12.5 %all-gather.1 = f32[64,8,128]{2,1,0:T(8,128)S(1)} all-gather(f32[16,8,128]{2,1,0:T(8,128)S(1)} %get-tuple-element.33), channel_id=3, replica_groups=mesh['mem'=4,'lat'=64] {'mem'}, dimensions={0}, use_global_device_ids=true | all-gather | bytes 327680 | tf_op jit(solution)/shard_map/all_gather | solution.py:333
  89.9 0.1 collective-permute-start.9
  90.0 1.5 %collective-permute-start.8 = (f32[8,8,128]{2,1,0:T(8,128)S(1)}, f32[8,8,128]{2,1,0:T(8,128)S(1)}, u32[]{:S(2)}, u32[]{:S(2)}) collective-permute-start(f32[8,8,128]{2,1,0:T(8,128)S(1)} %get-tuple-element.35.cb_ref), channel_id=1, source_target_pairs={{0,1},{1,2},{2,3},{3,4},{4,5},{5,6},{6,7},{7,8},{8,9},{9,10},{10,1... | collective-permute-start | bytes 98312 | tf_op jit(solution)/shard_map/ppermute | solution.py:292
  91.4 1.3 %collective-permute-done.9.db_ref = f32[8,8,128]{2,1,0:T(8,128)S(1)} collective-permute-done((f32[8,8,128]{2,1,0:T(8,128)S(1)}, f32[8,8,128]{2,1,0:T(8,128)S(1)}, u32[]{:S(2)}, u32[]{:S(2)}) %collective-permute-start.9) | collective-permute-done | bytes 32800 | tf_op jit(solution)/shard_map/ppermute | solution.py:297
  92.7 6.1 %collective-permute-done.8.da_ref = f32[8,8,128]{2,1,0:T(8,128)S(1)} collective-permute-done((f32[8,8,128]{2,1,0:T(8,128)S(1)}, f32[8,8,128]{2,1,0:T(8,128)S(1)}, u32[]{:S(2)}, u32[]{:S(2)}) %collective-permute-start.8) | collective-permute-done | bytes 32800 | tf_op jit(solution)/shard_map/ppermute | solution.py:292
  98.8 4.9 %shard_map.81 = (f32[8,8,128]{2,1,0:T(8,128)S(1)}, f32[8,8,128]{2,1,0:T(8,128)S(1)}) custom-call(f32[8,8,128]{2,1,0:T(8,128)S(1)} %get-tuple-element.34.ca_ref, f32[8,8,128]{2,1,0:T(8,128)S(1)} %get-tuple-element.35.cb_ref, f32[8,8,128]{2,1,0:T(8,128)S(1)} %collective-permute-done.8.da_ref, f32[8,8,128]{2,1,0:T(8,128)S(1)} %collective-permute-done.9.db_ref, ...), custom_call_target="tpu_custom_call" | custom-call | flops 1000000 | bytes 1000000 | tf_op jit(solution)/shard_map/pallas_call | solution.py:25
  103.8 0.3 collective-permute-start.11
  104.1 1.2 %collective-permute-start.10 = (f32[8,8,128]{2,1,0:T(8,128)S(1)}, f32[8,8,128]{2,1,0:T(8,128)S(1)}, u32[]{:S(2)}, u32[]{:S(2)}) collective-permute-start(f32[8,8,128]{2,1,0:T(8,128)S(1)} %get-tuple-element.37.lb_ref), channel_id=1, source_target_pairs={{0,1},{1,2},{2,3},{3,4},{4,5},{5,6},{6,7},{7,8},{8,9},{9,10},{10,1... | collective-permute-start | bytes 98312 | tf_op jit(solution)/shard_map/ppermute | solution.py:292
  105.3 1.3 %collective-permute-done.11.rb_ref = f32[8,8,128]{2,1,0:T(8,128)S(1)} collective-permute-done((f32[8,8,128]{2,1,0:T(8,128)S(1)}, f32[8,8,128]{2,1,0:T(8,128)S(1)}, u32[]{:S(2)}, u32[]{:S(2)}) %collective-permute-start.11) | collective-permute-done | bytes 32800 | tf_op jit(solution)/shard_map/ppermute | solution.py:297
  106.6 6.2 %collective-permute-done.10.ra_ref = f32[8,8,128]{2,1,0:T(8,128)S(1)} collective-permute-done((f32[8,8,128]{2,1,0:T(8,128)S(1)}, f32[8,8,128]{2,1,0:T(8,128)S(1)}, u32[]{:S(2)}, u32[]{:S(2)}) %collective-permute-start.10) | collective-permute-done | bytes 32800 | tf_op jit(solution)/shard_map/ppermute | solution.py:292
  112.9 2.5 %shard_map.82 = f32[32,16,128]{2,1,0:T(8,128)} custom-call(s32[2]{0:T(128)S(1)} %copy-done.6, s32[2]{0:T(128)S(1)} %pad_add_fusion.place_ref, f32[8,8,128]{2,1,0:T(8,128)S(1)} %get-tuple-element.36.la_ref, f32[8,8,128]{2,1,0:T(8,128)S(1)} %get-tuple-element.37.lb_ref, f32[8,8,128]{2,1,0:T(8,128)S(1)} %collective-permute-done.10.ra_ref, ...), custom_call_target="tpu_custom_call" | custom-call | flops 1000000 | bytes 1000000 | tf_op jit(solution)/shard_map/pallas_call | solution.py:25
  (3 shorter events, 0.0 us)
Async XLA Ops:
  0.0 1.2 %copy-start.1 = (f32[32,4,2,1024]{3,2,1,0:T(2,128)S(1)}, f32[32,4,2,1024]{3,2,1,0:T(2,128)}, u32[]{:S(2)}) copy-start(f32[32,4,2,1024]{3,2,1,0:T(2,128)} %param.8) | copy-start | bytes 3145732
  1.2 10.0 %copy-start = (f32[32,2,1024]{2,1,0:T(2,128)S(1)}, f32[32,2,1024]{2,1,0:T(2,128)}, u32[]{:S(2)}) copy-start(f32[32,2,1024]{2,1,0:T(2,128)} %param.7) | copy-start | bytes 786436
  1.4 73.1 %collective-permute-start.7 = (f32[128,8,128]{2,1,0:T(8,128)S(1)}, f32[128,8,128]{2,1,0:T(8,128)S(1)}, u32[]{:S(2)}, u32[]{:S(2)}) collective-permute-start(f32[128,8,128]{2,1,0:T(8,128)S(1)} %get-tuple-element.24.e0_ref), channel_id=1, source_target_pairs={{1,0},{2,1},{3,2},{4,3},{5,4},{6,5},{7,6},{8,7},{9,8},{10,9},{11,1... | collective-permute-start | bytes 1572872 | tf_op jit(solution)/shard_map/ppermute | solution.py:297
  11.2 0.7 copy-start.6
  11.2 63.2 %collective-permute-start.6 = (f32[128,8,128]{2,1,0:T(8,128)S(1)}, f32[128,8,128]{2,1,0:T(8,128)S(1)}, u32[]{:S(2)}, u32[]{:S(2)}) collective-permute-start(f32[128,8,128]{2,1,0:T(8,128)S(1)} %get-tuple-element.25.e1_ref), channel_id=1, source_target_pairs={{0,1},{1,2},{2,3},{3,4},{4,5},{5,6},{6,7},{7,8},{8,9},{9,10},{10,1... | collective-permute-start | bytes 1572872 | tf_op jit(solution)/shard_map/ppermute | solution.py:292
  14.1 10.5 %collective-permute-start.1 = (f32[32,8,128]{2,1,0:T(8,128)S(1)}, f32[32,8,128]{2,1,0:T(8,128)S(1)}, u32[]{:S(2)}, u32[]{:S(2)}) collective-permute-start(f32[32,8,128]{2,1,0:T(8,128)S(1)} %get-tuple-element.22.w0_ref), channel_id=1, source_target_pairs={{1,0},{2,1},{3,2},{4,3},{5,4},{6,5},{7,6},{8,7},{9,8},{10,9},{11,1... | collective-permute-start | bytes 393224 | tf_op jit(solution)/shard_map/ppermute | solution.py:297
  21.1 11.5 %collective-permute-start = (f32[32,8,128]{2,1,0:T(8,128)S(1)}, f32[32,8,128]{2,1,0:T(8,128)S(1)}, u32[]{:S(2)}, u32[]{:S(2)}) collective-permute-start(f32[32,8,128]{2,1,0:T(8,128)S(1)} %get-tuple-element.23.w1_ref), channel_id=1, source_target_pairs={{0,1},{1,2},{2,3},{3,4},{4,5},{5,6},{6,7},{7,8},{8,9},{9,10},{10,1... | collective-permute-start | bytes 393224 | tf_op jit(solution)/shard_map/ppermute | solution.py:292
  32.6 19.4 %copy-start.4 = (s32[4,4,2048]{2,1,0:T(4,128)S(1)}, s32[4,4,2048]{2,1,0:T(4,128)}, u32[]{:S(2)}) copy-start(s32[4,4,2048]{2,1,0:T(4,128)} %param.12) | copy-start | bytes 393220
  32.6 19.4 %copy-start.5 = (f32[4,4,2048]{2,1,0:T(4,128)S(1)}, f32[4,4,2048]{2,1,0:T(4,128)}, u32[]{:S(2)}) copy-start(f32[4,4,2048]{2,1,0:T(4,128)} %param.13) | copy-start | bytes 393220
  33.3 18.7 %copy-start.2 = (s32[4,4,2048]{2,1,0:T(4,128)S(1)}, s32[4,4,2048]{2,1,0:T(4,128)}, u32[]{:S(2)}) copy-start(s32[4,4,2048]{2,1,0:T(4,128)} %param.10) | copy-start | bytes 393220
  33.3 18.7 %copy-start.3 = (f32[4,4,2048]{2,1,0:T(4,128)S(1)}, f32[4,4,2048]{2,1,0:T(4,128)}, u32[]{:S(2)}) copy-start(f32[4,4,2048]{2,1,0:T(4,128)} %param.11) | copy-start | bytes 393220
  44.5 8.7 %collective-permute-start.2 = (f32[4,8,128]{2,1,0:T(8,128)S(1)}, f32[4,8,128]{2,1,0:T(8,128)S(1)}, u32[]{:S(2)}, u32[]{:S(2)}) collective-permute-start(f32[4,8,128]{2,1,0:T(8,128)S(1)} %get-tuple-element.26.c1_ref), channel_id=1, source_target_pairs={{0,1},{1,2},{2,3},{3,4},{4,5},{5,6},{6,7},{7,8},{8,9},{9,10},{10,1... | collective-permute-start | bytes 49160 | tf_op jit(solution)/shard_map/ppermute | solution.py:292
  44.6 8.6 %collective-permute-start.3 = (f32[4,8,128]{2,1,0:T(8,128)S(1)}, f32[4,8,128]{2,1,0:T(8,128)S(1)}, u32[]{:S(2)}, u32[]{:S(2)}) collective-permute-start(f32[4,8,128]{2,1,0:T(8,128)S(1)} %get-tuple-element.27.c0_ref), channel_id=1, source_target_pairs={{1,0},{2,1},{3,2},{4,3},{5,4},{6,5},{7,6},{8,7},{9,8},{10,9},{11,1... | collective-permute-start | bytes 49160 | tf_op jit(solution)/shard_map/ppermute | solution.py:297
  58.1 8.6 %collective-permute-start.5 = (f32[8,8,128]{2,1,0:T(8,128)S(1)}, f32[8,8,128]{2,1,0:T(8,128)S(1)}, u32[]{:S(2)}, u32[]{:S(2)}) collective-permute-start(f32[8,8,128]{2,1,0:T(8,128)S(1)} %get-tuple-element.31.la_ref), channel_id=1, source_target_pairs={{1,0},{2,1},{3,2},{4,3},{5,4},{6,5},{7,6},{8,7},{9,8},{10,9},{11,1... | collective-permute-start | bytes 98312 | tf_op jit(solution)/shard_map/ppermute | solution.py:297
  65.6 8.8 %collective-permute-start.4 = (f32[8,8,128]{2,1,0:T(8,128)S(1)}, f32[8,8,128]{2,1,0:T(8,128)S(1)}, u32[]{:S(2)}, u32[]{:S(2)}) collective-permute-start(f32[8,8,128]{2,1,0:T(8,128)S(1)} %get-tuple-element.32.lb_ref), channel_id=1, source_target_pairs={{0,1},{1,2},{2,3},{3,4},{4,5},{5,6},{6,7},{7,8},{8,9},{9,10},{10,1... | collective-permute-start | bytes 98312 | tf_op jit(solution)/shard_map/ppermute | solution.py:292
  89.9 2.8 %collective-permute-start.9 = (f32[8,8,128]{2,1,0:T(8,128)S(1)}, f32[8,8,128]{2,1,0:T(8,128)S(1)}, u32[]{:S(2)}, u32[]{:S(2)}) collective-permute-start(f32[8,8,128]{2,1,0:T(8,128)S(1)} %get-tuple-element.34.ca_ref), channel_id=1, source_target_pairs={{1,0},{2,1},{3,2},{4,3},{5,4},{6,5},{7,6},{8,7},{9,8},{10,9},{11,1... | collective-permute-start | bytes 98312 | tf_op jit(solution)/shard_map/ppermute | solution.py:297
  90.0 8.9 %collective-permute-start.8 = (f32[8,8,128]{2,1,0:T(8,128)S(1)}, f32[8,8,128]{2,1,0:T(8,128)S(1)}, u32[]{:S(2)}, u32[]{:S(2)}) collective-permute-start(f32[8,8,128]{2,1,0:T(8,128)S(1)} %get-tuple-element.35.cb_ref), channel_id=1, source_target_pairs={{0,1},{1,2},{2,3},{3,4},{4,5},{5,6},{6,7},{7,8},{8,9},{9,10},{10,1... | collective-permute-start | bytes 98312 | tf_op jit(solution)/shard_map/ppermute | solution.py:292
  103.8 2.8 %collective-permute-start.11 = (f32[8,8,128]{2,1,0:T(8,128)S(1)}, f32[8,8,128]{2,1,0:T(8,128)S(1)}, u32[]{:S(2)}, u32[]{:S(2)}) collective-permute-start(f32[8,8,128]{2,1,0:T(8,128)S(1)} %get-tuple-element.36.la_ref), channel_id=1, source_target_pairs={{1,0},{2,1},{3,2},{4,3},{5,4},{6,5},{7,6},{8,7},{9,8},{10,9},{11,1... | collective-permute-start | bytes 98312 | tf_op jit(solution)/shard_map/ppermute | solution.py:297
  104.1 8.8 %collective-permute-start.10 = (f32[8,8,128]{2,1,0:T(8,128)S(1)}, f32[8,8,128]{2,1,0:T(8,128)S(1)}, u32[]{:S(2)}, u32[]{:S(2)}) collective-permute-start(f32[8,8,128]{2,1,0:T(8,128)S(1)} %get-tuple-element.37.lb_ref), channel_id=1, source_target_pairs={{0,1},{1,2},{2,3},{3,4},{4,5},{5,6},{6,7},{7,8},{8,9},{9,10},{10,1... | collective-permute-start | bytes 98312 | tf_op jit(solution)/shard_map/ppermute | solution.py:292

commit v2 on v1

v2 whole, which is shorter than its diff:
```python
import jax
import jax.numpy as jnp
from jax import lax
from jax.experimental import pallas as pl
from jax.experimental.pallas import tpu as pltpu
from jax.sharding import PartitionSpec as P

STEP_SIZE = 0.5
C_MID = 0.5
C_SIDE = 0.25

F32 = jnp.float32
LIMIT = 40 * 1024 * 1024


def shape(*dims):
    return jax.ShapeDtypeStruct(dims, F32)


def call(kernel, outs, args, scalars=(), scratch=(), flops=1_000_000):
    in_specs = [pl.BlockSpec(memory_space=pltpu.SMEM)] * len(scalars)
    in_specs += [pl.BlockSpec(memory_space=pltpu.VMEM)] * len(args)
    args = tuple(scalars) + tuple(args)
    return pl.pallas_call(
        kernel,
        out_shape=outs,
        in_specs=in_specs,
        out_specs=jax.tree.map(lambda _: pl.BlockSpec(memory_space=pltpu.VMEM), outs),
        scratch_shapes=[pltpu.VMEM(dims, F32) for dims in scratch],
        compiler_params=pltpu.CompilerParams(vmem_limit_bytes=LIMIT),
        cost_estimate=pl.CostEstimate(flops=flops, transcendentals=0, bytes_accessed=1_000_000),
    )(*args)


def iota(shape_, dim):
    return lax.broadcasted_iota(jnp.int32, shape_, dim)


def position(k):
    return jnp.where(k < 128, k, jnp.where(k < 192, k, k - 256))


def widened(x):
    n = x.shape[0]
    y = jnp.where(iota(x.shape, 2) < 64, pltpu.roll(x, 7, 1), pltpu.roll(x, 1, 1))
    return jnp.concatenate([x.reshape(n * 8, 128), y.reshape(n * 8, 128)], axis=1)


def product(x, matrix):
    high = x.astype(jnp.bfloat16)
    rest = x - high.astype(F32)
    middle = rest.astype(jnp.bfloat16)
    low = (rest - middle.astype(F32)).astype(jnp.bfloat16)
    total = jnp.dot(low, matrix, preferred_element_type=F32)
    total = total + jnp.dot(middle, matrix, preferred_element_type=F32)
    return total + jnp.dot(high, matrix, preferred_element_type=F32)


def filtered(x, band, scale):
    return product(widened(x), band).reshape(x.shape) * scale


def scale_of(widths_ref, r):
    width = jnp.full((8, 128), widths_ref[r], jnp.int32)
    return 1.0 / (2.0 * width.astype(F32) + 1.0)


def if_inside(place_ref, above, below):
    band = jnp.full((8, 128), place_ref[0], jnp.int32)
    last = jnp.full((8, 128), place_ref[1], jnp.int32)
    return jnp.where(band > 0, above, 0.0), jnp.where(band < last, below, 0.0)


def filter_kernel(widths_ref, v_ref, w0_ref, w1_ref, band_ref):
    away = jnp.abs(position(iota((256, 128), 0)) - iota((256, 128), 1))
    for r, out in ((0, w0_ref), (1, w1_ref)):
        inside = away <= jnp.full((256, 128), widths_ref[r], jnp.int32)
        band = jnp.where(inside, 1.0, 0.0).astype(jnp.bfloat16)
        band_ref[r] = band
        scale = scale_of(widths_ref, r)
        for b in range(2):
            x = v_ref[pl.ds(b * 16, 16), pl.ds(r, 8, stride=2), :]
            out[pl.ds(b * 16, 16)] = filtered(x, band, scale)


def split_kernel(e_ref, e0_ref, e1_ref):
    def body(b, carry):
        at = pl.ds(b * 8, 8)
        e0_ref[at] = e_ref[at, pl.ds(0, 8, stride=2), :]
        e1_ref[at] = e_ref[at, pl.ds(1, 8, stride=2), :]
        return carry

    lax.fori_loop(0, 16, body, 0)


def planes_kernel(src_ref, wgt_ref, msk_ref, inn_ref, planes_ref, mask_ref, target_ref, refine_ref, gather_ref):
    parent = iota((8, 128), 0) * 128 + iota((8, 128), 1) // 2
    for j in range(8):
        half, fr = j // 4, j % 4
        at = pl.ds(j, 8, stride=8)
        codes, weights = [], []
        for s in range(4):
            src = src_ref[s, at, :]
            row_shift = lax.shift_right_logical(src, 10) - (fr // 2 + 1)
            col = jnp.bitwise_and(src, 1023)
            col_shift = jnp.bitwise_and(col - parent - half * 64 + 2, 1023) - 2
            codes.append((row_shift + 1) * 5 + col_shift + 2)
            weights.append(wgt_ref[s, at, :])
        for n in range(15):
            total = jnp.where(codes[0] == n, weights[0], 0.0)
            for s in range(1, 4):
                total = total + jnp.where(codes[s] == n, weights[s], 0.0)
            planes_ref[n, j] = total
        for t in range(4):
            mask_ref[t, j] = msk_ref[t, at, :].astype(F32)
            target_ref[t, j] = inn_ref[t, at, :]
    for n in range(10):
        d, half = n // 2 - 2, n % 2
        source = half * 64 + iota((256, 128), 1) // 2 + d
        hit = position(iota((256, 128), 0)) == source
        refine_ref[:, n * 128 : n * 128 + 128] = jnp.where(hit, 1.0, 0.0).astype(jnp.bfloat16)
        source = half * 64 + iota((128, 256), 0) // 2 + d
        hit = position(iota((128, 256), 1)) == source
        gather_ref[n * 128 : n * 128 + 128, :] = jnp.where(hit, 1.0, 0.0).astype(jnp.bfloat16)


def first_kernel(place_ref, w0_ref, w1_ref, above_ref, below_ref, e0_ref, e1_ref, part_ref):
    def body(m, sums):
        a, b = w0_ref[m], w1_ref[m]
        above, below = if_inside(place_ref, above_ref[m], below_ref[m])
        f0 = C_MID * a + C_SIDE * (above + b)
        f1 = C_MID * b + C_SIDE * (a + below)
        sums = list(sums)
        for t in range(4):
            sums[t] = sums[t] + e0_ref[m * 4 + t] * f0
            sums[4 + t] = sums[4 + t] + e1_ref[m * 4 + t] * f1
        return tuple(sums)

    sums = lax.fori_loop(0, 32, body, (jnp.zeros((8, 128), F32),) * 8, unroll=4)
    for n in range(8):
        part_ref[n] = sums[n]


def sum_kernel(parts_ref, a_ref, b_ref):
    count = a_ref.shape[0]
    for n in range(2 * count):
        total = (parts_ref[0, n] + parts_ref[1, n]) + (parts_ref[2, n] + parts_ref[3, n])
        if n < count:
            a_ref[n] = total
        else:
            b_ref[n - count] = total


def stencil(a, b):
    lane = iota((8, 128), 1)
    a1, b1 = pltpu.roll(a, 1, 1), pltpu.roll(b, 1, 1)
    left_a = jnp.where(lane == 0, pltpu.roll(b1, 1, 0), a1)
    left_b = jnp.where(lane == 0, a1, b1)
    a2, b2 = pltpu.roll(a, 127, 1), pltpu.roll(b, 127, 1)
    right_a = jnp.where(lane == 127, b2, a2)
    right_b = jnp.where(lane == 127, pltpu.roll(a2, 7, 0), b2)
    return 0.5 * a + 0.25 * (left_a + right_a), 0.5 * b + 0.25 * (left_b + right_b)


def observe(rows, planes_ref, mask_ref, target_ref, refine_ref, gather_ref, u_ref, la_ref, lb_ref):
    window = jnp.stack([rows[t][q] for t in range(4) for q in range(4)])
    u_ref[...] = product(widened(window), refine_ref[...])

    def piece(t, q, d, half):
        n = d * 2 + half
        return u_ref[pl.ds((t * 4 + q) * 8, 8), pl.ds(n * 128, 128)]

    back = {}
    for r in range(2):
        fine = {}
        for half in range(2):
            for rs in range(-1, 2):
                for d in range(5):
                    u = [piece(t, r + 1 + rs, d, half) for t in range(4)]
                    for fr in (2 * r, 2 * r + 1):
                        plane = planes_ref[(rs + 1) * 5 + d, half * 4 + fr]
                        for t in range(4):
                            key = (t, fr, half)
                            fine[key] = fine[key] + plane * u[t] if key in fine else plane * u[t]
        for t in range(4):
            for fr in (2 * r, 2 * r + 1):
                pair = stencil(fine[t, fr, 0], fine[t, fr, 1])
                pair = [
                    mask_ref[t, half * 4 + fr] * (pair[half] - target_ref[t, half * 4 + fr])
                    for half in range(2)
                ]
                back[t, fr, 0], back[t, fr, 1] = stencil(*pair)
    for half in range(2):
        for d in range(5):
            n = d * 2 + half
            for q in range(4):
                z = [None] * 4
                for fr in range(4):
                    rs = q - 1 - fr // 2
                    if -1 <= rs <= 1:
                        plane = planes_ref[(rs + 1) * 5 + d, half * 4 + fr]
                        for t in range(4):
                            term = plane * back[t, fr, half]
                            z[t] = term if z[t] is None else z[t] + term
                for t in range(4):
                    u_ref[pl.ds((t * 4 + q) * 8, 8), pl.ds(n * 128, 128)] = z[t]
    total = None
    for d in range(5):
        term = product(u_ref[:, d * 256 : d * 256 + 256], gather_ref[d * 256 : d * 256 + 256, :])
        total = term if total is None else total + term
    own, beside = total[:, :128].reshape(16, 8, 128), total[:, 128:].reshape(16, 8, 128)
    head = iota((16, 8, 128), 2) < 64
    landed = own + jnp.where(head, pltpu.roll(beside, 1, 1), pltpu.roll(beside, 7, 1))
    for t in range(4):
        la_ref[t], la_ref[4 + t] = landed[t * 4], landed[t * 4 + 1]
        lb_ref[t], lb_ref[4 + t] = landed[t * 4 + 2], landed[t * 4 + 3]


def first_observe_kernel(above_ref, c0_ref, c1_ref, below_ref, *refs):
    observe([[ref[t] for ref in (above_ref, c0_ref, c1_ref, below_ref)] for t in range(4)], *order(refs))


def second_observe_kernel(ca_ref, cb_ref, da_ref, db_ref, *refs):
    rows = [
        [
            mine[half * 4 + t] + theirs[half * 4 + t]
            for mine, theirs in ((ca_ref, da_ref), (cb_ref, db_ref))
            for half in range(2)
        ]
        for t in range(4)
    ]
    observe(rows, *order(refs))


def order(refs):
    *fields, la_ref, lb_ref, u_ref = refs
    return *fields, u_ref, la_ref, lb_ref


def adjoint_rows(place_ref, la_ref, lb_ref, ra_ref, rb_ref):
    rows = []
    for mine, theirs in ((la_ref, ra_ref), (lb_ref, rb_ref)):
        for half in range(2):
            rows.append([mine[half * 4 + t] + theirs[half * 4 + t] for t in range(4)])
    for t in range(4):
        rows[0][t], rows[3][t] = if_inside(place_ref, rows[0][t], rows[3][t])
    return rows


def smoothed_back(e_refs, rows, s_ref):
    def body(b, carry):
        back = []
        for q in range(4):
            x = e_refs[q][pl.ds(b * 16, 16)].reshape(4, 4, 8, 128)
            total = x[:, 0] * rows[q][0]
            for t in range(1, 4):
                total = total + x[:, t] * rows[q][t]
            back.append(total)
        for r in range(2):
            s_ref[r, pl.ds(b * 4, 4)] = C_MID * back[r + 1] + C_SIDE * (back[r] + back[r + 2])
        return carry

    lax.fori_loop(0, 8, body, 0, unroll=2)


def middle_kernel(
    widths_ref, place_ref, la_ref, lb_ref, ra_ref, rb_ref, em_ref, e0_ref, e1_ref, ep_ref,
    band_ref, v_ref, new_ref, part_ref, s_ref,
):
    rows = adjoint_rows(place_ref, la_ref, lb_ref, ra_ref, rb_ref)
    e_refs = (em_ref, e0_ref, e1_ref, ep_ref)
    smoothed_back(e_refs, rows, s_ref)
    for r in range(2):
        scale = scale_of(widths_ref, r)
        for b in range(2):
            at = pl.ds(b * 16, 16)
            old = v_ref[at, pl.ds(r, 8, stride=2), :]
            gradient = old + filtered(s_ref[r, at], band_ref[r], scale)
            new = old - STEP_SIZE * gradient
            new_ref[r, at] = new
            s_ref[r, at] = filtered(new, band_ref[r], scale)

    def body(b, sums):
        sums = list(sums)
        for i in range(4):
            m = b * 4 + i
            w = [s_ref[r, m] for r in range(2)]
            forward = [
                C_SIDE * w[0],
                C_MID * w[0] + C_SIDE * w[1],
                C_MID * w[1] + C_SIDE * w[0],
                C_SIDE * w[1],
            ]
            for q in range(4):
                for t in range(4):
                    sums[q * 4 + t] = sums[q * 4 + t] + e_refs[q][m * 4 + t] * forward[q]
        return tuple(sums)

    sums = list(lax.fori_loop(0, 8, body, (jnp.zeros((8, 128), F32),) * 16))
    for t in range(4):
        sums[t], sums[12 + t] = if_inside(place_ref, sums[t], sums[12 + t])
    for n in range(16):
        part_ref[n] = sums[n]


def last_kernel(
    widths_ref, place_ref, la_ref, lb_ref, ra_ref, rb_ref, em_ref, e0_ref, e1_ref, ep_ref,
    band_ref, v_ref, out_ref, s_ref,
):
    rows = adjoint_rows(place_ref, la_ref, lb_ref, ra_ref, rb_ref)
    smoothed_back((em_ref, e0_ref, e1_ref, ep_ref), rows, s_ref)
    for r in range(2):
        scale = scale_of(widths_ref, r)
        for b in range(2):
            at = pl.ds(b * 16, 16)
            old = v_ref[r, at]
            gradient = old + filtered(s_ref[r, at], band_ref[r], scale)
            out_ref[at, pl.ds(r, 8, stride=2), :] = old - STEP_SIZE * gradient


def ring(step):
    groups, bands = lax.axis_size("mem"), lax.axis_size("lat")
    pairs = []
    for m in range(groups):
        for i in range(bands):
            inside = 0 <= i + step < bands
            other = m if inside else (m + groups // 2) % groups
            pairs.append((m * bands + i, other * bands + (i + step) % bands))
    return pairs


def to_next(x):
    return lax.ppermute(x, ("mem", "lat"), ring(1))


def to_previous(x):
    return lax.ppermute(x, ("mem", "lat"), ring(-1))


def tiles(x):
    (rows, cols) = x.shape[-2:]
    x = x.reshape(-1, rows, cols // 128, 128).transpose(0, 2, 1, 3)
    return x.reshape(-1, cols // 128 * rows, 128)


def descent(control, ensemble, widths, interp_source, interp_weight, obs_mask, innovation):
    v = tiles(control)
    e = tiles(ensemble)
    place = jnp.stack([lax.axis_index("lat"), lax.axis_size("lat") - 1]).astype(jnp.int32)
    row = shape(32, 8, 128)
    band = jax.ShapeDtypeStruct((2, 256, 128), jnp.bfloat16)
    w0, w1, band = call(filter_kernel, (row, row, band), (v,), (widths,))
    above, below = to_next(w1), to_previous(w0)
    e, w0, w1 = lax.optimization_barrier((e, w0, w1))
    e0, e1 = call(split_kernel, (shape(128, 8, 128),) * 2, (e,))
    e_above, e_below = to_next(e1), to_previous(e0)
    fields = call(
        planes_kernel,
        (
            shape(15, 8, 8, 128),
            shape(4, 8, 8, 128),
            shape(4, 8, 8, 128),
            jax.ShapeDtypeStruct((256, 1280), jnp.bfloat16),
            jax.ShapeDtypeStruct((1280, 256), jnp.bfloat16),
        ),
        tuple(tiles(x) for x in (interp_source, interp_weight, obs_mask, innovation)),
    )
    part = call(first_kernel, shape(8, 8, 128), (w0, w1, above, below, e0, e1), (place,))
    four, eight = shape(4, 8, 128), shape(8, 8, 128)
    c0, c1 = call(sum_kernel, (four, four), (lax.all_gather(part, "mem"),))
    refined = ((128, 1280),)
    la, lb = call(
        first_observe_kernel,
        (eight, eight),
        (to_next(c1), c0, c1, to_previous(c0)) + tuple(fields),
        scratch=refined,
    )
    ra, rb = to_next(lb), to_previous(la)
    ensembles = (e_above, e0, e1, e_below, band)
    smoothed = ((2, 32, 8, 128),)
    new, part = call(
        middle_kernel,
        (shape(2, 32, 8, 128), shape(16, 8, 128)),
        (la, lb, ra, rb) + ensembles + (v,),
        (widths, place),
        smoothed,
    )
    ca, cb = call(sum_kernel, (eight, eight), (lax.all_gather(part, "mem"),))
    la, lb = call(
        second_observe_kernel,
        (eight, eight),
        (ca, cb, to_next(cb), to_previous(ca)) + tuple(fields),
        scratch=refined,
    )
    ra, rb = to_next(lb), to_previous(la)
    out = call(
        last_kernel,
        shape(32, 16, 128),
        (la, lb, ra, rb) + ensembles + (new,),
        (widths, place),
        smoothed,
    )
    return out.reshape(32, 8, 2, 128).transpose(0, 2, 1, 3).reshape(control.shape)


def solution(mesh):
    in_specs = (
        P("mem", "lat", None),
        P("mem", None, "lat", None),
        P("lat"),
        P(None, "lat", None),
        P(None, "lat", None),
        P(None, "lat", None),
        P(None, "lat", None),
    )
    out_specs = P("mem", "lat", None)
    return jax.shard_map(descent, mesh=mesh, in_specs=in_specs, out_specs=out_specs, check_vma=False)
```

time: 116 us -> 110 us (0.948)
  Pallas kernels: 18.6 us -> 9.18 us
  blocking collectives: 23.7 us -> 26.5 us
    pallas_call x10, Pallas kernels: 18.6 us -> 9.18 us  [call(): pl.pallas_call(kernel, out_shape=outs, in_specs=in_specs, out_specs=jax.t...]
    all_gather x2, blocking collectives: 23.7 us -> 26.5 us  [the longest x1 15.1 us: descent(): ca, cb = call(sum_kernel, (eight, eight), (lax.all_gather(part, 'mem'),))]
    unnamed x14 -> x16, local copies, waits for them, and re-layouts: 1.9 us -> 2.85 us
  transfers between devices with their start and end apart: 12 -> 12, of which waited for: 9 -> 9; matrix products, arithmetic and copies ran while one was open for 0% -> 0% of each run, Pallas kernels for 7% -> 3%
where the time goes in v2:
time: 110 us
  waiting for transfers between devices  36.4 us (33%)
  starting transfers between devices  35 us (32%)
  blocking collectives  26.5 us (24%)
  Pallas kernels  9.18 us (8%)
  local copies, waits for them, and re-layouts  2.85 us (3%)
    ppermute x6, starting transfers between devices, to_previous(): return lax.ppermute(x, ('mem', 'lat'), ring(-1))  32.1 us
    ppermute x6, waiting for transfers between devices, to_next(): return lax.ppermute(x, ('mem', 'lat'), ring(1))  26.3 us
    all_gather x1, blocking collectives, descent(): ca, cb = call(sum_kernel, (eight, eight), (lax.all_gather(part, 'mem'),))  15.1 us
    all_gather x1, blocking collectives, descent(): c0, c1 = call(sum_kernel, (four, four), (lax.all_gather(part, 'mem'),))  11.4 us
    ppermute x6, waiting for transfers between devices, to_previous(): return lax.ppermute(x, ('mem', 'lat'), ring(-1))  10.1 us
    pallas_call x10, Pallas kernels, call(): pl.pallas_call(kernel, out_shape=outs, in_specs=in_specs, out_specs=jax.t...  9.18 us
    ppermute x6, starting transfers between devices, to_next(): return lax.ppermute(x, ('mem', 'lat'), ring(1))  2.97 us
    unnamed x16, local copies, waits for them, and re-layouts  2.85 us
  transfers between devices with their start and end apart: 12, of which 9 were waited for; matrix products, arithmetic and copies ran while one was open for 0% of the time, Pallas kernels for 3%

profile of v2, /device:TPU:1, one launch (start us, length us, event | category | flops | bytes accessed | tf_op | source)
XLA Modules:
  0.0 110.1 jit_solution(1107487968439310829)
XLA Ops:
  0.0 0.0 copy-start.7
  0.0 0.7 copy-done.7
  0.7 0.0 copy-start
  0.7 0.9 copy-done
  1.6 0.9 shard_map.73
  2.5 0.0 copy-start.2
  2.5 1.2 %copy-done.2 = f32[32,4,2,1024]{3,2,1,0:T(2,128)S(1)} copy-done((f32[32,4,2,1024]{3,2,1,0:T(2,128)S(1)}, f32[32,4,2,1024]{3,2,1,0:T(2,128)}, u32[]{:S(2)}) %copy-start.2) | copy-done | bytes 1048600
  3.8 0.1 shard_map.74
  3.9 11.1 %collective-permute-start.7 = (f32[128,8,128]{2,1,0:T(8,128)S(1)}, f32[128,8,128]{2,1,0:T(8,128)S(1)}, u32[]{:S(2)}, u32[]{:S(2)}) collective-permute-start(f32[128,8,128]{2,1,0:T(8,128)S(1)} %get-tuple-element.33.e0_ref), channel_id=1, source_target_pairs={{0,191},{1,0},{2,1},{3,2},{4,3},{5,4},{6,5},{7,6},{8,7},{9,8},{10,... | collective-permute-start | bytes 1572872 | tf_op jit(solution)/shard_map/ppermute | solution.py:337
  15.0 0.0 collective-permute-start.6
  15.0 6.9 %collective-permute-start.1 = (f32[32,8,128]{2,1,0:T(8,128)S(1)}, f32[32,8,128]{2,1,0:T(8,128)S(1)}, u32[]{:S(2)}, u32[]{:S(2)}) collective-permute-start(f32[32,8,128]{2,1,0:T(8,128)S(1)} %get-tuple-element.30.w0_ref), channel_id=1, source_target_pairs={{0,191},{1,0},{2,1},{3,2},{4,3},{5,4},{6,5},{7,6},{8,7},{9,8},{10,... | collective-permute-start | bytes 393224 | tf_op jit(solution)/shard_map/ppermute | solution.py:337
  21.9 0.0 collective-permute-start
  21.9 0.1 pad_add_fusion.place_ref
  22.0 6.4 %collective-permute-done.1.below_ref = f32[32,8,128]{2,1,0:T(8,128)S(1)} collective-permute-done((f32[32,8,128]{2,1,0:T(8,128)S(1)}, f32[32,8,128]{2,1,0:T(8,128)S(1)}, u32[]{:S(2)}, u32[]{:S(2)}) %collective-permute-start.1) | collective-permute-done | bytes 131104 | tf_op jit(solution)/shard_map/ppermute | solution.py:337
  28.4 7.3 %collective-permute-done.above_ref = f32[32,8,128]{2,1,0:T(8,128)S(1)} collective-permute-done((f32[32,8,128]{2,1,0:T(8,128)S(1)}, f32[32,8,128]{2,1,0:T(8,128)S(1)}, u32[]{:S(2)}, u32[]{:S(2)}) %collective-permute-start) | collective-permute-done | bytes 131104 | tf_op jit(solution)/shard_map/ppermute | solution.py:333
  35.8 0.7 shard_map.75
  36.5 0.0 copy-start.3
  36.5 0.0 copy-start.4
  36.5 11.4 %all-gather = f32[32,8,128]{2,1,0:T(8,128)S(1)} all-gather(f32[8,8,128]{2,1,0:T(8,128)S(1)} %shard_map.75), channel_id=2, replica_groups=mesh['mem'=4,'lat'=64] {'mem'}, dimensions={0}, use_global_device_ids=true | all-gather | bytes 163840 | tf_op jit(solution)/shard_map/all_gather | solution.py:370
  48.0 0.1 collective-permute-start.2
  48.0 6.9 %collective-permute-start.3 = (f32[4,8,128]{2,1,0:T(8,128)S(1)}, f32[4,8,128]{2,1,0:T(8,128)S(1)}, u32[]{:S(2)}, u32[]{:S(2)}) collective-permute-start(f32[4,8,128]{2,1,0:T(8,128)S(1)} %get-tuple-element.36.c0_ref), channel_id=1, source_target_pairs={{0,191},{1,0},{2,1},{3,2},{4,3},{5,4},{6,5},{7,6},{8,7},{9,8},{10,... | collective-permute-start | bytes 49160 | tf_op jit(solution)/shard_map/ppermute | solution.py:337
  54.9 0.0 copy-done.5
  54.9 0.0 copy-done.6
  54.9 0.0 copy-done.3
  54.9 0.0 copy-done.4
  54.9 0.5 shard_map.77
  55.5 0.6 collective-permute-done.2.above_ref
  56.0 0.0 collective-permute-done.3.below_ref
  56.1 1.5 %shard_map.78 = (f32[8,8,128]{2,1,0:T(8,128)S(1)}, f32[8,8,128]{2,1,0:T(8,128)S(1)}) custom-call(f32[4,8,128]{2,1,0:T(8,128)S(1)} %collective-permute-done.2.above_ref, f32[4,8,128]{2,1,0:T(8,128)S(1)} %get-tuple-element.36.c0_ref, f32[4,8,128]{2,1,0:T(8,128)S(1)} %get-tuple-element.35.c1_ref, f32[4,8,128]{2,1,0:T(8,128)S(1)} %collective-permute-done.3.below_ref, ...), custom_call_target="tpu_custom_call" | custom-call | flops 1000000 | bytes 1000000 | tf_op jit(solution)/shard_map/pallas_call | solution.py:24
  57.6 7.0 %collective-permute-start.5 = (f32[8,8,128]{2,1,0:T(8,128)S(1)}, f32[8,8,128]{2,1,0:T(8,128)S(1)}, u32[]{:S(2)}, u32[]{:S(2)}) collective-permute-start(f32[8,8,128]{2,1,0:T(8,128)S(1)} %get-tuple-element.42.la_ref), channel_id=1, source_target_pairs={{0,191},{1,0},{2,1},{3,2},{4,3},{5,4},{6,5},{7,6},{8,7},{9,8},{10,... | collective-permute-start | bytes 98312 | tf_op jit(solution)/shard_map/ppermute | solution.py:337
  64.6 0.0 collective-permute-start.4
  64.6 1.0 collective-permute-done.5.rb_ref
  65.6 7.2 %collective-permute-done.4.ra_ref = f32[8,8,128]{2,1,0:T(8,128)S(1)} collective-permute-done((f32[8,8,128]{2,1,0:T(8,128)S(1)}, f32[8,8,128]{2,1,0:T(8,128)S(1)}, u32[]{:S(2)}, u32[]{:S(2)}) %collective-permute-start.4) | collective-permute-done | bytes 32800 | tf_op jit(solution)/shard_map/ppermute | solution.py:333
  72.8 0.0 collective-permute-done.7.ep_ref
  72.8 0.0 collective-permute-done.6.em_ref
  72.8 0.0 copy-done.1
  72.8 2.0 %shard_map.79 = (f32[2,32,8,128]{3,2,1,0:T(8,128)S(1)}, f32[16,8,128]{2,1,0:T(8,128)S(1)}) custom-call(s32[2]{0:T(128)S(1)} %copy-done.7, s32[2]{0:T(128)S(1)} %pad_add_fusion.place_ref, f32[8,8,128]{2,1,0:T(8,128)S(1)} %get-tuple-element.42.la_ref, f32[8,8,128]{2,1,0:T(8,128)S(1)} %get-tuple-element.43.lb_ref, ...), custom_call_target="tpu_custom_call" | custom-call | flops 1000000 | bytes 1000000 | tf_op jit(solution)/shard_map/pallas_call | solution.py:24
  74.8 15.1 %all-gather.1 = f32[64,8,128]{2,1,0:T(8,128)S(1)} all-gather(f32[16,8,128]{2,1,0:T(8,128)S(1)} %get-tuple-element.45), channel_id=3, replica_groups=mesh['mem'=4,'lat'=64] {'mem'}, dimensions={0}, use_global_device_ids=true | all-gather | bytes 327680 | tf_op jit(solution)/shard_map/all_gather | solution.py:388
  89.9 0.1 collective-permute-start.9
  90.0 1.5 %collective-permute-start.8 = (f32[8,8,128]{2,1,0:T(8,128)S(1)}, f32[8,8,128]{2,1,0:T(8,128)S(1)}, u32[]{:S(2)}, u32[]{:S(2)}) collective-permute-start(f32[8,8,128]{2,1,0:T(8,128)S(1)} %get-tuple-element.47.cb_ref), channel_id=1, source_target_pairs={{0,1},{1,2},{2,3},{3,4},{4,5},{5,6},{6,7},{7,8},{8,9},{9,10},{10,1... | collective-permute-start | bytes 98312 | tf_op jit(solution)/shard_map/ppermute | solution.py:333
  91.4 1.3 %collective-permute-done.9.db_ref = f32[8,8,128]{2,1,0:T(8,128)S(1)} collective-permute-done((f32[8,8,128]{2,1,0:T(8,128)S(1)}, f32[8,8,128]{2,1,0:T(8,128)S(1)}, u32[]{:S(2)}, u32[]{:S(2)}) %collective-permute-start.9) | collective-permute-done | bytes 32800 | tf_op jit(solution)/shard_map/ppermute | solution.py:337
  92.7 5.7 %collective-permute-done.8.da_ref = f32[8,8,128]{2,1,0:T(8,128)S(1)} collective-permute-done((f32[8,8,128]{2,1,0:T(8,128)S(1)}, f32[8,8,128]{2,1,0:T(8,128)S(1)}, u32[]{:S(2)}, u32[]{:S(2)}) %collective-permute-start.8) | collective-permute-done | bytes 32800 | tf_op jit(solution)/shard_map/ppermute | solution.py:333
  98.4 1.5 %shard_map.81 = (f32[8,8,128]{2,1,0:T(8,128)S(1)}, f32[8,8,128]{2,1,0:T(8,128)S(1)}) custom-call(f32[8,8,128]{2,1,0:T(8,128)S(1)} %get-tuple-element.46.ca_ref, f32[8,8,128]{2,1,0:T(8,128)S(1)} %get-tuple-element.47.cb_ref, f32[8,8,128]{2,1,0:T(8,128)S(1)} %collective-permute-done.8.da_ref, f32[8,8,128]{2,1,0:T(8,128)S(1)} %collective-permute-done.9.db_ref, ...), custom_call_target="tpu_custom_call" | custom-call | flops 1000000 | bytes 1000000 | tf_op jit(solution)/shard_map/pallas_call | solution.py:24
  100.0 0.1 collective-permute-start.11
  100.1 1.4 %collective-permute-start.10 = (f32[8,8,128]{2,1,0:T(8,128)S(1)}, f32[8,8,128]{2,1,0:T(8,128)S(1)}, u32[]{:S(2)}, u32[]{:S(2)}) collective-permute-start(f32[8,8,128]{2,1,0:T(8,128)S(1)} %get-tuple-element.49.lb_ref), channel_id=1, source_target_pairs={{0,1},{1,2},{2,3},{3,4},{4,5},{5,6},{6,7},{7,8},{8,9},{9,10},{10,1... | collective-permute-start | bytes 98312 | tf_op jit(solution)/shard_map/ppermute | solution.py:333
  101.5 1.3 %collective-permute-done.11.rb_ref = f32[8,8,128]{2,1,0:T(8,128)S(1)} collective-permute-done((f32[8,8,128]{2,1,0:T(8,128)S(1)}, f32[8,8,128]{2,1,0:T(8,128)S(1)}, u32[]{:S(2)}, u32[]{:S(2)}) %collective-permute-start.11) | collective-permute-done | bytes 32800 | tf_op jit(solution)/shard_map/ppermute | solution.py:337
  102.8 5.5 %collective-permute-done.10.ra_ref = f32[8,8,128]{2,1,0:T(8,128)S(1)} collective-permute-done((f32[8,8,128]{2,1,0:T(8,128)S(1)}, f32[8,8,128]{2,1,0:T(8,128)S(1)}, u32[]{:S(2)}, u32[]{:S(2)}) %collective-permute-start.10) | collective-permute-done | bytes 32800 | tf_op jit(solution)/shard_map/ppermute | solution.py:333
  108.3 1.8 %shard_map.82 = f32[32,16,128]{2,1,0:T(8,128)} custom-call(s32[2]{0:T(128)S(1)} %copy-done.7, s32[2]{0:T(128)S(1)} %pad_add_fusion.place_ref, f32[8,8,128]{2,1,0:T(8,128)S(1)} %get-tuple-element.48.la_ref, f32[8,8,128]{2,1,0:T(8,128)S(1)} %get-tuple-element.49.lb_ref, f32[8,8,128]{2,1,0:T(8,128)S(1)} %collective-permute-done.10.ra_ref, ...), custom_call_target="tpu_custom_call" | custom-call | flops 1000000 | bytes 1000000 | tf_op jit(solution)/shard_map/pallas_call | solution.py:24
  (5 shorter events, 0.0 us)
Async XLA Ops:
  0.0 0.7 copy-start.7
  0.7 0.9 copy-start
  2.5 1.2 %copy-start.2 = (f32[32,4,2,1024]{3,2,1,0:T(2,128)S(1)}, f32[32,4,2,1024]{3,2,1,0:T(2,128)}, u32[]{:S(2)}) copy-start(f32[32,4,2,1024]{3,2,1,0:T(2,128)} %param.8) | copy-start | bytes 3145732
  3.9 68.9 %collective-permute-start.7 = (f32[128,8,128]{2,1,0:T(8,128)S(1)}, f32[128,8,128]{2,1,0:T(8,128)S(1)}, u32[]{:S(2)}, u32[]{:S(2)}) collective-permute-start(f32[128,8,128]{2,1,0:T(8,128)S(1)} %get-tuple-element.33.e0_ref), channel_id=1, source_target_pairs={{0,191},{1,0},{2,1},{3,2},{4,3},{5,4},{6,5},{7,6},{8,7},{9,8},{10,... | collective-permute-start | bytes 1572872 | tf_op jit(solution)/shard_map/ppermute | solution.py:337
  15.0 57.7 %collective-permute-start.6 = (f32[128,8,128]{2,1,0:T(8,128)S(1)}, f32[128,8,128]{2,1,0:T(8,128)S(1)}, u32[]{:S(2)}, u32[]{:S(2)}) collective-permute-start(f32[128,8,128]{2,1,0:T(8,128)S(1)} %get-tuple-element.34.e1_ref), channel_id=1, source_target_pairs={{0,1},{1,2},{2,3},{3,4},{4,5},{5,6},{6,7},{7,8},{8,9},{9,10},{10,1... | collective-permute-start | bytes 1572872 | tf_op jit(solution)/shard_map/ppermute | solution.py:333
  15.0 13.4 %collective-permute-start.1 = (f32[32,8,128]{2,1,0:T(8,128)S(1)}, f32[32,8,128]{2,1,0:T(8,128)S(1)}, u32[]{:S(2)}, u32[]{:S(2)}) collective-permute-start(f32[32,8,128]{2,1,0:T(8,128)S(1)} %get-tuple-element.30.w0_ref), channel_id=1, source_target_pairs={{0,191},{1,0},{2,1},{3,2},{4,3},{5,4},{6,5},{7,6},{8,7},{9,8},{10,... | collective-permute-start | bytes 393224 | tf_op jit(solution)/shard_map/ppermute | solution.py:337
  21.9 13.9 %collective-permute-start = (f32[32,8,128]{2,1,0:T(8,128)S(1)}, f32[32,8,128]{2,1,0:T(8,128)S(1)}, u32[]{:S(2)}, u32[]{:S(2)}) collective-permute-start(f32[32,8,128]{2,1,0:T(8,128)S(1)} %get-tuple-element.31.w1_ref), channel_id=1, source_target_pairs={{0,1},{1,2},{2,3},{3,4},{4,5},{5,6},{6,7},{7,8},{8,9},{9,10},{10,1... | collective-permute-start | bytes 393224 | tf_op jit(solution)/shard_map/ppermute | solution.py:333
  35.8 19.1 %copy-start.5 = (s32[4,4,2048]{2,1,0:T(4,128)S(1)}, s32[4,4,2048]{2,1,0:T(4,128)}, u32[]{:S(2)}) copy-start(s32[4,4,2048]{2,1,0:T(4,128)} %param.12) | copy-start | bytes 393220
  35.8 19.1 %copy-start.6 = (f32[4,4,2048]{2,1,0:T(4,128)S(1)}, f32[4,4,2048]{2,1,0:T(4,128)}, u32[]{:S(2)}) copy-start(f32[4,4,2048]{2,1,0:T(4,128)} %param.13) | copy-start | bytes 393220
  36.5 18.4 %copy-start.3 = (s32[4,4,2048]{2,1,0:T(4,128)S(1)}, s32[4,4,2048]{2,1,0:T(4,128)}, u32[]{:S(2)}) copy-start(s32[4,4,2048]{2,1,0:T(4,128)} %param.10) | copy-start | bytes 393220
  36.5 18.4 %copy-start.4 = (f32[4,4,2048]{2,1,0:T(4,128)S(1)}, f32[4,4,2048]{2,1,0:T(4,128)}, u32[]{:S(2)}) copy-start(f32[4,4,2048]{2,1,0:T(4,128)} %param.11) | copy-start | bytes 393220
  48.0 8.1 %collective-permute-start.2 = (f32[4,8,128]{2,1,0:T(8,128)S(1)}, f32[4,8,128]{2,1,0:T(8,128)S(1)}, u32[]{:S(2)}, u32[]{:S(2)}) collective-permute-start(f32[4,8,128]{2,1,0:T(8,128)S(1)} %get-tuple-element.35.c1_ref), channel_id=1, source_target_pairs={{0,1},{1,2},{2,3},{3,4},{4,5},{5,6},{6,7},{7,8},{8,9},{9,10},{10,1... | collective-permute-start | bytes 49160 | tf_op jit(solution)/shard_map/ppermute | solution.py:333
  48.0 8.0 %collective-permute-start.3 = (f32[4,8,128]{2,1,0:T(8,128)S(1)}, f32[4,8,128]{2,1,0:T(8,128)S(1)}, u32[]{:S(2)}, u32[]{:S(2)}) collective-permute-start(f32[4,8,128]{2,1,0:T(8,128)S(1)} %get-tuple-element.36.c0_ref), channel_id=1, source_target_pairs={{0,191},{1,0},{2,1},{3,2},{4,3},{5,4},{6,5},{7,6},{8,7},{9,8},{10,... | collective-permute-start | bytes 49160 | tf_op jit(solution)/shard_map/ppermute | solution.py:337
  56.1 16.7 %copy-start.1 = (f32[32,2,1024]{2,1,0:T(2,128)S(1)}, f32[32,2,1024]{2,1,0:T(2,128)}, u32[]{:S(2)}) copy-start(f32[32,2,1024]{2,1,0:T(2,128)} %param.7) | copy-start | bytes 786436
  57.6 8.0 %collective-permute-start.5 = (f32[8,8,128]{2,1,0:T(8,128)S(1)}, f32[8,8,128]{2,1,0:T(8,128)S(1)}, u32[]{:S(2)}, u32[]{:S(2)}) collective-permute-start(f32[8,8,128]{2,1,0:T(8,128)S(1)} %get-tuple-element.42.la_ref), channel_id=1, source_target_pairs={{0,191},{1,0},{2,1},{3,2},{4,3},{5,4},{6,5},{7,6},{8,7},{9,8},{10,... | collective-permute-start | bytes 98312 | tf_op jit(solution)/shard_map/ppermute | solution.py:337
  64.6 8.2 %collective-permute-start.4 = (f32[8,8,128]{2,1,0:T(8,128)S(1)}, f32[8,8,128]{2,1,0:T(8,128)S(1)}, u32[]{:S(2)}, u32[]{:S(2)}) collective-permute-start(f32[8,8,128]{2,1,0:T(8,128)S(1)} %get-tuple-element.43.lb_ref), channel_id=1, source_target_pairs={{0,1},{1,2},{2,3},{3,4},{4,5},{5,6},{6,7},{7,8},{8,9},{9,10},{10,1... | collective-permute-start | bytes 98312 | tf_op jit(solution)/shard_map/ppermute | solution.py:333
  89.9 2.8 %collective-permute-start.9 = (f32[8,8,128]{2,1,0:T(8,128)S(1)}, f32[8,8,128]{2,1,0:T(8,128)S(1)}, u32[]{:S(2)}, u32[]{:S(2)}) collective-permute-start(f32[8,8,128]{2,1,0:T(8,128)S(1)} %get-tuple-element.46.ca_ref), channel_id=1, source_target_pairs={{0,191},{1,0},{2,1},{3,2},{4,3},{5,4},{6,5},{7,6},{8,7},{9,8},{10,... | collective-permute-start | bytes 98312 | tf_op jit(solution)/shard_map/ppermute | solution.py:337
  90.0 8.5 %collective-permute-start.8 = (f32[8,8,128]{2,1,0:T(8,128)S(1)}, f32[8,8,128]{2,1,0:T(8,128)S(1)}, u32[]{:S(2)}, u32[]{:S(2)}) collective-permute-start(f32[8,8,128]{2,1,0:T(8,128)S(1)} %get-tuple-element.47.cb_ref), channel_id=1, source_target_pairs={{0,1},{1,2},{2,3},{3,4},{4,5},{5,6},{6,7},{7,8},{8,9},{9,10},{10,1... | collective-permute-start | bytes 98312 | tf_op jit(solution)/shard_map/ppermute | solution.py:333
  100.0 2.8 %collective-permute-start.11 = (f32[8,8,128]{2,1,0:T(8,128)S(1)}, f32[8,8,128]{2,1,0:T(8,128)S(1)}, u32[]{:S(2)}, u32[]{:S(2)}) collective-permute-start(f32[8,8,128]{2,1,0:T(8,128)S(1)} %get-tuple-element.48.la_ref), channel_id=1, source_target_pairs={{0,191},{1,0},{2,1},{3,2},{4,3},{5,4},{6,5},{7,6},{8,7},{9,8},{10,... | collective-permute-start | bytes 98312 | tf_op jit(solution)/shard_map/ppermute | solution.py:337
  100.1 8.2 %collective-permute-start.10 = (f32[8,8,128]{2,1,0:T(8,128)S(1)}, f32[8,8,128]{2,1,0:T(8,128)S(1)}, u32[]{:S(2)}, u32[]{:S(2)}) collective-permute-start(f32[8,8,128]{2,1,0:T(8,128)S(1)} %get-tuple-element.49.lb_ref), channel_id=1, source_target_pairs={{0,1},{1,2},{2,3},{3,4},{4,5},{5,6},{6,7},{7,8},{8,9},{9,10},{10,1... | collective-permute-start | bytes 98312 | tf_op jit(solution)/shard_map/ppermute | solution.py:333

commit v3 on v2

--- a/solution.py
+++ b/solution.py
@@ -60,60 +60,76 @@
     return product(widened(x), band).reshape(x.shape) * scale
 
 
-def scale_of(widths_ref, r):
-    width = jnp.full((8, 128), widths_ref[r], jnp.int32)
-    return 1.0 / (2.0 * width.astype(F32) + 1.0)
-
-
-def if_inside(place_ref, above, below):
-    band = jnp.full((8, 128), place_ref[0], jnp.int32)
-    last = jnp.full((8, 128), place_ref[1], jnp.int32)
-    return jnp.where(band > 0, above, 0.0), jnp.where(band < last, below, 0.0)
-
-
-def filter_kernel(widths_ref, v_ref, w0_ref, w1_ref, band_ref):
+def width_of(widths_ref, place_ref, r):
+    return widths_ref[r + place_ref[0] * (1 - 2 * r)]
+
+
+def scale_of(width):
+    return 1.0 / (2.0 * jnp.full((8, 128), width, jnp.int32).astype(F32) + 1.0)
+
+
+def if_inside(place_ref, x):
+    return jnp.where(jnp.full((8, 128), place_ref[1], jnp.int32) > 0, x, 0.0)
+
+
+def if_odd(place_ref, odd, even):
+    return jnp.where(jnp.full((8, 128), place_ref[0], jnp.int32) > 0, odd, even)
+
+
+def filter_kernel(widths_ref, place_ref, v_ref, w0_ref, w1_ref, old_ref, band_ref):
     away = jnp.abs(position(iota((256, 128), 0)) - iota((256, 128), 1))
     for r, out in ((0, w0_ref), (1, w1_ref)):
-        inside = away <= jnp.full((256, 128), widths_ref[r], jnp.int32)
+        width = width_of(widths_ref, place_ref, r)
+        inside = away <= jnp.full((256, 128), width, jnp.int32)
         band = jnp.where(inside, 1.0, 0.0).astype(jnp.bfloat16)
         band_ref[r] = band
-        scale = scale_of(widths_ref, r)
         for b in range(2):
-            x = v_ref[pl.ds(b * 16, 16), pl.ds(r, 8, stride=2), :]
-            out[pl.ds(b * 16, 16)] = filtered(x, band, scale)
-
-
-def split_kernel(e_ref, e0_ref, e1_ref):
+            at = pl.ds(b * 16, 16)
+            top, bottom = (v_ref[at, pl.ds(n, 8, stride=2), :] for n in range(2))
+            x = if_odd(place_ref, top, bottom) if r else if_odd(place_ref, bottom, top)
+            old_ref[r, at] = x
+            out[at] = filtered(x, band, scale_of(width))
+
+
+def split_kernel(place_ref, e_ref, e0_ref, e1_ref):
     def body(b, carry):
         at = pl.ds(b * 8, 8)
-        e0_ref[at] = e_ref[at, pl.ds(0, 8, stride=2), :]
-        e1_ref[at] = e_ref[at, pl.ds(1, 8, stride=2), :]
+        top, bottom = (e_ref[at, pl.ds(n, 8, stride=2), :] for n in range(2))
+        e0_ref[at] = if_odd(place_ref, bottom, top)
+        e1_ref[at] = if_odd(place_ref, top, bottom)
         return carry
 
     lax.fori_loop(0, 16, body, 0)
 
 
-def planes_kernel(src_ref, wgt_ref, msk_ref, inn_ref, planes_ref, mask_ref, target_ref, refine_ref, gather_ref):
+def planes_kernel(place_ref, src_ref, wgt_ref, msk_ref, inn_ref, planes_ref, mask_ref, target_ref, refine_ref, gather_ref):
     parent = iota((8, 128), 0) * 128 + iota((8, 128), 1) // 2
+    odd = jnp.full((8, 128), place_ref[0], jnp.int32)
     for j in range(8):
         half, fr = j // 4, j % 4
-        at = pl.ds(j, 8, stride=8)
+        at, mirrored = pl.ds(j, 8, stride=8), pl.ds(half * 4 + 3 - fr, 8, stride=8)
+
+        def row(ref, n, at=at, mirrored=mirrored):
+            return jnp.where(odd > 0, ref[n, mirrored, :], ref[n, at, :])
+
+        own_row = jnp.where(odd > 0, 1 - fr // 2, fr // 2)
         codes, weights = [], []
         for s in range(4):
-            src = src_ref[s, at, :]
-            row_shift = lax.shift_right_logical(src, 10) - (fr // 2 + 1)
+            src = row(src_ref, s)
+            row_shift = lax.shift_right_logical(src, 10) - (own_row + 1)
+            row_shift = jnp.where(odd > 0, -row_shift, row_shift)
             col = jnp.bitwise_and(src, 1023)
             col_shift = jnp.bitwise_and(col - parent - half * 64 + 2, 1023) - 2
             codes.append((row_shift + 1) * 5 + col_shift + 2)
-            weights.append(wgt_ref[s, at, :])
+            weights.append(row(wgt_ref, s))
         for n in range(15):
             total = jnp.where(codes[0] == n, weights[0], 0.0)
             for s in range(1, 4):
                 total = total + jnp.where(codes[s] == n, weights[s], 0.0)
             planes_ref[n, j] = total
         for t in range(4):
-            mask_ref[t, j] = msk_ref[t, at, :].astype(F32)
-            target_ref[t, j] = inn_ref[t, at, :]
+            mask_ref[t, j] = row(msk_ref, t).astype(F32)
+            target_ref[t, j] = row(inn_ref, t)
     for n in range(10):
         d, half = n // 2 - 2, n % 2
         source = half * 64 + iota((256, 128), 1) // 2 + d
@@ -124,12 +140,11 @@
         gather_ref[n * 128 : n * 128 + 128, :] = jnp.where(hit, 1.0, 0.0).astype(jnp.bfloat16)
 
 
-def first_kernel(place_ref, w0_ref, w1_ref, above_ref, below_ref, e0_ref, e1_ref, part_ref):
+def first_kernel(place_ref, w0_ref, w1_ref, far_ref, near_ref, e0_ref, e1_ref, part_ref):
     def body(m, sums):
         a, b = w0_ref[m], w1_ref[m]
-        above, below = if_inside(place_ref, above_ref[m], below_ref[m])
-        f0 = C_MID * a + C_SIDE * (above + b)
-        f1 = C_MID * b + C_SIDE * (a + below)
+        f0 = C_MID * a + C_SIDE * (if_inside(place_ref, far_ref[m]) + b)
+        f1 = C_MID * b + C_SIDE * (a + near_ref[m])
         sums = list(sums)
         for t in range(4):
             sums[t] = sums[t] + e0_ref[m * 4 + t] * f0
@@ -162,7 +177,7 @@
     return 0.5 * a + 0.25 * (left_a + right_a), 0.5 * b + 0.25 * (left_b + right_b)
 
 
-def observe(rows, planes_ref, mask_ref, target_ref, refine_ref, gather_ref, u_ref, la_ref, lb_ref):
+def observe(rows, planes_ref, mask_ref, target_ref, refine_ref, gather_ref, u_ref, far_ref, near_ref):
     window = jnp.stack([rows[t][q] for t in range(4) for q in range(4)])
     u_ref[...] = product(widened(window), refine_ref[...])
 
@@ -212,38 +227,35 @@
     head = iota((16, 8, 128), 2) < 64
     landed = own + jnp.where(head, pltpu.roll(beside, 1, 1), pltpu.roll(beside, 7, 1))
     for t in range(4):
-        la_ref[t], la_ref[4 + t] = landed[t * 4], landed[t * 4 + 1]
-        lb_ref[t], lb_ref[4 + t] = landed[t * 4 + 2], landed[t * 4 + 3]
-
-
-def first_observe_kernel(above_ref, c0_ref, c1_ref, below_ref, *refs):
-    observe([[ref[t] for ref in (above_ref, c0_ref, c1_ref, below_ref)] for t in range(4)], *order(refs))
-
-
-def second_observe_kernel(ca_ref, cb_ref, da_ref, db_ref, *refs):
-    rows = [
-        [
-            mine[half * 4 + t] + theirs[half * 4 + t]
-            for mine, theirs in ((ca_ref, da_ref), (cb_ref, db_ref))
-            for half in range(2)
-        ]
-        for t in range(4)
-    ]
-    observe(rows, *order(refs))
+        far_ref[t], far_ref[4 + t] = landed[t * 4], landed[t * 4 + 1]
+        near_ref[t], near_ref[4 + t] = landed[t * 4 + 3], landed[t * 4 + 2]
+
+
+def first_observe_kernel(far_ref, c0_ref, c1_ref, near_ref, *refs):
+    observe([[ref[t] for ref in (far_ref, c0_ref, c1_ref, near_ref)] for t in range(4)], *order(refs))
+
+
+def second_observe_kernel(*refs):
+    rows = joined(*refs[:4])
+    observe([[rows[q][t] for q in range(4)] for t in range(4)], *order(refs[4:]))
 
 
 def order(refs):
-    *fields, la_ref, lb_ref, u_ref = refs
-    return *fields, u_ref, la_ref, lb_ref
-
-
-def adjoint_rows(place_ref, la_ref, lb_ref, ra_ref, rb_ref):
-    rows = []
-    for mine, theirs in ((la_ref, ra_ref), (lb_ref, rb_ref)):
-        for half in range(2):
-            rows.append([mine[half * 4 + t] + theirs[half * 4 + t] for t in range(4)])
-    for t in range(4):
-        rows[0][t], rows[3][t] = if_inside(place_ref, rows[0][t], rows[3][t])
+    *fields, far_ref, near_ref, u_ref = refs
+    return *fields, u_ref, far_ref, near_ref
+
+
+def joined(far_ref, near_ref, from_far_ref, from_near_ref):
+    rows = [None] * 4
+    for mine, theirs, halo, own in ((far_ref, from_far_ref, 0, 1), (near_ref, from_near_ref, 3, 2)):
+        rows[halo] = [mine[t] + theirs[4 + t] for t in range(4)]
+        rows[own] = [mine[4 + t] + theirs[t] for t in range(4)]
+    return rows
+
+
+def adjoint_rows(place_ref, refs):
+    rows = joined(*refs)
+    rows[0] = [if_inside(place_ref, x) for x in rows[0]]
     return rows
 
 
@@ -264,17 +276,17 @@
 
 
 def middle_kernel(
-    widths_ref, place_ref, la_ref, lb_ref, ra_ref, rb_ref, em_ref, e0_ref, e1_ref, ep_ref,
+    widths_ref, place_ref, lf_ref, ln_ref, rf_ref, rn_ref, ef_ref, e0_ref, e1_ref, en_ref,
     band_ref, v_ref, new_ref, part_ref, s_ref,
 ):
-    rows = adjoint_rows(place_ref, la_ref, lb_ref, ra_ref, rb_ref)
-    e_refs = (em_ref, e0_ref, e1_ref, ep_ref)
+    rows = adjoint_rows(place_ref, (lf_ref, ln_ref, rf_ref, rn_ref))
+    e_refs = (ef_ref, e0_ref, e1_ref, en_ref)
     smoothed_back(e_refs, rows, s_ref)
     for r in range(2):
-        scale = scale_of(widths_ref, r)
+        scale = scale_of(width_of(widths_ref, place_ref, r))
         for b in range(2):
             at = pl.ds(b * 16, 16)
-            old = v_ref[at, pl.ds(r, 8, stride=2), :]
+            old = v_ref[r, at]
             gradient = old + filtered(s_ref[r, at], band_ref[r], scale)
             new = old - STEP_SIZE * gradient
             new_ref[r, at] = new
@@ -298,43 +310,36 @@
 
     sums = list(lax.fori_loop(0, 8, body, (jnp.zeros((8, 128), F32),) * 16))
     for t in range(4):
-        sums[t], sums[12 + t] = if_inside(place_ref, sums[t], sums[12 + t])
-    for n in range(16):
-        part_ref[n] = sums[n]
+        part_ref[t], part_ref[4 + t] = if_inside(place_ref, sums[t]), sums[4 + t]
+        part_ref[8 + t], part_ref[12 + t] = sums[12 + t], sums[8 + t]
 
 
 def last_kernel(
-    widths_ref, place_ref, la_ref, lb_ref, ra_ref, rb_ref, em_ref, e0_ref, e1_ref, ep_ref,
+    widths_ref, place_ref, lf_ref, ln_ref, rf_ref, rn_ref, ef_ref, e0_ref, e1_ref, en_ref,
     band_ref, v_ref, out_ref, s_ref,
 ):
-    rows = adjoint_rows(place_ref, la_ref, lb_ref, ra_ref, rb_ref)
-    smoothed_back((em_ref, e0_ref, e1_ref, ep_ref), rows, s_ref)
+    rows = adjoint_rows(place_ref, (lf_ref, ln_ref, rf_ref, rn_ref))
+    smoothed_back((ef_ref, e0_ref, e1_ref, en_ref), rows, s_ref)
     for r in range(2):
-        scale = scale_of(widths_ref, r)
+        scale = scale_of(width_of(widths_ref, place_ref, r))
         for b in range(2):
             at = pl.ds(b * 16, 16)
             old = v_ref[r, at]
             gradient = old + filtered(s_ref[r, at], band_ref[r], scale)
-            out_ref[at, pl.ds(r, 8, stride=2), :] = old - STEP_SIZE * gradient
-
-
-def ring(step):
-    groups, bands = lax.axis_size("mem"), lax.axis_size("lat")
-    pairs = []
-    for m in range(groups):
-        for i in range(bands):
-            inside = 0 <= i + step < bands
-            other = m if inside else (m + groups // 2) % groups
-            pairs.append((m * bands + i, other * bands + (i + step) % bands))
-    return pairs
-
-
-def to_next(x):
-    return lax.ppermute(x, ("mem", "lat"), ring(1))
-
-
-def to_previous(x):
-    return lax.ppermute(x, ("mem", "lat"), ring(-1))
+            s_ref[r, at] = old - STEP_SIZE * gradient
+    for b in range(2):
+        at = pl.ds(b * 16, 16)
+        out_ref[at, pl.ds(0, 8, stride=2), :] = if_odd(place_ref, s_ref[1, at], s_ref[0, at])
+        out_ref[at, pl.ds(1, 8, stride=2), :] = if_odd(place_ref, s_ref[0, at], s_ref[1, at])
+
+
+def swapped(far, near):
+    bands = lax.axis_size("lat")
+    ends = (0, bands - 1)
+    pairs = [(i, i if i in ends else i + (1 if i % 2 else -1)) for i in range(bands)]
+    far = lax.ppermute(far, "lat", pairs)
+    near = lax.ppermute(near, "lat", [(i, i ^ 1) for i in range(bands)])
+    return far, near
 
 
 def tiles(x):
@@ -346,14 +351,16 @@
 def descent(control, ensemble, widths, interp_source, interp_weight, obs_mask, innovation):
     v = tiles(control)
     e = tiles(ensemble)
-    place = jnp.stack([lax.axis_index("lat"), lax.axis_size("lat") - 1]).astype(jnp.int32)
-    row = shape(32, 8, 128)
+    lat, last = lax.axis_index("lat"), lax.axis_size("lat") - 1
+    place = jnp.stack([lat % 2, (lat != 0) & (lat != last)]).astype(jnp.int32)
+    scalars = (widths, place)
+    row, rows = shape(32, 8, 128), shape(2, 32, 8, 128)
     band = jax.ShapeDtypeStruct((2, 256, 128), jnp.bfloat16)
-    w0, w1, band = call(filter_kernel, (row, row, band), (v,), (widths,))
-    above, below = to_next(w1), to_previous(w0)
+    w0, w1, old, band = call(filter_kernel, (row, row, rows, band), (v,), scalars)
+    far, near = swapped(w0, w1)
     e, w0, w1 = lax.optimization_barrier((e, w0, w1))
-    e0, e1 = call(split_kernel, (shape(128, 8, 128),) * 2, (e,))
-    e_above, e_below = to_next(e1), to_previous(e0)
+    e0, e1 = call(split_kernel, (shape(128, 8, 128),) * 2, (e,), (place,))
+    e_far, e_near = swapped(e0, e1)
     fields = call(
         planes_kernel,
         (
@@ -364,40 +371,37 @@
             jax.ShapeDtypeStruct((1280, 256), jnp.bfloat16),
         ),
         tuple(tiles(x) for x in (interp_source, interp_weight, obs_mask, innovation)),
-    )
-    part = call(first_kernel, shape(8, 8, 128), (w0, w1, above, below, e0, e1), (place,))
+        (place,),
+    )
+    part = call(first_kernel, shape(8, 8, 128), (w0, w1, far, near, e0, e1), (place,))
     four, eight = shape(4, 8, 128), shape(8, 8, 128)
     c0, c1 = call(sum_kernel, (four, four), (lax.all_gather(part, "mem"),))
+    far, near = swapped(c0, c1)
     refined = ((128, 1280),)
-    la, lb = call(
-        first_observe_kernel,
-        (eight, eight),
-        (to_next(c1), c0, c1, to_previous(c0)) + tuple(fields),
-        scratch=refined,
-    )
-    ra, rb = to_next(lb), to_previous(la)
-    ensembles = (e_above, e0, e1, e_below, band)
+    sent = call(
+        first_observe_kernel, (eight, eight), (far, c0, c1, near) + tuple(fields), scratch=refined
+    )
+    ensembles = (e_far, e0, e1, e_near, band)
     smoothed = ((2, 32, 8, 128),)
     new, part = call(
         middle_kernel,
-        (shape(2, 32, 8, 128), shape(16, 8, 128)),
-        (la, lb, ra, rb) + ensembles + (v,),
-        (widths, place),
+        (rows, shape(16, 8, 128)),
+        tuple(sent) + swapped(*sent) + ensembles + (old,),
+        scalars,
         smoothed,
     )
-    ca, cb = call(sum_kernel, (eight, eight), (lax.all_gather(part, "mem"),))
-    la, lb = call(
+    sent = call(sum_kernel, (eight, eight), (lax.all_gather(part, "mem"),))
+    sent = call(
         second_observe_kernel,
         (eight, eight),
-        (ca, cb, to_next(cb), to_previous(ca)) + tuple(fields),
+        tuple(sent) + swapped(*sent) + tuple(fields),
         scratch=refined,
     )
-    ra, rb = to_next(lb), to_previous(la)
     out = call(
         last_kernel,
         shape(32, 16, 128),
-        (la, lb, ra, rb) + ensembles + (new,),
-        (widths, place),
+        tuple(sent) + swapped(*sent) + ensembles + (new,),
+        scalars,
         smoothed,
     )
     return out.reshape(32, 8, 2, 128).transpose(0, 2, 1, 3).reshape(control.shape)

time: 110 us -> 97.5 us (0.89)
  the two profiles are of different devices: /device:TPU:1 before, /device:TPU:30 now
where the time goes in v3:
time: 97.5 us; the launch traced here: 95.8 us
  waiting for transfers between devices  33.5 us (34%)
  starting transfers between devices  27.8 us (29%)
  blocking collectives  21.1 us (22%)
  Pallas kernels  10.3 us (11%)
  local copies, waits for them, and re-layouts  2.84 us (3%)
    ppermute x6, waiting for transfers between devices, swapped(): far = lax.ppermute(far, 'lat', pairs)  33.4 us
    ppermute x6, starting transfers between devices, swapped(): far = lax.ppermute(far, 'lat', pairs)  27.3 us
    all_gather x1, blocking collectives, descent(): c0, c1 = call(sum_kernel, (four, four), (lax.all_gather(part, 'mem'),))  11 us
    pallas_call x10, Pallas kernels, call(): pl.pallas_call(kernel, out_shape=outs, in_specs=in_specs, out_specs=jax.t...  10.3 us
    all_gather x1, blocking collectives, descent(): sent = call(sum_kernel, (eight, eight), (lax.all_gather(part, 'mem'),))  10.1 us
    unnamed x14, local copies, waits for them, and re-layouts  2.84 us
  transfers between devices with their start and end apart: 12, of which 5 were waited for; matrix products, arithmetic and copies ran while one was open for 0% of the time, Pallas kernels for 3%

profile of v3, /device:TPU:30, one launch (start us, length us, event | category | flops | bytes accessed | tf_op | source)
XLA Modules:
  0.0 95.8 jit_solution(6103890094056056239)
XLA Ops:
  0.0 0.1 pad_add_fusion.place_ref
  0.1 0.0 copy-start.6
  0.1 0.7 copy-done.6
  0.7 0.0 copy-start.1
  0.7 0.9 copy-done.1
  1.7 0.9 shard_map.73
  2.6 0.0 copy-start
  2.6 1.2 %copy-done = f32[32,4,2,1024]{3,2,1,0:T(2,128)S(1)} copy-done((f32[32,4,2,1024]{3,2,1,0:T(2,128)S(1)}, f32[32,4,2,1024]{3,2,1,0:T(2,128)}, u32[]{:S(2)}) %copy-start) | copy-done | bytes 1048600
  3.8 0.7 shard_map.74
  4.5 3.4 %collective-permute-start.6 = (f32[128,8,128]{2,1,0:T(8,128)S(1)}, f32[128,8,128]{2,1,0:T(8,128)S(1)}, u32[]{:S(2)}, u32[]{:S(2)}) collective-permute-start(f32[128,8,128]{2,1,0:T(8,128)S(1)} %get-tuple-element.34.e0_ref), channel_id=1, source_target_pairs={{0,0},{1,2},{2,1},{3,4},{4,3},{5,6},{6,5},{7,8},{8,7},{9,10},{10,9... | collective-permute-start | bytes 1572872 | tf_op jit(solution)/shard_map/ppermute | solution.py:340
  7.9 0.1 collective-permute-start.7
  8.0 6.7 %collective-permute-start = (f32[32,8,128]{2,1,0:T(8,128)S(1)}, f32[32,8,128]{2,1,0:T(8,128)S(1)}, u32[]{:S(2)}, u32[]{:S(2)}) collective-permute-start(f32[32,8,128]{2,1,0:T(8,128)S(1)} %get-tuple-element.31.w0_ref), channel_id=1, source_target_pairs={{0,0},{1,2},{2,1},{3,4},{4,3},{5,6},{6,5},{7,8},{8,7},{9,10},{10,9... | collective-permute-start | bytes 393224 | tf_op jit(solution)/shard_map/ppermute | solution.py:340
  14.7 0.1 collective-permute-start.1
  14.8 12.3 %collective-permute-done.far_ref = f32[32,8,128]{2,1,0:T(8,128)S(1)} collective-permute-done((f32[32,8,128]{2,1,0:T(8,128)S(1)}, f32[32,8,128]{2,1,0:T(8,128)S(1)}, u32[]{:S(2)}, u32[]{:S(2)}) %collective-permute-start) | collective-permute-done | bytes 131104 | tf_op jit(solution)/shard_map/ppermute | solution.py:340
  27.1 0.0 collective-permute-done.1.near_ref
  27.1 0.0 copy-start.4
  27.1 0.7 shard_map.75
  27.8 0.0 copy-start.2
  27.8 0.0 copy-start.3
  27.9 11.0 %all-gather = f32[32,8,128]{2,1,0:T(8,128)S(1)} all-gather(f32[8,8,128]{2,1,0:T(8,128)S(1)} %shard_map.75), channel_id=2, replica_groups=mesh['mem'=4,'lat'=64] {'mem'}, dimensions={0}, use_global_device_ids=true | all-gather | bytes 163840 | tf_op jit(solution)/shard_map/all_gather | solution.py:378
  38.8 3.7 %collective-permute-start.2 = (f32[4,8,128]{2,1,0:T(8,128)S(1)}, f32[4,8,128]{2,1,0:T(8,128)S(1)}, u32[]{:S(2)}, u32[]{:S(2)}) collective-permute-start(f32[4,8,128]{2,1,0:T(8,128)S(1)} %get-tuple-element.36.c0_ref), channel_id=1, source_target_pairs={{0,0},{1,2},{2,1},{3,4},{4,3},{5,6},{6,5},{7,8},{8,7},{9,10},{10,9... | collective-permute-start | bytes 49160 | tf_op jit(solution)/shard_map/ppermute | solution.py:340
  42.5 0.1 collective-permute-start.3
  42.6 0.0 copy-done.4
  42.6 0.0 copy-done.5
  42.6 0.0 copy-done.2
  42.6 0.0 copy-done.3
  42.6 1.1 %shard_map.77 = (f32[15,8,8,128]{3,2,1,0:T(8,128)S(1)}, f32[4,8,8,128]{3,2,1,0:T(8,128)S(1)}, f32[4,8,8,128]{3,2,1,0:T(8,128)S(1)}, bf16[256,1280]{1,0:T(8,128)(2,1)S(1)}, bf16[1280,256]{1,0:T(8,128)(2,1)S(1)}) custom-call(s32[2]{0:T(128)S(1)} %pad_add_fusion.place_ref, s32[4,64,128]{2,1,0:T(8,128)S(1)} %bitcast.43, f32[4,64,128]{2,1,0:T(8,128)S(1)} %bitcast.44, ...), custom_call_target="tpu_custom_call" | custom-call | flops 1000000 | bytes 1000000 | tf_op jit(solution)/shard_map/pallas_call | solution.py:24
  43.8 4.9 %collective-permute-done.2.far_ref = f32[4,8,128]{2,1,0:T(8,128)S(1)} collective-permute-done((f32[4,8,128]{2,1,0:T(8,128)S(1)}, f32[4,8,128]{2,1,0:T(8,128)S(1)}, u32[]{:S(2)}, u32[]{:S(2)}) %collective-permute-start.2) | collective-permute-done | bytes 16416 | tf_op jit(solution)/shard_map/ppermute | solution.py:340
  48.7 0.0 collective-permute-done.3.near_ref
  48.7 1.5 %shard_map.78 = (f32[8,8,128]{2,1,0:T(8,128)S(1)}, f32[8,8,128]{2,1,0:T(8,128)S(1)}) custom-call(f32[4,8,128]{2,1,0:T(8,128)S(1)} %collective-permute-done.2.far_ref, f32[4,8,128]{2,1,0:T(8,128)S(1)} %get-tuple-element.36.c0_ref, f32[4,8,128]{2,1,0:T(8,128)S(1)} %get-tuple-element.37.c1_ref, f32[4,8,128]{2,1,0:T(8,128)S(1)} %collective-permute-done.3.near_ref, ...), custom_call_target="tpu_custom_call" | custom-call | flops 1000000 | bytes 1000000 | tf_op jit(solution)/shard_map/pallas_call | solution.py:24
  50.2 4.0 %collective-permute-start.4 = (f32[8,8,128]{2,1,0:T(8,128)S(1)}, f32[8,8,128]{2,1,0:T(8,128)S(1)}, u32[]{:S(2)}, u32[]{:S(2)}) collective-permute-start(f32[8,8,128]{2,1,0:T(8,128)S(1)} %get-tuple-element.43.lf_ref), channel_id=1, source_target_pairs={{0,0},{1,2},{2,1},{3,4},{4,3},{5,6},{6,5},{7,8},{8,7},{9,10},{10,9... | collective-permute-start | bytes 98312 | tf_op jit(solution)/shard_map/ppermute | solution.py:340
  54.3 0.1 collective-permute-start.5
  54.4 5.9 %collective-permute-done.4.rf_ref = f32[8,8,128]{2,1,0:T(8,128)S(1)} collective-permute-done((f32[8,8,128]{2,1,0:T(8,128)S(1)}, f32[8,8,128]{2,1,0:T(8,128)S(1)}, u32[]{:S(2)}, u32[]{:S(2)}) %collective-permute-start.4) | collective-permute-done | bytes 32800 | tf_op jit(solution)/shard_map/ppermute | solution.py:340
  60.3 0.0 collective-permute-done.5.rn_ref
  60.3 0.0 collective-permute-done.6.ef_ref
  60.3 0.0 collective-permute-done.7.en_ref
  60.3 2.0 %shard_map.79 = (f32[2,32,8,128]{3,2,1,0:T(8,128)S(1)}, f32[16,8,128]{2,1,0:T(8,128)S(1)}) custom-call(s32[2]{0:T(128)S(1)} %copy-done.6, s32[2]{0:T(128)S(1)} %pad_add_fusion.place_ref, f32[8,8,128]{2,1,0:T(8,128)S(1)} %get-tuple-element.43.lf_ref, f32[8,8,128]{2,1,0:T(8,128)S(1)} %get-tuple-element.44.ln_ref, ...), custom_call_target="tpu_custom_call" | custom-call | flops 1000000 | bytes 1000000 | tf_op jit(solution)/shard_map/pallas_call | solution.py:24
  62.3 10.1 %all-gather.1 = f32[64,8,128]{2,1,0:T(8,128)S(1)} all-gather(f32[16,8,128]{2,1,0:T(8,128)S(1)} %get-tuple-element.47), channel_id=3, replica_groups=mesh['mem'=4,'lat'=64] {'mem'}, dimensions={0}, use_global_device_ids=true | all-gather | bytes 327680 | tf_op jit(solution)/shard_map/all_gather | solution.py:393
  72.4 4.8 %collective-permute-start.8 = (f32[8,8,128]{2,1,0:T(8,128)S(1)}, f32[8,8,128]{2,1,0:T(8,128)S(1)}, u32[]{:S(2)}, u32[]{:S(2)}) collective-permute-start(f32[8,8,128]{2,1,0:T(8,128)S(1)} %get-tuple-element.48.refs_0_), channel_id=1, source_target_pairs={{0,0},{1,2},{2,1},{3,4},{4,3},{5,6},{6,5},{7,8},{8,7},{9,10},{10,9... | collective-permute-start | bytes 98312 | tf_op jit(solution)/shard_map/ppermute | solution.py:340
  77.2 0.1 collective-permute-start.9
  77.3 5.2 %collective-permute-done.8.refs_2_ = f32[8,8,128]{2,1,0:T(8,128)S(1)} collective-permute-done((f32[8,8,128]{2,1,0:T(8,128)S(1)}, f32[8,8,128]{2,1,0:T(8,128)S(1)}, u32[]{:S(2)}, u32[]{:S(2)}) %collective-permute-start.8) | collective-permute-done | bytes 32800 | tf_op jit(solution)/shard_map/ppermute | solution.py:340
  82.5 0.0 collective-permute-done.9.refs_3_
  82.5 1.5 %shard_map.81 = (f32[8,8,128]{2,1,0:T(8,128)S(1)}, f32[8,8,128]{2,1,0:T(8,128)S(1)}) custom-call(f32[8,8,128]{2,1,0:T(8,128)S(1)} %get-tuple-element.48.refs_0_, f32[8,8,128]{2,1,0:T(8,128)S(1)} %get-tuple-element.49.refs_1_, f32[8,8,128]{2,1,0:T(8,128)S(1)} %collective-permute-done.8.refs_2_, f32[8,8,128]{2,1,0:T(8,128)S(1)} %collective-permute-done.9.refs_3_, ...), custom_call_target="tpu_custom_call" | custom-call | flops 1000000 | bytes 1000000 | tf_op jit(solution)/shard_map/pallas_call | solution.py:24
  84.0 4.8 %collective-permute-start.10 = (f32[8,8,128]{2,1,0:T(8,128)S(1)}, f32[8,8,128]{2,1,0:T(8,128)S(1)}, u32[]{:S(2)}, u32[]{:S(2)}) collective-permute-start(f32[8,8,128]{2,1,0:T(8,128)S(1)} %get-tuple-element.50.lf_ref), channel_id=1, source_target_pairs={{0,0},{1,2},{2,1},{3,4},{4,3},{5,6},{6,5},{7,8},{8,7},{9,10},{10,9... | collective-permute-start | bytes 98312 | tf_op jit(solution)/shard_map/ppermute | solution.py:340
  88.8 0.1 collective-permute-start.11
  88.9 5.2 %collective-permute-done.10.rf_ref = f32[8,8,128]{2,1,0:T(8,128)S(1)} collective-permute-done((f32[8,8,128]{2,1,0:T(8,128)S(1)}, f32[8,8,128]{2,1,0:T(8,128)S(1)}, u32[]{:S(2)}, u32[]{:S(2)}) %collective-permute-start.10) | collective-permute-done | bytes 32800 | tf_op jit(solution)/shard_map/ppermute | solution.py:340
  94.0 0.0 collective-permute-done.11.rn_ref
  94.0 1.8 %shard_map.82 = f32[32,16,128]{2,1,0:T(8,128)} custom-call(s32[2]{0:T(128)S(1)} %copy-done.6, s32[2]{0:T(128)S(1)} %pad_add_fusion.place_ref, f32[8,8,128]{2,1,0:T(8,128)S(1)} %get-tuple-element.50.lf_ref, f32[8,8,128]{2,1,0:T(8,128)S(1)} %get-tuple-element.51.ln_ref, f32[8,8,128]{2,1,0:T(8,128)S(1)} %collective-permute-done.10.rf_ref, ...), custom_call_target="tpu_custom_call" | custom-call | flops 1000000 | bytes 1000000 | tf_op jit(solution)/shard_map/pallas_call | solution.py:24
  (3 shorter events, 0.0 us)
Async XLA Ops:
  0.1 0.7 copy-start.6
  0.7 0.9 copy-start.1
  2.6 1.2 %copy-start = (f32[32,4,2,1024]{3,2,1,0:T(2,128)S(1)}, f32[32,4,2,1024]{3,2,1,0:T(2,128)}, u32[]{:S(2)}) copy-start(f32[32,4,2,1024]{3,2,1,0:T(2,128)} %param.8) | copy-start | bytes 3145732
  4.5 55.7 %collective-permute-start.6 = (f32[128,8,128]{2,1,0:T(8,128)S(1)}, f32[128,8,128]{2,1,0:T(8,128)S(1)}, u32[]{:S(2)}, u32[]{:S(2)}) collective-permute-start(f32[128,8,128]{2,1,0:T(8,128)S(1)} %get-tuple-element.34.e0_ref), channel_id=1, source_target_pairs={{0,0},{1,2},{2,1},{3,4},{4,3},{5,6},{6,5},{7,8},{8,7},{9,10},{10,9... | collective-permute-start | bytes 1572872 | tf_op jit(solution)/shard_map/ppermute | solution.py:340
  7.9 52.3 %collective-permute-start.7 = (f32[128,8,128]{2,1,0:T(8,128)S(1)}, f32[128,8,128]{2,1,0:T(8,128)S(1)}, u32[]{:S(2)}, u32[]{:S(2)}) collective-permute-start(f32[128,8,128]{2,1,0:T(8,128)S(1)} %get-tuple-element.35.e1_ref), channel_id=1, source_target_pairs={{0,1},{1,0},{2,3},{3,2},{4,5},{5,4},{6,7},{7,6},{8,9},{9,8},{10,11... | collective-permute-start | bytes 1572872 | tf_op jit(solution)/shard_map/ppermute | solution.py:341
  8.0 19.1 %collective-permute-start = (f32[32,8,128]{2,1,0:T(8,128)S(1)}, f32[32,8,128]{2,1,0:T(8,128)S(1)}, u32[]{:S(2)}, u32[]{:S(2)}) collective-permute-start(f32[32,8,128]{2,1,0:T(8,128)S(1)} %get-tuple-element.31.w0_ref), channel_id=1, source_target_pairs={{0,0},{1,2},{2,1},{3,4},{4,3},{5,6},{6,5},{7,8},{8,7},{9,10},{10,9... | collective-permute-start | bytes 393224 | tf_op jit(solution)/shard_map/ppermute | solution.py:340
  14.7 12.4 %collective-permute-start.1 = (f32[32,8,128]{2,1,0:T(8,128)S(1)}, f32[32,8,128]{2,1,0:T(8,128)S(1)}, u32[]{:S(2)}, u32[]{:S(2)}) collective-permute-start(f32[32,8,128]{2,1,0:T(8,128)S(1)} %get-tuple-element.32.w1_ref), channel_id=1, source_target_pairs={{0,1},{1,0},{2,3},{3,2},{4,5},{5,4},{6,7},{7,6},{8,9},{9,8},{10,11... | collective-permute-start | bytes 393224 | tf_op jit(solution)/shard_map/ppermute | solution.py:341
  27.1 15.5 %copy-start.4 = (s32[4,4,2048]{2,1,0:T(4,128)S(1)}, s32[4,4,2048]{2,1,0:T(4,128)}, u32[]{:S(2)}) copy-start(s32[4,4,2048]{2,1,0:T(4,128)} %param.12) | copy-start | bytes 393220
  27.1 15.5 %copy-start.5 = (f32[4,4,2048]{2,1,0:T(4,128)S(1)}, f32[4,4,2048]{2,1,0:T(4,128)}, u32[]{:S(2)}) copy-start(f32[4,4,2048]{2,1,0:T(4,128)} %param.13) | copy-start | bytes 393220
  27.8 14.8 %copy-start.2 = (s32[4,4,2048]{2,1,0:T(4,128)S(1)}, s32[4,4,2048]{2,1,0:T(4,128)}, u32[]{:S(2)}) copy-start(s32[4,4,2048]{2,1,0:T(4,128)} %param.10) | copy-start | bytes 393220
  27.8 14.8 %copy-start.3 = (f32[4,4,2048]{2,1,0:T(4,128)S(1)}, f32[4,4,2048]{2,1,0:T(4,128)}, u32[]{:S(2)}) copy-start(f32[4,4,2048]{2,1,0:T(4,128)} %param.11) | copy-start | bytes 393220
  38.8 9.9 %collective-permute-start.2 = (f32[4,8,128]{2,1,0:T(8,128)S(1)}, f32[4,8,128]{2,1,0:T(8,128)S(1)}, u32[]{:S(2)}, u32[]{:S(2)}) collective-permute-start(f32[4,8,128]{2,1,0:T(8,128)S(1)} %get-tuple-element.36.c0_ref), channel_id=1, source_target_pairs={{0,0},{1,2},{2,1},{3,4},{4,3},{5,6},{6,5},{7,8},{8,7},{9,10},{10,9... | collective-permute-start | bytes 49160 | tf_op jit(solution)/shard_map/ppermute | solution.py:340
  42.5 6.2 %collective-permute-start.3 = (f32[4,8,128]{2,1,0:T(8,128)S(1)}, f32[4,8,128]{2,1,0:T(8,128)S(1)}, u32[]{:S(2)}, u32[]{:S(2)}) collective-permute-start(f32[4,8,128]{2,1,0:T(8,128)S(1)} %get-tuple-element.37.c1_ref), channel_id=1, source_target_pairs={{0,1},{1,0},{2,3},{3,2},{4,5},{5,4},{6,7},{7,6},{8,9},{9,8},{10,11... | collective-permute-start | bytes 49160 | tf_op jit(solution)/shard_map/ppermute | solution.py:341
  50.2 10.0 %collective-permute-start.4 = (f32[8,8,128]{2,1,0:T(8,128)S(1)}, f32[8,8,128]{2,1,0:T(8,128)S(1)}, u32[]{:S(2)}, u32[]{:S(2)}) collective-permute-start(f32[8,8,128]{2,1,0:T(8,128)S(1)} %get-tuple-element.43.lf_ref), channel_id=1, source_target_pairs={{0,0},{1,2},{2,1},{3,4},{4,3},{5,6},{6,5},{7,8},{8,7},{9,10},{10,9... | collective-permute-start | bytes 98312 | tf_op jit(solution)/shard_map/ppermute | solution.py:340
  54.3 6.0 %collective-permute-start.5 = (f32[8,8,128]{2,1,0:T(8,128)S(1)}, f32[8,8,128]{2,1,0:T(8,128)S(1)}, u32[]{:S(2)}, u32[]{:S(2)}) collective-permute-start(f32[8,8,128]{2,1,0:T(8,128)S(1)} %get-tuple-element.44.ln_ref), channel_id=1, source_target_pairs={{0,1},{1,0},{2,3},{3,2},{4,5},{5,4},{6,7},{7,6},{8,9},{9,8},{10,11... | collective-permute-start | bytes 98312 | tf_op jit(solution)/shard_map/ppermute | solution.py:341
  72.4 10.0 %collective-permute-start.8 = (f32[8,8,128]{2,1,0:T(8,128)S(1)}, f32[8,8,128]{2,1,0:T(8,128)S(1)}, u32[]{:S(2)}, u32[]{:S(2)}) collective-permute-start(f32[8,8,128]{2,1,0:T(8,128)S(1)} %get-tuple-element.48.refs_0_), channel_id=1, source_target_pairs={{0,0},{1,2},{2,1},{3,4},{4,3},{5,6},{6,5},{7,8},{8,7},{9,10},{10,9... | collective-permute-start | bytes 98312 | tf_op jit(solution)/shard_map/ppermute | solution.py:340
  77.2 5.3 %collective-permute-start.9 = (f32[8,8,128]{2,1,0:T(8,128)S(1)}, f32[8,8,128]{2,1,0:T(8,128)S(1)}, u32[]{:S(2)}, u32[]{:S(2)}) collective-permute-start(f32[8,8,128]{2,1,0:T(8,128)S(1)} %get-tuple-element.49.refs_1_), channel_id=1, source_target_pairs={{0,1},{1,0},{2,3},{3,2},{4,5},{5,4},{6,7},{7,6},{8,9},{9,8},{10,11... | collective-permute-start | bytes 98312 | tf_op jit(solution)/shard_map/ppermute | solution.py:341
  84.0 10.0 %collective-permute-start.10 = (f32[8,8,128]{2,1,0:T(8,128)S(1)}, f32[8,8,128]{2,1,0:T(8,128)S(1)}, u32[]{:S(2)}, u32[]{:S(2)}) collective-permute-start(f32[8,8,128]{2,1,0:T(8,128)S(1)} %get-tuple-element.50.lf_ref), channel_id=1, source_target_pairs={{0,0},{1,2},{2,1},{3,4},{4,3},{5,6},{6,5},{7,8},{8,7},{9,10},{10,9... | collective-permute-start | bytes 98312 | tf_op jit(solution)/shard_map/ppermute | solution.py:340
  88.8 5.3 %collective-permute-start.11 = (f32[8,8,128]{2,1,0:T(8,128)S(1)}, f32[8,8,128]{2,1,0:T(8,128)S(1)}, u32[]{:S(2)}, u32[]{:S(2)}) collective-permute-start(f32[8,8,128]{2,1,0:T(8,128)S(1)} %get-tuple-element.51.ln_ref), channel_id=1, source_target_pairs={{0,1},{1,0},{2,3},{3,2},{4,5},{5,4},{6,7},{7,6},{8,9},{9,8},{10,11... | collective-permute-start | bytes 98312 | tf_op jit(solution)/shard_map/ppermute | solution.py:341

commit v4 on v3

--- a/solution.py
+++ b/solution.py
@@ -1,5 +1,6 @@
 import jax
 import jax.numpy as jnp
+import numpy as np
 from jax import lax
 from jax.experimental import pallas as pl
 from jax.experimental.pallas import tpu as pltpu
@@ -40,6 +41,14 @@
     return jnp.where(k < 128, k, jnp.where(k < 192, k, k - 256))
 
 
+def refining_matrix():
+    k = np.arange(256)
+    place = np.where(k < 128, k, np.where(k < 192, k, k - 256))
+    n, lane = np.arange(1280) // 128, np.arange(1280) % 128
+    source = n % 2 * 64 + lane // 2 + n // 2 - 2
+    return jnp.asarray(place[:, None] == source[None, :], jnp.bfloat16)
+
+
 def widened(x):
     n = x.shape[0]
     y = jnp.where(iota(x.shape, 2) < 64, pltpu.roll(x, 7, 1), pltpu.roll(x, 1, 1))
@@ -60,10 +69,6 @@
     return product(widened(x), band).reshape(x.shape) * scale
 
 
-def width_of(widths_ref, place_ref, r):
-    return widths_ref[r + place_ref[0] * (1 - 2 * r)]
-
-
 def scale_of(width):
     return 1.0 / (2.0 * jnp.full((8, 128), width, jnp.int32).astype(F32) + 1.0)
 
@@ -76,10 +81,10 @@
     return jnp.where(jnp.full((8, 128), place_ref[0], jnp.int32) > 0, odd, even)
 
 
-def filter_kernel(widths_ref, place_ref, v_ref, w0_ref, w1_ref, old_ref, band_ref):
+def filter_kernel(place_ref, v_ref, w0_ref, w1_ref, old_ref, band_ref):
     away = jnp.abs(position(iota((256, 128), 0)) - iota((256, 128), 1))
     for r, out in ((0, w0_ref), (1, w1_ref)):
-        width = width_of(widths_ref, place_ref, r)
+        width = place_ref[2 + r]
         inside = away <= jnp.full((256, 128), width, jnp.int32)
         band = jnp.where(inside, 1.0, 0.0).astype(jnp.bfloat16)
         band_ref[r] = band
@@ -91,18 +96,20 @@
             out[at] = filtered(x, band, scale_of(width))
 
 
-def split_kernel(place_ref, e_ref, e0_ref, e1_ref):
-    def body(b, carry):
-        at = pl.ds(b * 8, 8)
-        top, bottom = (e_ref[at, pl.ds(n, 8, stride=2), :] for n in range(2))
-        e0_ref[at] = if_odd(place_ref, bottom, top)
-        e1_ref[at] = if_odd(place_ref, top, bottom)
-        return carry
-
-    lax.fori_loop(0, 16, body, 0)
-
-
-def planes_kernel(place_ref, src_ref, wgt_ref, msk_ref, inn_ref, planes_ref, mask_ref, target_ref, refine_ref, gather_ref):
+def split_kernel(place_ref, e_ref, *out_refs):
+    for half in range(2):
+
+        def body(b, carry, half=half):
+            at = pl.ds(half * 64 + b * 8, 8)
+            top, bottom = (e_ref[at, pl.ds(n, 8, stride=2), :] for n in range(2))
+            out_refs[half][pl.ds(b * 8, 8)] = if_odd(place_ref, bottom, top)
+            out_refs[2 + half][pl.ds(b * 8, 8)] = if_odd(place_ref, top, bottom)
+            return carry
+
+        lax.fori_loop(0, 8, body, 0)
+
+
+def planes_kernel(place_ref, src_ref, wgt_ref, msk_ref, inn_ref, planes_ref, mask_ref, target_ref):
     parent = iota((8, 128), 0) * 128 + iota((8, 128), 1) // 2
     odd = jnp.full((8, 128), place_ref[0], jnp.int32)
     for j in range(8):
@@ -130,28 +137,25 @@
         for t in range(4):
             mask_ref[t, j] = row(msk_ref, t).astype(F32)
             target_ref[t, j] = row(inn_ref, t)
-    for n in range(10):
-        d, half = n // 2 - 2, n % 2
-        source = half * 64 + iota((256, 128), 1) // 2 + d
-        hit = position(iota((256, 128), 0)) == source
-        refine_ref[:, n * 128 : n * 128 + 128] = jnp.where(hit, 1.0, 0.0).astype(jnp.bfloat16)
-        source = half * 64 + iota((128, 256), 0) // 2 + d
-        hit = position(iota((128, 256), 1)) == source
-        gather_ref[n * 128 : n * 128 + 128, :] = jnp.where(hit, 1.0, 0.0).astype(jnp.bfloat16)
-
-
-def first_kernel(place_ref, w0_ref, w1_ref, far_ref, near_ref, e0_ref, e1_ref, part_ref):
-    def body(m, sums):
-        a, b = w0_ref[m], w1_ref[m]
-        f0 = C_MID * a + C_SIDE * (if_inside(place_ref, far_ref[m]) + b)
-        f1 = C_MID * b + C_SIDE * (a + near_ref[m])
-        sums = list(sums)
-        for t in range(4):
-            sums[t] = sums[t] + e0_ref[m * 4 + t] * f0
-            sums[4 + t] = sums[4 + t] + e1_ref[m * 4 + t] * f1
-        return tuple(sums)
-
-    sums = lax.fori_loop(0, 32, body, (jnp.zeros((8, 128), F32),) * 8, unroll=4)
+
+
+def first_kernel(place_ref, w0_ref, w1_ref, far_ref, near_ref, *refs):
+    *e_refs, part_ref = refs
+    sums = (jnp.zeros((8, 128), F32),) * 8
+    for half in range(2):
+
+        def body(n, sums, half=half):
+            m = half * 16 + n
+            a, b = w0_ref[m], w1_ref[m]
+            f0 = C_MID * a + C_SIDE * (if_inside(place_ref, far_ref[m]) + b)
+            f1 = C_MID * b + C_SIDE * (a + near_ref[m])
+            sums = list(sums)
+            for t in range(4):
+                sums[t] = sums[t] + e_refs[half][n * 4 + t] * f0
+                sums[4 + t] = sums[4 + t] + e_refs[2 + half][n * 4 + t] * f1
+            return tuple(sums)
+
+        sums = lax.fori_loop(0, 16, body, sums, unroll=4)
     for n in range(8):
         part_ref[n] = sums[n]
 
@@ -260,30 +264,30 @@
 
 
 def smoothed_back(e_refs, rows, s_ref):
-    def body(b, carry):
-        back = []
-        for q in range(4):
-            x = e_refs[q][pl.ds(b * 16, 16)].reshape(4, 4, 8, 128)
-            total = x[:, 0] * rows[q][0]
-            for t in range(1, 4):
-                total = total + x[:, t] * rows[q][t]
-            back.append(total)
-        for r in range(2):
-            s_ref[r, pl.ds(b * 4, 4)] = C_MID * back[r + 1] + C_SIDE * (back[r] + back[r + 2])
-        return carry
-
-    lax.fori_loop(0, 8, body, 0, unroll=2)
-
-
-def middle_kernel(
-    widths_ref, place_ref, lf_ref, ln_ref, rf_ref, rn_ref, ef_ref, e0_ref, e1_ref, en_ref,
-    band_ref, v_ref, new_ref, part_ref, s_ref,
-):
+    for half in range(2):
+
+        def body(b, carry, half=half):
+            back = []
+            for q in range(4):
+                x = e_refs[q * 2 + half][pl.ds(b * 16, 16)].reshape(4, 4, 8, 128)
+                total = x[:, 0] * rows[q][0]
+                for t in range(1, 4):
+                    total = total + x[:, t] * rows[q][t]
+                back.append(total)
+            at = pl.ds(half * 16 + b * 4, 4)
+            for r in range(2):
+                s_ref[r, at] = C_MID * back[r + 1] + C_SIDE * (back[r] + back[r + 2])
+            return carry
+
+        lax.fori_loop(0, 4, body, 0, unroll=2)
+
+
+def middle_kernel(place_ref, lf_ref, ln_ref, rf_ref, rn_ref, *refs):
+    *e_refs, band_ref, v_ref, new_ref, part_ref, s_ref = refs
     rows = adjoint_rows(place_ref, (lf_ref, ln_ref, rf_ref, rn_ref))
-    e_refs = (ef_ref, e0_ref, e1_ref, en_ref)
     smoothed_back(e_refs, rows, s_ref)
     for r in range(2):
-        scale = scale_of(width_of(widths_ref, place_ref, r))
+        scale = scale_of(place_ref[2 + r])
         for b in range(2):
             at = pl.ds(b * 16, 16)
             old = v_ref[r, at]
@@ -291,37 +295,38 @@
             new = old - STEP_SIZE * gradient
             new_ref[r, at] = new
             s_ref[r, at] = filtered(new, band_ref[r], scale)
-
-    def body(b, sums):
-        sums = list(sums)
-        for i in range(4):
-            m = b * 4 + i
-            w = [s_ref[r, m] for r in range(2)]
-            forward = [
-                C_SIDE * w[0],
-                C_MID * w[0] + C_SIDE * w[1],
-                C_MID * w[1] + C_SIDE * w[0],
-                C_SIDE * w[1],
-            ]
-            for q in range(4):
-                for t in range(4):
-                    sums[q * 4 + t] = sums[q * 4 + t] + e_refs[q][m * 4 + t] * forward[q]
-        return tuple(sums)
-
-    sums = list(lax.fori_loop(0, 8, body, (jnp.zeros((8, 128), F32),) * 16))
+    sums = (jnp.zeros((8, 128), F32),) * 16
+    for half in range(2):
+
+        def body(b, sums, half=half):
+            sums = list(sums)
+            for i in range(4):
+                n = b * 4 + i
+                w = [s_ref[r, half * 16 + n] for r in range(2)]
+                forward = [
+                    C_SIDE * w[0],
+                    C_MID * w[0] + C_SIDE * w[1],
+                    C_MID * w[1] + C_SIDE * w[0],
+                    C_SIDE * w[1],
+                ]
+                for q in range(4):
+                    for t in range(4):
+                        x = e_refs[q * 2 + half][n * 4 + t]
+                        sums[q * 4 + t] = sums[q * 4 + t] + x * forward[q]
+            return tuple(sums)
+
+        sums = lax.fori_loop(0, 4, body, sums)
     for t in range(4):
         part_ref[t], part_ref[4 + t] = if_inside(place_ref, sums[t]), sums[4 + t]
         part_ref[8 + t], part_ref[12 + t] = sums[12 + t], sums[8 + t]
 
 
-def last_kernel(
-    widths_ref, place_ref, lf_ref, ln_ref, rf_ref, rn_ref, ef_ref, e0_ref, e1_ref, en_ref,
-    band_ref, v_ref, out_ref, s_ref,
-):
+def last_kernel(place_ref, lf_ref, ln_ref, rf_ref, rn_ref, *refs):
+    *e_refs, band_ref, v_ref, out_ref, s_ref = refs
     rows = adjoint_rows(place_ref, (lf_ref, ln_ref, rf_ref, rn_ref))
-    smoothed_back((ef_ref, e0_ref, e1_ref, en_ref), rows, s_ref)
+    smoothed_back(e_refs, rows, s_ref)
     for r in range(2):
-        scale = scale_of(width_of(widths_ref, place_ref, r))
+        scale = scale_of(place_ref[2 + r])
         for b in range(2):
             at = pl.ds(b * 16, 16)
             old = v_ref[r, at]
@@ -333,13 +338,18 @@
         out_ref[at, pl.ds(1, 8, stride=2), :] = if_odd(place_ref, s_ref[0, at], s_ref[1, at])
 
 
+def from_far(x):
+    bands = lax.axis_size("lat")
+    pairs = [(i, i if i in (0, bands - 1) else i + (1 if i % 2 else -1)) for i in range(bands)]
+    return lax.ppermute(x, "lat", pairs)
+
+
+def from_near(x):
+    return lax.ppermute(x, "lat", [(i, i ^ 1) for i in range(lax.axis_size("lat"))])
+
+
 def swapped(far, near):
-    bands = lax.axis_size("lat")
-    ends = (0, bands - 1)
-    pairs = [(i, i if i in ends else i + (1 if i % 2 else -1)) for i in range(bands)]
-    far = lax.ppermute(far, "lat", pairs)
-    near = lax.ppermute(near, "lat", [(i, i ^ 1) for i in range(bands)])
-    return far, near
+    return from_far(far), from_near(near)
 
 
 def tiles(x):
@@ -352,36 +362,39 @@
     v = tiles(control)
     e = tiles(ensemble)
     lat, last = lax.axis_index("lat"), lax.axis_size("lat") - 1
-    place = jnp.stack([lat % 2, (lat != 0) & (lat != last)]).astype(jnp.int32)
-    scalars = (widths, place)
+    odd = lat % 2
+    ends = jnp.stack([odd, (lat != 0) & (lat != last)]).astype(jnp.int32)
+    place = jnp.concatenate([ends, jnp.where(odd > 0, widths[::-1], widths)])
+    scalars = (place,)
     row, rows = shape(32, 8, 128), shape(2, 32, 8, 128)
     band = jax.ShapeDtypeStruct((2, 256, 128), jnp.bfloat16)
     w0, w1, old, band = call(filter_kernel, (row, row, rows, band), (v,), scalars)
     far, near = swapped(w0, w1)
-    e, w0, w1 = lax.optimization_barrier((e, w0, w1))
-    e0, e1 = call(split_kernel, (shape(128, 8, 128),) * 2, (e,), (place,))
-    e_far, e_near = swapped(e0, e1)
+    e0, e0_late, e1, e1_late = call(split_kernel, (shape(64, 8, 128),) * 4, (e,), scalars)
+    ensembles = (
+        *(from_far(e0), from_far(e0_late)),
+        *(e0, e0_late, e1, e1_late),
+        *(from_near(e1), from_near(e1_late)),
+        band,
+    )
     fields = call(
         planes_kernel,
-        (
-            shape(15, 8, 8, 128),
-            shape(4, 8, 8, 128),
-            shape(4, 8, 8, 128),
-            jax.ShapeDtypeStruct((256, 1280), jnp.bfloat16),
-            jax.ShapeDtypeStruct((1280, 256), jnp.bfloat16),
-        ),
+        (shape(15, 8, 8, 128), shape(4, 8, 8, 128), shape(4, 8, 8, 128)),
         tuple(tiles(x) for x in (interp_source, interp_weight, obs_mask, innovation)),
-        (place,),
-    )
-    part = call(first_kernel, shape(8, 8, 128), (w0, w1, far, near, e0, e1), (place,))
+        scalars,
+    )
+    refine = refining_matrix()
+    fields = tuple(fields) + (refine, refine.T)
+    part = call(
+        first_kernel, shape(8, 8, 128), (w0, w1, far, near, e0, e0_late, e1, e1_late), scalars
+    )
     four, eight = shape(4, 8, 128), shape(8, 8, 128)
     c0, c1 = call(sum_kernel, (four, four), (lax.all_gather(part, "mem"),))
     far, near = swapped(c0, c1)
     refined = ((128, 1280),)
     sent = call(
-        first_observe_kernel, (eight, eight), (far, c0, c1, near) + tuple(fields), scratch=refined
-    )
-    ensembles = (e_far, e0, e1, e_near, band)
+        first_observe_kernel, (eight, eight), (far, c0, c1, near) + fields, scratch=refined
+    )
     smoothed = ((2, 32, 8, 128),)
     new, part = call(
         middle_kernel,
@@ -394,7 +407,7 @@
     sent = call(
         second_observe_kernel,
         (eight, eight),
-        tuple(sent) + swapped(*sent) + tuple(fields),
+        tuple(sent) + swapped(*sent) + fields,
         scratch=refined,
     )
     out = call(

time: 97.5 us -> 102 us (1.046)
  the two profiles are of different devices: /device:TPU:30 before, /device:TPU:32 now
where the time goes in v4:
time: 102 us; the launch traced here: 101 us
  starting transfers between devices  40.4 us (40%)
  waiting for transfers between devices  25.2 us (25%)
  blocking collectives  22.6 us (22%)
  Pallas kernels  10 us (10%)
  local copies, waits for them, and re-layouts  2.95 us (3%)
    ppermute x7, starting transfers between devices, from_far(): return lax.ppermute(x, 'lat', pairs)  38 us
    ppermute x7, waiting for transfers between devices, from_far(): return lax.ppermute(x, 'lat', pairs)  18.4 us
    all_gather x1, blocking collectives, descent(): c0, c1 = call(sum_kernel, (four, four), (lax.all_gather(part, 'mem'),))  11.5 us
    all_gather x1, blocking collectives, descent(): sent = call(sum_kernel, (eight, eight), (lax.all_gather(part, 'mem'),))  11.1 us
    pallas_call x10, Pallas kernels, call(): pl.pallas_call(kernel, out_shape=outs, in_specs=in_specs, out_specs=jax.t...  10 us
    ppermute x7, waiting for transfers between devices, from_near(): lax.ppermute(x, 'lat', [(i, i ^ 1) for i in range(lax.axis_size('lat'))])  6.78 us
    unnamed x18, local copies, waits for them, and re-layouts  2.86 us
    ppermute x7, starting transfers between devices, from_near(): lax.ppermute(x, 'lat', [(i, i ^ 1) for i in range(lax.axis_size('lat'))])  2.38 us
  transfers between devices with their start and end apart: 14, of which 6 were waited for; matrix products, arithmetic and copies ran while one was open for 0% of the time, Pallas kernels for 4%

profile of v4, /device:TPU:32, one launch (start us, length us, event | category | flops | bytes accessed | tf_op | source)
XLA Modules:
  0.0 101.5 jit_solution(9801627012208562722)
XLA Ops:
  0.0 0.7 copy-done.8
  0.7 0.1 rev.3
  0.8 0.1 pad_add_fusion.place_ref
  0.8 0.9 copy-done.3
  1.8 0.9 shard_map.82
  2.7 6.7 %collective-permute-start = (f32[32,8,128]{2,1,0:T(8,128)S(1)}, f32[32,8,128]{2,1,0:T(8,128)S(1)}, u32[]{:S(2)}, u32[]{:S(2)}) collective-permute-start(f32[32,8,128]{2,1,0:T(8,128)S(1)} %get-tuple-element.26.w0_ref), channel_id=1, source_target_pairs={{0,0},{1,2},{2,1},{3,4},{4,3},{5,6},{6,5},{7,8},{8,7},{9,10},{10,9... | collective-permute-start | bytes 393224 | tf_op jit(solution)/shard_map/ppermute | solution.py:344
  9.4 0.1 collective-permute-start.1
  9.5 0.0 copy-start.2
  9.5 1.2 %copy-done.2 = f32[32,4,2,1024]{3,2,1,0:T(2,128)S(1)} copy-done((f32[32,4,2,1024]{3,2,1,0:T(2,128)S(1)}, f32[32,4,2,1024]{3,2,1,0:T(2,128)}, u32[]{:S(2)}) %copy-start.2) | copy-done | bytes 1048600
  10.7 0.7 shard_map.83
  11.4 3.4 %collective-permute-start.6 = (f32[64,8,128]{2,1,0:T(8,128)S(1)}, f32[64,8,128]{2,1,0:T(8,128)S(1)}, u32[]{:S(2)}, u32[]{:S(2)}) collective-permute-start(f32[64,8,128]{2,1,0:T(8,128)S(1)} %get-tuple-element.28.refs_0_.refs_2_), channel_id=1, source_target_pairs={{0,0},{1,2},{2,1},{3,4},{4,3},{5,6},{6,5},{7,8},{8,7},{9,10},{10,9... | collective-permute-start | bytes 786440 | tf_op jit(solution)/shard_map/ppermute | solution.py:344
  14.8 6.7 %collective-permute-start.7 = (f32[64,8,128]{2,1,0:T(8,128)S(1)}, f32[64,8,128]{2,1,0:T(8,128)S(1)}, u32[]{:S(2)}, u32[]{:S(2)}) collective-permute-start(f32[64,8,128]{2,1,0:T(8,128)S(1)} %get-tuple-element.29.refs_1_.refs_3_), channel_id=1, source_target_pairs={{0,0},{1,2},{2,1},{3,4},{4,3},{5,6},{6,5},{7,8},{8,7},{9,10},{10,9... | collective-permute-start | bytes 786440 | tf_op jit(solution)/shard_map/ppermute | solution.py:344
  21.5 0.1 collective-permute-start.8
  21.6 0.0 collective-permute-done.far_ref
  21.6 2.0 %collective-permute-start.9 = (f32[64,8,128]{2,1,0:T(8,128)S(1)}, f32[64,8,128]{2,1,0:T(8,128)S(1)}, u32[]{:S(2)}, u32[]{:S(2)}) collective-permute-start(f32[64,8,128]{2,1,0:T(8,128)S(1)} %get-tuple-element.31.refs_3_.refs_5_), channel_id=1, source_target_pairs={{0,1},{1,0},{2,3},{3,2},{4,5},{5,4},{6,7},{7,6},{8,9},{9,8},{10,11... | collective-permute-start | bytes 786440 | tf_op jit(solution)/shard_map/ppermute | solution.py:348
  23.6 0.0 collective-permute-done.1.near_ref
  23.6 0.0 copy-start.7
  23.6 0.0 copy-start.1
  23.7 0.7 shard_map.84
  24.4 0.0 copy-start
  24.4 11.5 %all-gather = f32[32,8,128]{2,1,0:T(8,128)S(1)} all-gather(f32[8,8,128]{2,1,0:T(8,128)S(1)} %shard_map.84), channel_id=2, replica_groups=mesh['mem'=4,'lat'=64] {'mem'}, dimensions={0}, use_global_device_ids=true | all-gather | bytes 163840 | tf_op jit(solution)/shard_map/all_gather | solution.py:392
  35.9 6.0 %collective-permute-start.2 = (f32[4,8,128]{2,1,0:T(8,128)S(1)}, f32[4,8,128]{2,1,0:T(8,128)S(1)}, u32[]{:S(2)}, u32[]{:S(2)}) collective-permute-start(f32[4,8,128]{2,1,0:T(8,128)S(1)} %get-tuple-element.32.c0_ref), channel_id=1, source_target_pairs={{0,0},{1,2},{2,1},{3,4},{4,3},{5,6},{6,5},{7,8},{8,7},{9,10},{10,9... | collective-permute-start | bytes 49160 | tf_op jit(solution)/shard_map/ppermute | solution.py:344
  41.9 3.8 %collective-permute-done.2.far_ref = f32[4,8,128]{2,1,0:T(8,128)S(1)} collective-permute-done((f32[4,8,128]{2,1,0:T(8,128)S(1)}, f32[4,8,128]{2,1,0:T(8,128)S(1)}, u32[]{:S(2)}, u32[]{:S(2)}) %collective-permute-start.2) | collective-permute-done | bytes 16416 | tf_op jit(solution)/shard_map/ppermute | solution.py:344
  45.7 0.0 collective-permute-start.3
  45.7 0.0 copy-done.4
  45.8 0.8 shard_map.86
  46.6 2.9 %collective-permute-done.3.near_ref = f32[4,8,128]{2,1,0:T(8,128)S(1)} collective-permute-done((f32[4,8,128]{2,1,0:T(8,128)S(1)}, f32[4,8,128]{2,1,0:T(8,128)S(1)}, u32[]{:S(2)}, u32[]{:S(2)}) %collective-permute-start.3) | collective-permute-done | bytes 16416 | tf_op jit(solution)/shard_map/ppermute | solution.py:348
  49.5 1.5 %shard_map.87 = (f32[8,8,128]{2,1,0:T(8,128)S(1)}, f32[8,8,128]{2,1,0:T(8,128)S(1)}) custom-call(f32[4,8,128]{2,1,0:T(8,128)S(1)} %collective-permute-done.2.far_ref, f32[4,8,128]{2,1,0:T(8,128)S(1)} %get-tuple-element.32.c0_ref, f32[4,8,128]{2,1,0:T(8,128)S(1)} %get-tuple-element.33.c1_ref, f32[4,8,128]{2,1,0:T(8,128)S(1)} %collective-permute-done.3.near_ref, ...), custom_call_target="tpu_custom_call" | custom-call | flops 1000000 | bytes 1000000 | tf_op jit(solution)/shard_map/pallas_call | solution.py:25
  51.0 6.0 %collective-permute-start.4 = (f32[8,8,128]{2,1,0:T(8,128)S(1)}, f32[8,8,128]{2,1,0:T(8,128)S(1)}, u32[]{:S(2)}, u32[]{:S(2)}) collective-permute-start(f32[8,8,128]{2,1,0:T(8,128)S(1)} %get-tuple-element.37.lf_ref), channel_id=1, source_target_pairs={{0,0},{1,2},{2,1},{3,4},{4,3},{5,6},{6,5},{7,8},{8,7},{9,10},{10,9... | collective-permute-start | bytes 98312 | tf_op jit(solution)/shard_map/ppermute | solution.py:344
  57.0 4.0 %collective-permute-done.4.rf_ref = f32[8,8,128]{2,1,0:T(8,128)S(1)} collective-permute-done((f32[8,8,128]{2,1,0:T(8,128)S(1)}, f32[8,8,128]{2,1,0:T(8,128)S(1)}, u32[]{:S(2)}, u32[]{:S(2)}) %collective-permute-start.4) | collective-permute-done | bytes 32800 | tf_op jit(solution)/shard_map/ppermute | solution.py:344
  61.0 0.0 collective-permute-start.5
  61.0 3.9 %collective-permute-done.5.rn_ref = f32[8,8,128]{2,1,0:T(8,128)S(1)} collective-permute-done((f32[8,8,128]{2,1,0:T(8,128)S(1)}, f32[8,8,128]{2,1,0:T(8,128)S(1)}, u32[]{:S(2)}, u32[]{:S(2)}) %collective-permute-start.5) | collective-permute-done | bytes 32800 | tf_op jit(solution)/shard_map/ppermute | solution.py:348
  64.9 0.0 collective-permute-done.6.refs_0_
  65.0 0.0 collective-permute-done.7.refs_1_
  65.0 0.0 collective-permute-done.8.refs_6_
  65.0 0.0 collective-permute-done.9.refs_7_
  65.0 2.0 %shard_map.88 = (f32[2,32,8,128]{3,2,1,0:T(8,128)S(1)}, f32[16,8,128]{2,1,0:T(8,128)S(1)}) custom-call(s32[4]{0:T(128)S(1)} %pad_add_fusion.place_ref, f32[8,8,128]{2,1,0:T(8,128)S(1)} %get-tuple-element.37.lf_ref, f32[8,8,128]{2,1,0:T(8,128)S(1)} %get-tuple-element.38.ln_ref, f32[8,8,128]{2,1,0:T(8,128)S(1)} %collective-permute-done.4.rf_ref, ...), custom_call_target="tpu_custom_call" | custom-call | flops 1000000 | bytes 1000000 | tf_op jit(solution)/shard_map/pallas_call | solution.py:25
  67.0 11.1 %all-gather.1 = f32[64,8,128]{2,1,0:T(8,128)S(1)} all-gather(f32[16,8,128]{2,1,0:T(8,128)S(1)} %get-tuple-element.41), channel_id=3, replica_groups=mesh['mem'=4,'lat'=64] {'mem'}, dimensions={0}, use_global_device_ids=true | all-gather | bytes 327680 | tf_op jit(solution)/shard_map/all_gather | solution.py:406
  78.1 4.6 %collective-permute-start.10 = (f32[8,8,128]{2,1,0:T(8,128)S(1)}, f32[8,8,128]{2,1,0:T(8,128)S(1)}, u32[]{:S(2)}, u32[]{:S(2)}) collective-permute-start(f32[8,8,128]{2,1,0:T(8,128)S(1)} %get-tuple-element.42.refs_0_), channel_id=1, source_target_pairs={{0,0},{1,2},{2,1},{3,4},{4,3},{5,6},{6,5},{7,8},{8,7},{9,10},{10,9... | collective-permute-start | bytes 98312 | tf_op jit(solution)/shard_map/ppermute | solution.py:344
  82.7 0.1 collective-permute-start.11
  82.8 5.3 %collective-permute-done.10.refs_2_ = f32[8,8,128]{2,1,0:T(8,128)S(1)} collective-permute-done((f32[8,8,128]{2,1,0:T(8,128)S(1)}, f32[8,8,128]{2,1,0:T(8,128)S(1)}, u32[]{:S(2)}, u32[]{:S(2)}) %collective-permute-start.10) | collective-permute-done | bytes 32800 | tf_op jit(solution)/shard_map/ppermute | solution.py:344
  88.1 0.0 collective-permute-done.11.refs_3_
  88.1 1.5 %shard_map.90 = (f32[8,8,128]{2,1,0:T(8,128)S(1)}, f32[8,8,128]{2,1,0:T(8,128)S(1)}) custom-call(f32[8,8,128]{2,1,0:T(8,128)S(1)} %get-tuple-element.42.refs_0_, f32[8,8,128]{2,1,0:T(8,128)S(1)} %get-tuple-element.43.refs_1_, f32[8,8,128]{2,1,0:T(8,128)S(1)} %collective-permute-done.10.refs_2_, f32[8,8,128]{2,1,0:T(8,128)S(1)} %collective-permute-done.11.refs_3_, ...), custom_call_target="tpu_custom_call" | custom-call | flops 1000000 | bytes 1000000 | tf_op jit(solution)/shard_map/pallas_call | solution.py:25
  89.7 4.6 %collective-permute-start.12 = (f32[8,8,128]{2,1,0:T(8,128)S(1)}, f32[8,8,128]{2,1,0:T(8,128)S(1)}, u32[]{:S(2)}, u32[]{:S(2)}) collective-permute-start(f32[8,8,128]{2,1,0:T(8,128)S(1)} %get-tuple-element.44.lf_ref), channel_id=1, source_target_pairs={{0,0},{1,2},{2,1},{3,4},{4,3},{5,6},{6,5},{7,8},{8,7},{9,10},{10,9... | collective-permute-start | bytes 98312 | tf_op jit(solution)/shard_map/ppermute | solution.py:344
  94.3 0.1 collective-permute-start.13
  94.4 5.3 %collective-permute-done.12.rf_ref = f32[8,8,128]{2,1,0:T(8,128)S(1)} collective-permute-done((f32[8,8,128]{2,1,0:T(8,128)S(1)}, f32[8,8,128]{2,1,0:T(8,128)S(1)}, u32[]{:S(2)}, u32[]{:S(2)}) %collective-permute-start.12) | collective-permute-done | bytes 32800 | tf_op jit(solution)/shard_map/ppermute | solution.py:344
  99.7 0.0 collective-permute-done.13.rn_ref
  99.7 1.8 %shard_map.91 = f32[32,16,128]{2,1,0:T(8,128)} custom-call(s32[4]{0:T(128)S(1)} %pad_add_fusion.place_ref, f32[8,8,128]{2,1,0:T(8,128)S(1)} %get-tuple-element.44.lf_ref, f32[8,8,128]{2,1,0:T(8,128)S(1)} %get-tuple-element.45.ln_ref, f32[8,8,128]{2,1,0:T(8,128)S(1)} %collective-permute-done.12.rf_ref, f32[8,8,128]{2,1,0:T(8,128)S(1)} %collective-permute-done.13.rn_ref, ...), custom_call_target="tpu_custom_call" | custom-call | flops 1000000 | bytes 1000000 | tf_op jit(solution)/shard_map/pallas_call | solution.py:25
  (13 shorter events, 0.1 us)
Async XLA Ops:
  0.0 0.7 copy-start.8
  0.8 1.0 copy-start.3
  2.7 18.9 %collective-permute-start = (f32[32,8,128]{2,1,0:T(8,128)S(1)}, f32[32,8,128]{2,1,0:T(8,128)S(1)}, u32[]{:S(2)}, u32[]{:S(2)}) collective-permute-start(f32[32,8,128]{2,1,0:T(8,128)S(1)} %get-tuple-element.26.w0_ref), channel_id=1, source_target_pairs={{0,0},{1,2},{2,1},{3,4},{4,3},{5,6},{6,5},{7,8},{8,7},{9,10},{10,9... | collective-permute-start | bytes 393224 | tf_op jit(solution)/shard_map/ppermute | solution.py:344
  9.4 14.2 %collective-permute-start.1 = (f32[32,8,128]{2,1,0:T(8,128)S(1)}, f32[32,8,128]{2,1,0:T(8,128)S(1)}, u32[]{:S(2)}, u32[]{:S(2)}) collective-permute-start(f32[32,8,128]{2,1,0:T(8,128)S(1)} %get-tuple-element.27.w1_ref), channel_id=1, source_target_pairs={{0,1},{1,0},{2,3},{3,2},{4,5},{5,4},{6,7},{7,6},{8,9},{9,8},{10,11... | collective-permute-start | bytes 393224 | tf_op jit(solution)/shard_map/ppermute | solution.py:348
  9.5 1.2 %copy-start.2 = (f32[32,4,2,1024]{3,2,1,0:T(2,128)S(1)}, f32[32,4,2,1024]{3,2,1,0:T(2,128)}, u32[]{:S(2)}) copy-start(f32[32,4,2,1024]{3,2,1,0:T(2,128)} %param.9) | copy-start | bytes 3145732
  11.4 53.5 %collective-permute-start.6 = (f32[64,8,128]{2,1,0:T(8,128)S(1)}, f32[64,8,128]{2,1,0:T(8,128)S(1)}, u32[]{:S(2)}, u32[]{:S(2)}) collective-permute-start(f32[64,8,128]{2,1,0:T(8,128)S(1)} %get-tuple-element.28.refs_0_.refs_2_), channel_id=1, source_target_pairs={{0,0},{1,2},{2,1},{3,4},{4,3},{5,6},{6,5},{7,8},{8,7},{9,10},{10,9... | collective-permute-start | bytes 786440 | tf_op jit(solution)/shard_map/ppermute | solution.py:344
  14.8 50.1 %collective-permute-start.7 = (f32[64,8,128]{2,1,0:T(8,128)S(1)}, f32[64,8,128]{2,1,0:T(8,128)S(1)}, u32[]{:S(2)}, u32[]{:S(2)}) collective-permute-start(f32[64,8,128]{2,1,0:T(8,128)S(1)} %get-tuple-element.29.refs_1_.refs_3_), channel_id=1, source_target_pairs={{0,0},{1,2},{2,1},{3,4},{4,3},{5,6},{6,5},{7,8},{8,7},{9,10},{10,9... | collective-permute-start | bytes 786440 | tf_op jit(solution)/shard_map/ppermute | solution.py:344
  21.5 43.5 %collective-permute-start.8 = (f32[64,8,128]{2,1,0:T(8,128)S(1)}, f32[64,8,128]{2,1,0:T(8,128)S(1)}, u32[]{:S(2)}, u32[]{:S(2)}) collective-permute-start(f32[64,8,128]{2,1,0:T(8,128)S(1)} %get-tuple-element.30.refs_2_.refs_4_), channel_id=1, source_target_pairs={{0,1},{1,0},{2,3},{3,2},{4,5},{5,4},{6,7},{7,6},{8,9},{9,8},{10,11... | collective-permute-start | bytes 786440 | tf_op jit(solution)/shard_map/ppermute | solution.py:348
  21.6 43.4 %collective-permute-start.9 = (f32[64,8,128]{2,1,0:T(8,128)S(1)}, f32[64,8,128]{2,1,0:T(8,128)S(1)}, u32[]{:S(2)}, u32[]{:S(2)}) collective-permute-start(f32[64,8,128]{2,1,0:T(8,128)S(1)} %get-tuple-element.31.refs_3_.refs_5_), channel_id=1, source_target_pairs={{0,1},{1,0},{2,3},{3,2},{4,5},{5,4},{6,7},{7,6},{8,9},{9,8},{10,11... | collective-permute-start | bytes 786440 | tf_op jit(solution)/shard_map/ppermute | solution.py:348
  23.6 22.1 %copy-start.4 = (s32[4,4,2048]{2,1,0:T(4,128)S(1)}, s32[4,4,2048]{2,1,0:T(4,128)}, u32[]{:S(2)}) copy-start(s32[4,4,2048]{2,1,0:T(4,128)} %param.11) | copy-start | bytes 393220
  23.6 22.1 %copy-start.5 = (f32[4,4,2048]{2,1,0:T(4,128)S(1)}, f32[4,4,2048]{2,1,0:T(4,128)}, u32[]{:S(2)}) copy-start(f32[4,4,2048]{2,1,0:T(4,128)} %param.12) | copy-start | bytes 393220
  23.6 22.1 %copy-start.6 = (s32[4,4,2048]{2,1,0:T(4,128)S(1)}, s32[4,4,2048]{2,1,0:T(4,128)}, u32[]{:S(2)}) copy-start(s32[4,4,2048]{2,1,0:T(4,128)} %param.13) | copy-start | bytes 393220
  23.6 22.1 %copy-start.7 = (f32[4,4,2048]{2,1,0:T(4,128)S(1)}, f32[4,4,2048]{2,1,0:T(4,128)}, u32[]{:S(2)}) copy-start(f32[4,4,2048]{2,1,0:T(4,128)} %param.14) | copy-start | bytes 393220
  23.6 25.8 %copy-start.1 = (bf16[256,1280]{1,0:T(8,128)(2,1)S(1)}, bf16[256,1280]{1,0:T(8,128)(2,1)}, u32[]{:S(2)}) copy-start(bf16[256,1280]{1,0:T(8,128)(2,1)} %constant.22.clone.refs_3_.refs_7_) | copy-start | bytes 1966084
  24.4 25.1 %copy-start = (bf16[1280,256]{1,0:T(8,128)(2,1)S(1)}, bf16[1280,256]{1,0:T(8,128)(2,1)}, u32[]{:S(2)}) copy-start(bf16[1280,256]{1,0:T(8,128)(2,1)} %constant.30.refs_4_.refs_8_) | copy-start | bytes 1966084
  35.9 9.9 %collective-permute-start.2 = (f32[4,8,128]{2,1,0:T(8,128)S(1)}, f32[4,8,128]{2,1,0:T(8,128)S(1)}, u32[]{:S(2)}, u32[]{:S(2)}) collective-permute-start(f32[4,8,128]{2,1,0:T(8,128)S(1)} %get-tuple-element.32.c0_ref), channel_id=1, source_target_pairs={{0,0},{1,2},{2,1},{3,4},{4,3},{5,6},{6,5},{7,8},{8,7},{9,10},{10,9... | collective-permute-start | bytes 49160 | tf_op jit(solution)/shard_map/ppermute | solution.py:344
  45.7 3.7 %collective-permute-start.3 = (f32[4,8,128]{2,1,0:T(8,128)S(1)}, f32[4,8,128]{2,1,0:T(8,128)S(1)}, u32[]{:S(2)}, u32[]{:S(2)}) collective-permute-start(f32[4,8,128]{2,1,0:T(8,128)S(1)} %get-tuple-element.33.c1_ref), channel_id=1, source_target_pairs={{0,1},{1,0},{2,3},{3,2},{4,5},{5,4},{6,7},{7,6},{8,9},{9,8},{10,11... | collective-permute-start | bytes 49160 | tf_op jit(solution)/shard_map/ppermute | solution.py:348
  51.0 10.0 %collective-permute-start.4 = (f32[8,8,128]{2,1,0:T(8,128)S(1)}, f32[8,8,128]{2,1,0:T(8,128)S(1)}, u32[]{:S(2)}, u32[]{:S(2)}) collective-permute-start(f32[8,8,128]{2,1,0:T(8,128)S(1)} %get-tuple-element.37.lf_ref), channel_id=1, source_target_pairs={{0,0},{1,2},{2,1},{3,4},{4,3},{5,6},{6,5},{7,8},{8,7},{9,10},{10,9... | collective-permute-start | bytes 98312 | tf_op jit(solution)/shard_map/ppermute | solution.py:344
  61.0 3.9 %collective-permute-start.5 = (f32[8,8,128]{2,1,0:T(8,128)S(1)}, f32[8,8,128]{2,1,0:T(8,128)S(1)}, u32[]{:S(2)}, u32[]{:S(2)}) collective-permute-start(f32[8,8,128]{2,1,0:T(8,128)S(1)} %get-tuple-element.38.ln_ref), channel_id=1, source_target_pairs={{0,1},{1,0},{2,3},{3,2},{4,5},{5,4},{6,7},{7,6},{8,9},{9,8},{10,11... | collective-permute-start | bytes 98312 | tf_op jit(solution)/shard_map/ppermute | solution.py:348
  78.1 10.0 %collective-permute-start.10 = (f32[8,8,128]{2,1,0:T(8,128)S(1)}, f32[8,8,128]{2,1,0:T(8,128)S(1)}, u32[]{:S(2)}, u32[]{:S(2)}) collective-permute-start(f32[8,8,128]{2,1,0:T(8,128)S(1)} %get-tuple-element.42.refs_0_), channel_id=1, source_target_pairs={{0,0},{1,2},{2,1},{3,4},{4,3},{5,6},{6,5},{7,8},{8,7},{9,10},{10,9... | collective-permute-start | bytes 98312 | tf_op jit(solution)/shard_map/ppermute | solution.py:344
  82.7 5.4 %collective-permute-start.11 = (f32[8,8,128]{2,1,0:T(8,128)S(1)}, f32[8,8,128]{2,1,0:T(8,128)S(1)}, u32[]{:S(2)}, u32[]{:S(2)}) collective-permute-start(f32[8,8,128]{2,1,0:T(8,128)S(1)} %get-tuple-element.43.refs_1_), channel_id=1, source_target_pairs={{0,1},{1,0},{2,3},{3,2},{4,5},{5,4},{6,7},{7,6},{8,9},{9,8},{10,11... | collective-permute-start | bytes 98312 | tf_op jit(solution)/shard_map/ppermute | solution.py:348
  89.7 10.0 %collective-permute-start.12 = (f32[8,8,128]{2,1,0:T(8,128)S(1)}, f32[8,8,128]{2,1,0:T(8,128)S(1)}, u32[]{:S(2)}, u32[]{:S(2)}) collective-permute-start(f32[8,8,128]{2,1,0:T(8,128)S(1)} %get-tuple-element.44.lf_ref), channel_id=1, source_target_pairs={{0,0},{1,2},{2,1},{3,4},{4,3},{5,6},{6,5},{7,8},{8,7},{9,10},{10,9... | collective-permute-start | bytes 98312 | tf_op jit(solution)/shard_map/ppermute | solution.py:344
  94.3 5.4 %collective-permute-start.13 = (f32[8,8,128]{2,1,0:T(8,128)S(1)}, f32[8,8,128]{2,1,0:T(8,128)S(1)}, u32[]{:S(2)}, u32[]{:S(2)}) collective-permute-start(f32[8,8,128]{2,1,0:T(8,128)S(1)} %get-tuple-element.45.ln_ref), channel_id=1, source_target_pairs={{0,1},{1,0},{2,3},{3,2},{4,5},{5,4},{6,7},{7,6},{8,9},{9,8},{10,11... | collective-permute-start | bytes 98312 | tf_op jit(solution)/shard_map/ppermute | solution.py:348

commit v5 on v4

--- a/solution.py
+++ b/solution.py
@@ -18,18 +18,20 @@
     return jax.ShapeDtypeStruct(dims, F32)
 
 
-def call(kernel, outs, args, scalars=(), scratch=(), flops=1_000_000):
+def call(kernel, outs, args, scalars=(), scratch=(), far_args=()):
     in_specs = [pl.BlockSpec(memory_space=pltpu.SMEM)] * len(scalars)
+    in_specs += [pl.BlockSpec(memory_space=pltpu.HBM)] * len(far_args)
     in_specs += [pl.BlockSpec(memory_space=pltpu.VMEM)] * len(args)
-    args = tuple(scalars) + tuple(args)
+    far_args = tuple(pltpu.with_memory_space_constraint(x, pltpu.HBM) for x in far_args)
+    args = tuple(scalars) + far_args + tuple(args)
     return pl.pallas_call(
         kernel,
         out_shape=outs,
         in_specs=in_specs,
         out_specs=jax.tree.map(lambda _: pl.BlockSpec(memory_space=pltpu.VMEM), outs),
-        scratch_shapes=[pltpu.VMEM(dims, F32) for dims in scratch],
+        scratch_shapes=list(scratch),
         compiler_params=pltpu.CompilerParams(vmem_limit_bytes=LIMIT),
-        cost_estimate=pl.CostEstimate(flops=flops, transcendentals=0, bytes_accessed=1_000_000),
+        cost_estimate=pl.CostEstimate(flops=1_000_000, transcendentals=0, bytes_accessed=1_000_000),
     )(*args)
 
 
@@ -81,32 +83,51 @@
     return jnp.where(jnp.full((8, 128), place_ref[0], jnp.int32) > 0, odd, even)
 
 
-def filter_kernel(place_ref, v_ref, w0_ref, w1_ref, old_ref, band_ref):
+def filter_kernel(
+    place_ref, widths_hbm, v_hbm, w0_ref, w1_ref, old_ref, band_ref, widths_ref, v_ref, sems
+):
+    fetch = [pltpu.make_async_copy(widths_hbm, widths_ref, sems.at[0])]
+    for b in range(2):
+        at = pl.ds(b * 16, 16)
+        fetch.append(pltpu.make_async_copy(v_hbm.at[at], v_ref.at[at], sems.at[1 + b]))
+    for copy in fetch:
+        copy.start()
     away = jnp.abs(position(iota((256, 128), 0)) - iota((256, 128), 1))
-    for r, out in ((0, w0_ref), (1, w1_ref)):
-        width = place_ref[2 + r]
+    fetch[0].wait()
+    scales = []
+    for r in range(2):
+        width = widths_ref[r + place_ref[0] * (1 - 2 * r)]
         inside = away <= jnp.full((256, 128), width, jnp.int32)
-        band = jnp.where(inside, 1.0, 0.0).astype(jnp.bfloat16)
-        band_ref[r] = band
-        for b in range(2):
-            at = pl.ds(b * 16, 16)
-            top, bottom = (v_ref[at, pl.ds(n, 8, stride=2), :] for n in range(2))
+        band_ref[r] = jnp.where(inside, 1.0, 0.0).astype(jnp.bfloat16)
+        scales.append(scale_of(width))
+    for b in range(2):
+        at = pl.ds(b * 16, 16)
+        fetch[1 + b].wait()
+        top, bottom = (v_ref[at, pl.ds(n, 8, stride=2), :] for n in range(2))
+        for r, out in ((0, w0_ref), (1, w1_ref)):
             x = if_odd(place_ref, top, bottom) if r else if_odd(place_ref, bottom, top)
             old_ref[r, at] = x
-            out[at] = filtered(x, band, scale_of(width))
-
-
-def split_kernel(place_ref, e_ref, *out_refs):
-    for half in range(2):
-
-        def body(b, carry, half=half):
-            at = pl.ds(half * 64 + b * 8, 8)
+            out[at] = filtered(x, band_ref[r], scales[r])
+
+
+def split_kernel(place_ref, e_hbm, far_ref, far_late_ref, near_ref, e_ref, sems):
+    fetch = []
+    for part in range(4):
+        at = pl.ds(part * 32, 32)
+        fetch.append(pltpu.make_async_copy(e_hbm.at[at], e_ref.at[at], sems.at[part]))
+        fetch[-1].start()
+    for part in range(4):
+        fetch[part].wait()
+        out = (far_ref, far_late_ref)[part // 2]
+
+        def body(b, carry, part=part, out=out):
+            at = pl.ds(part * 32 + b * 8, 8)
             top, bottom = (e_ref[at, pl.ds(n, 8, stride=2), :] for n in range(2))
-            out_refs[half][pl.ds(b * 8, 8)] = if_odd(place_ref, bottom, top)
-            out_refs[2 + half][pl.ds(b * 8, 8)] = if_odd(place_ref, top, bottom)
+            out[pl.ds(part % 2 * 32 + b * 8, 8)] = if_odd(place_ref, bottom, top)
+            near_ref[at] = if_odd(place_ref, top, bottom)
             return carry
 
-        lax.fori_loop(0, 8, body, 0)
+        lax.fori_loop(0, 4, body, 0)
 
 
 def planes_kernel(place_ref, src_ref, wgt_ref, msk_ref, inn_ref, planes_ref, mask_ref, target_ref):
@@ -139,6 +160,12 @@
             target_ref[t, j] = row(inn_ref, t)
 
 
+def members(e_refs, q, half):
+    if q < 2:
+        return e_refs[q * 2 + half], 0
+    return e_refs[q + 2], half * 64
+
+
 def first_kernel(place_ref, w0_ref, w1_ref, far_ref, near_ref, *refs):
     *e_refs, part_ref = refs
     sums = (jnp.zeros((8, 128), F32),) * 8
@@ -152,7 +179,7 @@
             sums = list(sums)
             for t in range(4):
                 sums[t] = sums[t] + e_refs[half][n * 4 + t] * f0
-                sums[4 + t] = sums[4 + t] + e_refs[2 + half][n * 4 + t] * f1
+                sums[4 + t] = sums[4 + t] + e_refs[2][half * 64 + n * 4 + t] * f1
             return tuple(sums)
 
         sums = lax.fori_loop(0, 16, body, sums, unroll=4)
@@ -269,7 +296,8 @@
         def body(b, carry, half=half):
             back = []
             for q in range(4):
-                x = e_refs[q * 2 + half][pl.ds(b * 16, 16)].reshape(4, 4, 8, 128)
+                ref, first = members(e_refs, q, half)
+                x = ref[pl.ds(first + b * 16, 16)].reshape(4, 4, 8, 128)
                 total = x[:, 0] * rows[q][0]
                 for t in range(1, 4):
                     total = total + x[:, t] * rows[q][t]
@@ -310,8 +338,9 @@
                     C_SIDE * w[1],
                 ]
                 for q in range(4):
+                    ref, first = members(e_refs, q, half)
                     for t in range(4):
-                        x = e_refs[q * 2 + half][n * 4 + t]
+                        x = ref[first + n * 4 + t]
                         sums[q * 4 + t] = sums[q * 4 + t] + x * forward[q]
             return tuple(sums)
 
@@ -368,15 +397,28 @@
     scalars = (place,)
     row, rows = shape(32, 8, 128), shape(2, 32, 8, 128)
     band = jax.ShapeDtypeStruct((2, 256, 128), jnp.bfloat16)
-    w0, w1, old, band = call(filter_kernel, (row, row, rows, band), (v,), scalars)
+    w0, w1, old, band = call(
+        filter_kernel,
+        (row, row, rows, band),
+        (),
+        (ends,),
+        (
+            pltpu.SMEM((2,), jnp.int32),
+            pltpu.VMEM((32, 16, 128), F32),
+            pltpu.SemaphoreType.DMA((3,)),
+        ),
+        (widths, v),
+    )
     far, near = swapped(w0, w1)
-    e0, e0_late, e1, e1_late = call(split_kernel, (shape(64, 8, 128),) * 4, (e,), scalars)
-    ensembles = (
-        *(from_far(e0), from_far(e0_late)),
-        *(e0, e0_late, e1, e1_late),
-        *(from_near(e1), from_near(e1_late)),
-        band,
-    )
+    e0, e0_late, e1 = call(
+        split_kernel,
+        (shape(64, 8, 128), shape(64, 8, 128), shape(128, 8, 128)),
+        (),
+        scalars,
+        (pltpu.VMEM((128, 16, 128), F32), pltpu.SemaphoreType.DMA((4,))),
+        (e,),
+    )
+    ensembles = (*(from_far(e0), from_far(e0_late)), *(e0, e0_late, e1, from_near(e1)), band)
     fields = call(
         planes_kernel,
         (shape(15, 8, 8, 128), shape(4, 8, 8, 128), shape(4, 8, 8, 128)),
@@ -386,16 +428,16 @@
     refine = refining_matrix()
     fields = tuple(fields) + (refine, refine.T)
     part = call(
-        first_kernel, shape(8, 8, 128), (w0, w1, far, near, e0, e0_late, e1, e1_late), scalars
+        first_kernel, shape(8, 8, 128), (w0, w1, far, near, e0, e0_late, e1), scalars
     )
     four, eight = shape(4, 8, 128), shape(8, 8, 128)
     c0, c1 = call(sum_kernel, (four, four), (lax.all_gather(part, "mem"),))
     far, near = swapped(c0, c1)
-    refined = ((128, 1280),)
+    refined = (pltpu.VMEM((128, 1280), F32),)
     sent = call(
         first_observe_kernel, (eight, eight), (far, c0, c1, near) + fields, scratch=refined
     )
-    smoothed = ((2, 32, 8, 128),)
+    smoothed = (pltpu.VMEM((2, 32, 8, 128), F32),)
     new, part = call(
         middle_kernel,
         (rows, shape(16, 8, 128)),

time: 102 us -> 97.1 us (0.952)
  the two profiles are of different devices: /device:TPU:32 before, /device:TPU:30 now
where the time goes in v5:
time: 97.1 us; the launch traced here: 95.4 us
  starting transfers between devices  33 us (34%)
  waiting for transfers between devices  27.9 us (29%)
  blocking collectives  21.1 us (22%)
  Pallas kernels  12.2 us (13%)
    ppermute x7, starting transfers between devices, from_far(): return lax.ppermute(x, 'lat', pairs)  31.7 us
    ppermute x7, waiting for transfers between devices, from_far(): return lax.ppermute(x, 'lat', pairs)  27.9 us
    pallas_call x10, Pallas kernels, call(): pl.pallas_call(kernel, out_shape=outs, in_specs=in_specs, out_specs=jax.t...  12.2 us
    all_gather x1, blocking collectives, descent(): c0, c1 = call(sum_kernel, (four, four), (lax.all_gather(part, 'mem'),))  11 us
    all_gather x1, blocking collectives, descent(): sent = call(sum_kernel, (eight, eight), (lax.all_gather(part, 'mem'),))  10.1 us
  transfers between devices with their start and end apart: 13, of which 5 were waited for; matrix products, arithmetic and copies ran while one was open for 0% of the time, Pallas kernels for 5%

profile of v5, /device:TPU:30, one launch (start us, length us, event | category | flops | bytes accessed | tf_op | source)
XLA Modules:
  0.0 95.4 jit_solution(16402132911860623039)
XLA Ops:
  0.0 0.7 copy-done.6
  0.7 0.1 rev.3
  0.8 0.1 pad_add_fusion.place_ref
  0.8 1.8 %shard_map.83 = (f32[64,8,128]{2,1,0:T(8,128)S(1)}, f32[64,8,128]{2,1,0:T(8,128)S(1)}, f32[128,8,128]{2,1,0:T(8,128)S(1)}) custom-call(s32[4]{0:T(128)S(1)} %pad_add_fusion.place_ref, f32[128,16,128]{2,1,0:T(8,128)} %bitcast.45), custom_call_target="tpu_custom_call" | custom-call | flops 1000000 | bytes 1000000 | tf_op jit(solution)/shard_map/pallas_call | solution.py:27
  2.6 0.8 collective-permute-start.8
  3.5 4.2 %collective-permute-start.6 = (f32[64,8,128]{2,1,0:T(8,128)S(1)}, f32[64,8,128]{2,1,0:T(8,128)S(1)}, u32[]{:S(2)}, u32[]{:S(2)}) collective-permute-start(f32[64,8,128]{2,1,0:T(8,128)S(1)} %get-tuple-element.27.refs_0_.refs_2_), channel_id=1, source_target_pairs={{0,0},{1,2},{2,1},{3,4},{4,3},{5,6},{6,5},{7,8},{8,7},{9,10},{10,9... | collective-permute-start | bytes 786440 | tf_op jit(solution)/shard_map/ppermute | solution.py:373
  7.7 5.8 %collective-permute-start.7 = (f32[64,8,128]{2,1,0:T(8,128)S(1)}, f32[64,8,128]{2,1,0:T(8,128)S(1)}, u32[]{:S(2)}, u32[]{:S(2)}) collective-permute-start(f32[64,8,128]{2,1,0:T(8,128)S(1)} %get-tuple-element.28.refs_1_.refs_3_), channel_id=1, source_target_pairs={{0,0},{1,2},{2,1},{3,4},{4,3},{5,6},{6,5},{7,8},{8,7},{9,10},{10,9... | collective-permute-start | bytes 786440 | tf_op jit(solution)/shard_map/ppermute | solution.py:373
  13.5 0.1 pad_add_fusion.1.place_ref
  13.6 2.0 %shard_map.82 = (f32[32,8,128]{2,1,0:T(8,128)S(1)}, f32[32,8,128]{2,1,0:T(8,128)S(1)}, f32[2,32,8,128]{3,2,1,0:T(8,128)S(1)}, bf16[2,256,128]{2,1,0:T(8,128)(2,1)S(1)}) custom-call(s32[2]{0:T(128)S(1)} %pad_add_fusion.1.place_ref, s32[2]{0:T(128)} %widths_hbm.1, f32[32,16,128]{2,1,0:T(8,128)} %bitcast.46), custom_call_target="tpu_custom_call" | custom-call | flops 1000000 | bytes 1000000 | tf_op jit(solution)/shard_map/pallas_call | solution.py:27
  15.6 4.2 %collective-permute-start = (f32[32,8,128]{2,1,0:T(8,128)S(1)}, f32[32,8,128]{2,1,0:T(8,128)S(1)}, u32[]{:S(2)}, u32[]{:S(2)}) collective-permute-start(f32[32,8,128]{2,1,0:T(8,128)S(1)} %get-tuple-element.25.w0_ref), channel_id=1, source_target_pairs={{0,0},{1,2},{2,1},{3,4},{4,3},{5,6},{6,5},{7,8},{8,7},{9,10},{10,9... | collective-permute-start | bytes 393224 | tf_op jit(solution)/shard_map/ppermute | solution.py:373
  19.9 0.1 collective-permute-start.1
  20.0 6.7 %collective-permute-done.far_ref = f32[32,8,128]{2,1,0:T(8,128)S(1)} collective-permute-done((f32[32,8,128]{2,1,0:T(8,128)S(1)}, f32[32,8,128]{2,1,0:T(8,128)S(1)}, u32[]{:S(2)}, u32[]{:S(2)}) %collective-permute-start) | collective-permute-done | bytes 131104 | tf_op jit(solution)/shard_map/ppermute | solution.py:373
  26.7 0.0 collective-permute-done.1.near_ref
  26.7 0.0 copy-start.5
  26.7 0.0 copy-start.1
  26.7 0.7 shard_map.84
  27.4 0.0 copy-start
  27.4 11.0 %all-gather = f32[32,8,128]{2,1,0:T(8,128)S(1)} all-gather(f32[8,8,128]{2,1,0:T(8,128)S(1)} %shard_map.84), channel_id=2, replica_groups=mesh['mem'=4,'lat'=64] {'mem'}, dimensions={0}, use_global_device_ids=true | all-gather | bytes 163840 | tf_op jit(solution)/shard_map/all_gather | solution.py:434
  38.4 3.9 %collective-permute-start.2 = (f32[4,8,128]{2,1,0:T(8,128)S(1)}, f32[4,8,128]{2,1,0:T(8,128)S(1)}, u32[]{:S(2)}, u32[]{:S(2)}) collective-permute-start(f32[4,8,128]{2,1,0:T(8,128)S(1)} %get-tuple-element.30.c0_ref), channel_id=1, source_target_pairs={{0,0},{1,2},{2,1},{3,4},{4,3},{5,6},{6,5},{7,8},{8,7},{9,10},{10,9... | collective-permute-start | bytes 49160 | tf_op jit(solution)/shard_map/ppermute | solution.py:373
  42.4 0.1 collective-permute-start.3
  42.5 0.0 copy-done.2
  42.5 0.0 copy-done.3
  42.5 0.0 copy-done.4
  42.5 0.0 copy-done.5
  42.5 0.8 shard_map.86
  43.4 4.9 %collective-permute-done.2.far_ref = f32[4,8,128]{2,1,0:T(8,128)S(1)} collective-permute-done((f32[4,8,128]{2,1,0:T(8,128)S(1)}, f32[4,8,128]{2,1,0:T(8,128)S(1)}, u32[]{:S(2)}, u32[]{:S(2)}) %collective-permute-start.2) | collective-permute-done | bytes 16416 | tf_op jit(solution)/shard_map/ppermute | solution.py:373
  48.3 0.0 collective-permute-done.3.near_ref
  48.3 0.0 copy-done.1
  48.3 1.5 %shard_map.87 = (f32[8,8,128]{2,1,0:T(8,128)S(1)}, f32[8,8,128]{2,1,0:T(8,128)S(1)}) custom-call(f32[4,8,128]{2,1,0:T(8,128)S(1)} %collective-permute-done.2.far_ref, f32[4,8,128]{2,1,0:T(8,128)S(1)} %get-tuple-element.30.c0_ref, f32[4,8,128]{2,1,0:T(8,128)S(1)} %get-tuple-element.31.c1_ref, f32[4,8,128]{2,1,0:T(8,128)S(1)} %collective-permute-done.3.near_ref, ...), custom_call_target="tpu_custom_call" | custom-call | flops 1000000 | bytes 1000000 | tf_op jit(solution)/shard_map/pallas_call | solution.py:27
  49.8 4.0 %collective-permute-start.4 = (f32[8,8,128]{2,1,0:T(8,128)S(1)}, f32[8,8,128]{2,1,0:T(8,128)S(1)}, u32[]{:S(2)}, u32[]{:S(2)}) collective-permute-start(f32[8,8,128]{2,1,0:T(8,128)S(1)} %get-tuple-element.35.lf_ref), channel_id=1, source_target_pairs={{0,0},{1,2},{2,1},{3,4},{4,3},{5,6},{6,5},{7,8},{8,7},{9,10},{10,9... | collective-permute-start | bytes 98312 | tf_op jit(solution)/shard_map/ppermute | solution.py:373
  53.9 0.1 collective-permute-start.5
  54.0 5.9 %collective-permute-done.4.rf_ref = f32[8,8,128]{2,1,0:T(8,128)S(1)} collective-permute-done((f32[8,8,128]{2,1,0:T(8,128)S(1)}, f32[8,8,128]{2,1,0:T(8,128)S(1)}, u32[]{:S(2)}, u32[]{:S(2)}) %collective-permute-start.4) | collective-permute-done | bytes 32800 | tf_op jit(solution)/shard_map/ppermute | solution.py:373
  59.8 0.0 collective-permute-done.5.rn_ref
  59.8 0.0 collective-permute-done.6.refs_0_
  59.8 0.0 collective-permute-done.7.refs_1_
  59.9 0.0 collective-permute-done.8.refs_5_
  59.9 2.0 %shard_map.88 = (f32[2,32,8,128]{3,2,1,0:T(8,128)S(1)}, f32[16,8,128]{2,1,0:T(8,128)S(1)}) custom-call(s32[4]{0:T(128)S(1)} %pad_add_fusion.place_ref, f32[8,8,128]{2,1,0:T(8,128)S(1)} %get-tuple-element.35.lf_ref, f32[8,8,128]{2,1,0:T(8,128)S(1)} %get-tuple-element.36.ln_ref, f32[8,8,128]{2,1,0:T(8,128)S(1)} %collective-permute-done.4.rf_ref, ...), custom_call_target="tpu_custom_call" | custom-call | flops 1000000 | bytes 1000000 | tf_op jit(solution)/shard_map/pallas_call | solution.py:27
  61.9 10.1 %all-gather.1 = f32[64,8,128]{2,1,0:T(8,128)S(1)} all-gather(f32[16,8,128]{2,1,0:T(8,128)S(1)} %get-tuple-element.39), channel_id=3, replica_groups=mesh['mem'=4,'lat'=64] {'mem'}, dimensions={0}, use_global_device_ids=true | all-gather | bytes 327680 | tf_op jit(solution)/shard_map/all_gather | solution.py:448
  72.0 4.7 %collective-permute-start.9 = (f32[8,8,128]{2,1,0:T(8,128)S(1)}, f32[8,8,128]{2,1,0:T(8,128)S(1)}, u32[]{:S(2)}, u32[]{:S(2)}) collective-permute-start(f32[8,8,128]{2,1,0:T(8,128)S(1)} %get-tuple-element.40.refs_0_), channel_id=1, source_target_pairs={{0,0},{1,2},{2,1},{3,4},{4,3},{5,6},{6,5},{7,8},{8,7},{9,10},{10,9... | collective-permute-start | bytes 98312 | tf_op jit(solution)/shard_map/ppermute | solution.py:373
  76.8 0.1 collective-permute-start.10
  76.9 5.2 %collective-permute-done.9.refs_2_ = f32[8,8,128]{2,1,0:T(8,128)S(1)} collective-permute-done((f32[8,8,128]{2,1,0:T(8,128)S(1)}, f32[8,8,128]{2,1,0:T(8,128)S(1)}, u32[]{:S(2)}, u32[]{:S(2)}) %collective-permute-start.9) | collective-permute-done | bytes 32800 | tf_op jit(solution)/shard_map/ppermute | solution.py:373
  82.1 0.0 collective-permute-done.10.refs_3_
  82.1 1.5 %shard_map.90 = (f32[8,8,128]{2,1,0:T(8,128)S(1)}, f32[8,8,128]{2,1,0:T(8,128)S(1)}) custom-call(f32[8,8,128]{2,1,0:T(8,128)S(1)} %get-tuple-element.40.refs_0_, f32[8,8,128]{2,1,0:T(8,128)S(1)} %get-tuple-element.41.refs_1_, f32[8,8,128]{2,1,0:T(8,128)S(1)} %collective-permute-done.9.refs_2_, f32[8,8,128]{2,1,0:T(8,128)S(1)} %collective-permute-done.10.refs_3_, ...), custom_call_target="tpu_custom_call" | custom-call | flops 1000000 | bytes 1000000 | tf_op jit(solution)/shard_map/pallas_call | solution.py:27
  83.6 4.7 %collective-permute-start.11 = (f32[8,8,128]{2,1,0:T(8,128)S(1)}, f32[8,8,128]{2,1,0:T(8,128)S(1)}, u32[]{:S(2)}, u32[]{:S(2)}) collective-permute-start(f32[8,8,128]{2,1,0:T(8,128)S(1)} %get-tuple-element.42.lf_ref), channel_id=1, source_target_pairs={{0,0},{1,2},{2,1},{3,4},{4,3},{5,6},{6,5},{7,8},{8,7},{9,10},{10,9... | collective-permute-start | bytes 98312 | tf_op jit(solution)/shard_map/ppermute | solution.py:373
  88.4 0.1 collective-permute-start.12
  88.5 5.2 %collective-permute-done.11.rf_ref = f32[8,8,128]{2,1,0:T(8,128)S(1)} collective-permute-done((f32[8,8,128]{2,1,0:T(8,128)S(1)}, f32[8,8,128]{2,1,0:T(8,128)S(1)}, u32[]{:S(2)}, u32[]{:S(2)}) %collective-permute-start.11) | collective-permute-done | bytes 32800 | tf_op jit(solution)/shard_map/ppermute | solution.py:373
  93.6 0.0 collective-permute-done.12.rn_ref
  93.6 1.8 %shard_map.91 = f32[32,16,128]{2,1,0:T(8,128)} custom-call(s32[4]{0:T(128)S(1)} %pad_add_fusion.place_ref, f32[8,8,128]{2,1,0:T(8,128)S(1)} %get-tuple-element.42.lf_ref, f32[8,8,128]{2,1,0:T(8,128)S(1)} %get-tuple-element.43.ln_ref, f32[8,8,128]{2,1,0:T(8,128)S(1)} %collective-permute-done.11.rf_ref, f32[8,8,128]{2,1,0:T(8,128)S(1)} %collective-permute-done.12.rn_ref, ...), custom_call_target="tpu_custom_call" | custom-call | flops 1000000 | bytes 1000000 | tf_op jit(solution)/shard_map/pallas_call | solution.py:27
  (8 shorter events, 0.0 us)
Async XLA Ops:
  0.0 0.7 copy-start.6
  2.6 57.2 %collective-permute-start.8 = (f32[128,8,128]{2,1,0:T(8,128)S(1)}, f32[128,8,128]{2,1,0:T(8,128)S(1)}, u32[]{:S(2)}, u32[]{:S(2)}) collective-permute-start(f32[128,8,128]{2,1,0:T(8,128)S(1)} %get-tuple-element.29.refs_2_.refs_4_), channel_id=1, source_target_pairs={{0,1},{1,0},{2,3},{3,2},{4,5},{5,4},{6,7},{7,6},{8,9},{9,8},{10,11... | collective-permute-start | bytes 1572872 | tf_op jit(solution)/shard_map/ppermute | solution.py:377
  3.5 56.4 %collective-permute-start.6 = (f32[64,8,128]{2,1,0:T(8,128)S(1)}, f32[64,8,128]{2,1,0:T(8,128)S(1)}, u32[]{:S(2)}, u32[]{:S(2)}) collective-permute-start(f32[64,8,128]{2,1,0:T(8,128)S(1)} %get-tuple-element.27.refs_0_.refs_2_), channel_id=1, source_target_pairs={{0,0},{1,2},{2,1},{3,4},{4,3},{5,6},{6,5},{7,8},{8,7},{9,10},{10,9... | collective-permute-start | bytes 786440 | tf_op jit(solution)/shard_map/ppermute | solution.py:373
  7.7 52.2 %collective-permute-start.7 = (f32[64,8,128]{2,1,0:T(8,128)S(1)}, f32[64,8,128]{2,1,0:T(8,128)S(1)}, u32[]{:S(2)}, u32[]{:S(2)}) collective-permute-start(f32[64,8,128]{2,1,0:T(8,128)S(1)} %get-tuple-element.28.refs_1_.refs_3_), channel_id=1, source_target_pairs={{0,0},{1,2},{2,1},{3,4},{4,3},{5,6},{6,5},{7,8},{8,7},{9,10},{10,9... | collective-permute-start | bytes 786440 | tf_op jit(solution)/shard_map/ppermute | solution.py:373
  15.6 11.1 %collective-permute-start = (f32[32,8,128]{2,1,0:T(8,128)S(1)}, f32[32,8,128]{2,1,0:T(8,128)S(1)}, u32[]{:S(2)}, u32[]{:S(2)}) collective-permute-start(f32[32,8,128]{2,1,0:T(8,128)S(1)} %get-tuple-element.25.w0_ref), channel_id=1, source_target_pairs={{0,0},{1,2},{2,1},{3,4},{4,3},{5,6},{6,5},{7,8},{8,7},{9,10},{10,9... | collective-permute-start | bytes 393224 | tf_op jit(solution)/shard_map/ppermute | solution.py:373
  19.9 6.8 %collective-permute-start.1 = (f32[32,8,128]{2,1,0:T(8,128)S(1)}, f32[32,8,128]{2,1,0:T(8,128)S(1)}, u32[]{:S(2)}, u32[]{:S(2)}) collective-permute-start(f32[32,8,128]{2,1,0:T(8,128)S(1)} %get-tuple-element.26.w1_ref), channel_id=1, source_target_pairs={{0,1},{1,0},{2,3},{3,2},{4,5},{5,4},{6,7},{7,6},{8,9},{9,8},{10,11... | collective-permute-start | bytes 393224 | tf_op jit(solution)/shard_map/ppermute | solution.py:377
  26.7 15.8 %copy-start.2 = (s32[4,4,2048]{2,1,0:T(4,128)S(1)}, s32[4,4,2048]{2,1,0:T(4,128)}, u32[]{:S(2)}) copy-start(s32[4,4,2048]{2,1,0:T(4,128)} %param.11) | copy-start | bytes 393220
  26.7 15.8 %copy-start.3 = (f32[4,4,2048]{2,1,0:T(4,128)S(1)}, f32[4,4,2048]{2,1,0:T(4,128)}, u32[]{:S(2)}) copy-start(f32[4,4,2048]{2,1,0:T(4,128)} %param.12) | copy-start | bytes 393220
  26.7 15.8 %copy-start.4 = (s32[4,4,2048]{2,1,0:T(4,128)S(1)}, s32[4,4,2048]{2,1,0:T(4,128)}, u32[]{:S(2)}) copy-start(s32[4,4,2048]{2,1,0:T(4,128)} %param.13) | copy-start | bytes 393220
  26.7 15.8 %copy-start.5 = (f32[4,4,2048]{2,1,0:T(4,128)S(1)}, f32[4,4,2048]{2,1,0:T(4,128)}, u32[]{:S(2)}) copy-start(f32[4,4,2048]{2,1,0:T(4,128)} %param.14) | copy-start | bytes 393220
  26.7 21.6 %copy-start.1 = (bf16[256,1280]{1,0:T(8,128)(2,1)S(1)}, bf16[256,1280]{1,0:T(8,128)(2,1)}, u32[]{:S(2)}) copy-start(bf16[256,1280]{1,0:T(8,128)(2,1)} %constant.22.clone.refs_3_.refs_7_) | copy-start | bytes 1966084
  27.4 20.9 %copy-start = (bf16[1280,256]{1,0:T(8,128)(2,1)S(1)}, bf16[1280,256]{1,0:T(8,128)(2,1)}, u32[]{:S(2)}) copy-start(bf16[1280,256]{1,0:T(8,128)(2,1)} %constant.30.refs_4_.refs_8_) | copy-start | bytes 1966084
  38.4 9.9 %collective-permute-start.2 = (f32[4,8,128]{2,1,0:T(8,128)S(1)}, f32[4,8,128]{2,1,0:T(8,128)S(1)}, u32[]{:S(2)}, u32[]{:S(2)}) collective-permute-start(f32[4,8,128]{2,1,0:T(8,128)S(1)} %get-tuple-element.30.c0_ref), channel_id=1, source_target_pairs={{0,0},{1,2},{2,1},{3,4},{4,3},{5,6},{6,5},{7,8},{8,7},{9,10},{10,9... | collective-permute-start | bytes 49160 | tf_op jit(solution)/shard_map/ppermute | solution.py:373
  42.4 5.9 %collective-permute-start.3 = (f32[4,8,128]{2,1,0:T(8,128)S(1)}, f32[4,8,128]{2,1,0:T(8,128)S(1)}, u32[]{:S(2)}, u32[]{:S(2)}) collective-permute-start(f32[4,8,128]{2,1,0:T(8,128)S(1)} %get-tuple-element.31.c1_ref), channel_id=1, source_target_pairs={{0,1},{1,0},{2,3},{3,2},{4,5},{5,4},{6,7},{7,6},{8,9},{9,8},{10,11... | collective-permute-start | bytes 49160 | tf_op jit(solution)/shard_map/ppermute | solution.py:377
  49.8 10.0 %collective-permute-start.4 = (f32[8,8,128]{2,1,0:T(8,128)S(1)}, f32[8,8,128]{2,1,0:T(8,128)S(1)}, u32[]{:S(2)}, u32[]{:S(2)}) collective-permute-start(f32[8,8,128]{2,1,0:T(8,128)S(1)} %get-tuple-element.35.lf_ref), channel_id=1, source_target_pairs={{0,0},{1,2},{2,1},{3,4},{4,3},{5,6},{6,5},{7,8},{8,7},{9,10},{10,9... | collective-permute-start | bytes 98312 | tf_op jit(solution)/shard_map/ppermute | solution.py:373
  53.9 6.0 %collective-permute-start.5 = (f32[8,8,128]{2,1,0:T(8,128)S(1)}, f32[8,8,128]{2,1,0:T(8,128)S(1)}, u32[]{:S(2)}, u32[]{:S(2)}) collective-permute-start(f32[8,8,128]{2,1,0:T(8,128)S(1)} %get-tuple-element.36.ln_ref), channel_id=1, source_target_pairs={{0,1},{1,0},{2,3},{3,2},{4,5},{5,4},{6,7},{7,6},{8,9},{9,8},{10,11... | collective-permute-start | bytes 98312 | tf_op jit(solution)/shard_map/ppermute | solution.py:377
  72.0 10.0 %collective-permute-start.9 = (f32[8,8,128]{2,1,0:T(8,128)S(1)}, f32[8,8,128]{2,1,0:T(8,128)S(1)}, u32[]{:S(2)}, u32[]{:S(2)}) collective-permute-start(f32[8,8,128]{2,1,0:T(8,128)S(1)} %get-tuple-element.40.refs_0_), channel_id=1, source_target_pairs={{0,0},{1,2},{2,1},{3,4},{4,3},{5,6},{6,5},{7,8},{8,7},{9,10},{10,9... | collective-permute-start | bytes 98312 | tf_op jit(solution)/shard_map/ppermute | solution.py:373
  76.8 5.3 %collective-permute-start.10 = (f32[8,8,128]{2,1,0:T(8,128)S(1)}, f32[8,8,128]{2,1,0:T(8,128)S(1)}, u32[]{:S(2)}, u32[]{:S(2)}) collective-permute-start(f32[8,8,128]{2,1,0:T(8,128)S(1)} %get-tuple-element.41.refs_1_), channel_id=1, source_target_pairs={{0,1},{1,0},{2,3},{3,2},{4,5},{5,4},{6,7},{7,6},{8,9},{9,8},{10,11... | collective-permute-start | bytes 98312 | tf_op jit(solution)/shard_map/ppermute | solution.py:377
  83.6 10.0 %collective-permute-start.11 = (f32[8,8,128]{2,1,0:T(8,128)S(1)}, f32[8,8,128]{2,1,0:T(8,128)S(1)}, u32[]{:S(2)}, u32[]{:S(2)}) collective-permute-start(f32[8,8,128]{2,1,0:T(8,128)S(1)} %get-tuple-element.42.lf_ref), channel_id=1, source_target_pairs={{0,0},{1,2},{2,1},{3,4},{4,3},{5,6},{6,5},{7,8},{8,7},{9,10},{10,9... | collective-permute-start | bytes 98312 | tf_op jit(solution)/shard_map/ppermute | solution.py:373
  88.4 5.3 %collective-permute-start.12 = (f32[8,8,128]{2,1,0:T(8,128)S(1)}, f32[8,8,128]{2,1,0:T(8,128)S(1)}, u32[]{:S(2)}, u32[]{:S(2)}) collective-permute-start(f32[8,8,128]{2,1,0:T(8,128)S(1)} %get-tuple-element.43.ln_ref), channel_id=1, source_target_pairs={{0,1},{1,0},{2,3},{3,2},{4,5},{5,4},{6,7},{7,6},{8,9},{9,8},{10,11... | collective-permute-start | bytes 98312 | tf_op jit(solution)/shard_map/ppermute | solution.py:377

commit v6 on v5

--- a/solution.py
+++ b/solution.py
@@ -12,6 +12,7 @@
 
 F32 = jnp.float32
 LIMIT = 40 * 1024 * 1024
+PIECES = ((0, 8), (8, 24))
 
 
 def shape(*dims):
@@ -118,12 +119,13 @@
         fetch[-1].start()
     for part in range(4):
         fetch[part].wait()
-        out = (far_ref, far_late_ref)[part // 2]
-
-        def body(b, carry, part=part, out=out):
+        out = far_late_ref if part else far_ref
+        first = max(part - 1, 0) * 32
+
+        def body(b, carry, part=part, out=out, first=first):
             at = pl.ds(part * 32 + b * 8, 8)
             top, bottom = (e_ref[at, pl.ds(n, 8, stride=2), :] for n in range(2))
-            out[pl.ds(part % 2 * 32 + b * 8, 8)] = if_odd(place_ref, bottom, top)
+            out[pl.ds(first + b * 8, 8)] = if_odd(place_ref, bottom, top)
             near_ref[at] = if_odd(place_ref, top, bottom)
             return carry
 
@@ -160,29 +162,29 @@
             target_ref[t, j] = row(inn_ref, t)
 
 
-def members(e_refs, q, half):
+def members(e_refs, q, piece):
     if q < 2:
-        return e_refs[q * 2 + half], 0
-    return e_refs[q + 2], half * 64
+        return e_refs[q * 2 + piece], 0
+    return e_refs[q + 2], PIECES[piece][0] * 4
 
 
 def first_kernel(place_ref, w0_ref, w1_ref, far_ref, near_ref, *refs):
     *e_refs, part_ref = refs
     sums = (jnp.zeros((8, 128), F32),) * 8
-    for half in range(2):
-
-        def body(n, sums, half=half):
-            m = half * 16 + n
+    for piece, (first, count) in enumerate(PIECES):
+
+        def body(n, sums, piece=piece, first=first):
+            m = first + n
             a, b = w0_ref[m], w1_ref[m]
             f0 = C_MID * a + C_SIDE * (if_inside(place_ref, far_ref[m]) + b)
             f1 = C_MID * b + C_SIDE * (a + near_ref[m])
             sums = list(sums)
             for t in range(4):
-                sums[t] = sums[t] + e_refs[half][n * 4 + t] * f0
-                sums[4 + t] = sums[4 + t] + e_refs[2][half * 64 + n * 4 + t] * f1
+                sums[t] = sums[t] + e_refs[piece][n * 4 + t] * f0
+                sums[4 + t] = sums[4 + t] + e_refs[2][m * 4 + t] * f1
             return tuple(sums)
 
-        sums = lax.fori_loop(0, 16, body, sums, unroll=4)
+        sums = lax.fori_loop(0, count, body, sums, unroll=8)
     for n in range(8):
         part_ref[n] = sums[n]
 
@@ -291,46 +293,47 @@
 
 
 def smoothed_back(e_refs, rows, s_ref):
-    for half in range(2):
-
-        def body(b, carry, half=half):
+    for piece, (first, count) in enumerate(PIECES):
+
+        def body(b, carry, piece=piece, first=first):
             back = []
             for q in range(4):
-                ref, first = members(e_refs, q, half)
-                x = ref[pl.ds(first + b * 16, 16)].reshape(4, 4, 8, 128)
+                ref, start = members(e_refs, q, piece)
+                x = ref[pl.ds(start + b * 16, 16)].reshape(4, 4, 8, 128)
                 total = x[:, 0] * rows[q][0]
                 for t in range(1, 4):
                     total = total + x[:, t] * rows[q][t]
                 back.append(total)
-            at = pl.ds(half * 16 + b * 4, 4)
+            at = pl.ds(first + b * 4, 4)
             for r in range(2):
                 s_ref[r, at] = C_MID * back[r + 1] + C_SIDE * (back[r] + back[r + 2])
             return carry
 
-        lax.fori_loop(0, 4, body, 0, unroll=2)
+        lax.fori_loop(0, count // 4, body, 0, unroll=2)
 
 
 def middle_kernel(place_ref, lf_ref, ln_ref, rf_ref, rn_ref, *refs):
-    *e_refs, band_ref, v_ref, new_ref, part_ref, s_ref = refs
+    *e_refs, band_ref, v_ref, new_ref, part_ref, s_ref, w_ref = refs
     rows = adjoint_rows(place_ref, (lf_ref, ln_ref, rf_ref, rn_ref))
     smoothed_back(e_refs, rows, s_ref)
-    for r in range(2):
-        scale = scale_of(place_ref[2 + r])
-        for b in range(2):
-            at = pl.ds(b * 16, 16)
-            old = v_ref[r, at]
-            gradient = old + filtered(s_ref[r, at], band_ref[r], scale)
-            new = old - STEP_SIZE * gradient
-            new_ref[r, at] = new
-            s_ref[r, at] = filtered(new, band_ref[r], scale)
+    chunks = [(r, pl.ds(b * 16, 16)) for b in range(2) for r in range(2)]
+    scales = [scale_of(place_ref[2 + r]) for r in range(2)]
+    fresh = []
+    for r, at in chunks:
+        old = v_ref[r, at]
+        gradient = old + filtered(s_ref[r, at], band_ref[r], scales[r])
+        fresh.append(old - STEP_SIZE * gradient)
+        new_ref[r, at] = fresh[-1]
+    for (r, at), new in zip(chunks, fresh):
+        w_ref[r, at] = filtered(new, band_ref[r], scales[r])
     sums = (jnp.zeros((8, 128), F32),) * 16
-    for half in range(2):
-
-        def body(b, sums, half=half):
+    for piece, (first, count) in enumerate(PIECES):
+
+        def body(b, sums, piece=piece, first=first):
             sums = list(sums)
             for i in range(4):
                 n = b * 4 + i
-                w = [s_ref[r, half * 16 + n] for r in range(2)]
+                w = [w_ref[r, first + n] for r in range(2)]
                 forward = [
                     C_SIDE * w[0],
                     C_MID * w[0] + C_SIDE * w[1],
@@ -338,13 +341,13 @@
                     C_SIDE * w[1],
                 ]
                 for q in range(4):
-                    ref, first = members(e_refs, q, half)
+                    ref, start = members(e_refs, q, piece)
                     for t in range(4):
-                        x = ref[first + n * 4 + t]
+                        x = ref[start + n * 4 + t]
                         sums[q * 4 + t] = sums[q * 4 + t] + x * forward[q]
             return tuple(sums)
 
-        sums = lax.fori_loop(0, 4, body, sums)
+        sums = lax.fori_loop(0, count // 4, body, sums, unroll=2)
     for t in range(4):
         part_ref[t], part_ref[4 + t] = if_inside(place_ref, sums[t]), sums[4 + t]
         part_ref[8 + t], part_ref[12 + t] = sums[12 + t], sums[8 + t]
@@ -354,17 +357,16 @@
     *e_refs, band_ref, v_ref, out_ref, s_ref = refs
     rows = adjoint_rows(place_ref, (lf_ref, ln_ref, rf_ref, rn_ref))
     smoothed_back(e_refs, rows, s_ref)
-    for r in range(2):
-        scale = scale_of(place_ref[2 + r])
-        for b in range(2):
-            at = pl.ds(b * 16, 16)
-            old = v_ref[r, at]
-            gradient = old + filtered(s_ref[r, at], band_ref[r], scale)
-            s_ref[r, at] = old - STEP_SIZE * gradient
+    scales = [scale_of(place_ref[2 + r]) for r in range(2)]
     for b in range(2):
         at = pl.ds(b * 16, 16)
-        out_ref[at, pl.ds(0, 8, stride=2), :] = if_odd(place_ref, s_ref[1, at], s_ref[0, at])
-        out_ref[at, pl.ds(1, 8, stride=2), :] = if_odd(place_ref, s_ref[0, at], s_ref[1, at])
+        new = []
+        for r in range(2):
+            old = v_ref[r, at]
+            gradient = old + filtered(s_ref[r, at], band_ref[r], scales[r])
+            new.append(old - STEP_SIZE * gradient)
+        out_ref[at, pl.ds(0, 8, stride=2), :] = if_odd(place_ref, new[1], new[0])
+        out_ref[at, pl.ds(1, 8, stride=2), :] = if_odd(place_ref, new[0], new[1])
 
 
 def from_far(x):
@@ -412,7 +414,7 @@
     far, near = swapped(w0, w1)
     e0, e0_late, e1 = call(
         split_kernel,
-        (shape(64, 8, 128), shape(64, 8, 128), shape(128, 8, 128)),
+        (shape(32, 8, 128), shape(96, 8, 128), shape(128, 8, 128)),
         (),
         scalars,
         (pltpu.VMEM((128, 16, 128), F32), pltpu.SemaphoreType.DMA((4,))),
@@ -443,7 +445,7 @@
         (rows, shape(16, 8, 128)),
         tuple(sent) + swapped(*sent) + ensembles + (old,),
         scalars,
-        smoothed,
+        smoothed * 2,
     )
     sent = call(sum_kernel, (eight, eight), (lax.all_gather(part, "mem"),))
     sent = call(

time: 97.1 us -> 92.8 us (0.956)
  waiting for transfers between devices: 27.9 us -> 24.4 us
    ppermute x7, waiting for transfers between devices: 27.9 us -> 24.4 us  [from_far(): return lax.ppermute(x, 'lat', pairs)]
  transfers between devices with their start and end apart: 13 -> 13, of which waited for: 5 -> 5; matrix products, arithmetic and copies ran while one was open for 0% -> 0% of each run, Pallas kernels for 5% -> 6%
where the time goes in v6:
time: 92.8 us; the launch traced here: 91.1 us
  starting transfers between devices  32.8 us (35%)
  waiting for transfers between devices  24.4 us (26%)
  blocking collectives  21.1 us (23%)
  Pallas kernels  11.6 us (12%)
    ppermute x7, starting transfers between devices, from_far(): return lax.ppermute(x, 'lat', pairs)  31.5 us
    ppermute x7, waiting for transfers between devices, from_far(): return lax.ppermute(x, 'lat', pairs)  24.4 us
    pallas_call x10, Pallas kernels, call(): pl.pallas_call(kernel, out_shape=outs, in_specs=in_specs, out_specs=jax.t...  11.6 us
    all_gather x1, blocking collectives, descent(): c0, c1 = call(sum_kernel, (four, four), (lax.all_gather(part, 'mem'),))  11 us
    all_gather x1, blocking collectives, descent(): sent = call(sum_kernel, (eight, eight), (lax.all_gather(part, 'mem'),))  10.1 us
  transfers between devices with their start and end apart: 13, of which 5 were waited for; matrix products, arithmetic and copies ran while one was open for 0% of the time, Pallas kernels for 6%

profile of v6, /device:TPU:30, one launch (start us, length us, event | category | flops | bytes accessed | tf_op | source)
XLA Modules:
  0.0 91.1 jit_solution(1933405062288053963)
XLA Ops:
  0.0 0.7 copy-done.6
  0.7 0.1 rev.3
  0.8 0.1 pad_add_fusion.place_ref
  0.8 1.8 %shard_map.83 = (f32[32,8,128]{2,1,0:T(8,128)S(1)}, f32[96,8,128]{2,1,0:T(8,128)S(1)}, f32[128,8,128]{2,1,0:T(8,128)S(1)}) custom-call(s32[4]{0:T(128)S(1)} %pad_add_fusion.place_ref, f32[128,16,128]{2,1,0:T(8,128)} %bitcast.45), custom_call_target="tpu_custom_call" | custom-call | flops 1000000 | bytes 1000000 | tf_op jit(solution)/shard_map/pallas_call | solution.py:28
  2.6 0.8 collective-permute-start.8
  3.5 4.2 %collective-permute-start.7 = (f32[96,8,128]{2,1,0:T(8,128)S(1)}, f32[96,8,128]{2,1,0:T(8,128)S(1)}, u32[]{:S(2)}, u32[]{:S(2)}) collective-permute-start(f32[96,8,128]{2,1,0:T(8,128)S(1)} %get-tuple-element.28.refs_1_.refs_3_), channel_id=1, source_target_pairs={{0,0},{1,2},{2,1},{3,4},{4,3},{5,6},{6,5},{7,8},{8,7},{9,10},{10,9... | collective-permute-start | bytes 1179656 | tf_op jit(solution)/shard_map/ppermute | solution.py:375
  7.7 0.1 pad_add_fusion.1.place_ref
  7.8 2.0 %shard_map.82 = (f32[32,8,128]{2,1,0:T(8,128)S(1)}, f32[32,8,128]{2,1,0:T(8,128)S(1)}, f32[2,32,8,128]{3,2,1,0:T(8,128)S(1)}, bf16[2,256,128]{2,1,0:T(8,128)(2,1)S(1)}) custom-call(s32[2]{0:T(128)S(1)} %pad_add_fusion.1.place_ref, s32[2]{0:T(128)} %widths_hbm.1, f32[32,16,128]{2,1,0:T(8,128)} %bitcast.46), custom_call_target="tpu_custom_call" | custom-call | flops 1000000 | bytes 1000000 | tf_op jit(solution)/shard_map/pallas_call | solution.py:28
  9.8 5.8 %collective-permute-start = (f32[32,8,128]{2,1,0:T(8,128)S(1)}, f32[32,8,128]{2,1,0:T(8,128)S(1)}, u32[]{:S(2)}, u32[]{:S(2)}) collective-permute-start(f32[32,8,128]{2,1,0:T(8,128)S(1)} %get-tuple-element.25.w0_ref), channel_id=1, source_target_pairs={{0,0},{1,2},{2,1},{3,4},{4,3},{5,6},{6,5},{7,8},{8,7},{9,10},{10,9... | collective-permute-start | bytes 393224 | tf_op jit(solution)/shard_map/ppermute | solution.py:375
  15.6 0.1 collective-permute-start.1
  15.7 4.2 %collective-permute-start.6 = (f32[32,8,128]{2,1,0:T(8,128)S(1)}, f32[32,8,128]{2,1,0:T(8,128)S(1)}, u32[]{:S(2)}, u32[]{:S(2)}) collective-permute-start(f32[32,8,128]{2,1,0:T(8,128)S(1)} %get-tuple-element.27.refs_0_.refs_2_), channel_id=1, source_target_pairs={{0,0},{1,2},{2,1},{3,4},{4,3},{5,6},{6,5},{7,8},{8,7},{9,10},{10,9... | collective-permute-start | bytes 393224 | tf_op jit(solution)/shard_map/ppermute | solution.py:375
  20.0 3.0 %collective-permute-done.far_ref = f32[32,8,128]{2,1,0:T(8,128)S(1)} collective-permute-done((f32[32,8,128]{2,1,0:T(8,128)S(1)}, f32[32,8,128]{2,1,0:T(8,128)S(1)}, u32[]{:S(2)}, u32[]{:S(2)}) %collective-permute-start) | collective-permute-done | bytes 131104 | tf_op jit(solution)/shard_map/ppermute | solution.py:375
  23.0 0.0 collective-permute-done.1.near_ref
  23.0 0.0 copy-start.5
  23.0 0.0 copy-start.1
  23.0 0.7 shard_map.84
  23.7 0.0 copy-start
  23.7 11.0 %all-gather = f32[32,8,128]{2,1,0:T(8,128)S(1)} all-gather(f32[8,8,128]{2,1,0:T(8,128)S(1)} %shard_map.84), channel_id=2, replica_groups=mesh['mem'=4,'lat'=64] {'mem'}, dimensions={0}, use_global_device_ids=true | all-gather | bytes 163840 | tf_op jit(solution)/shard_map/all_gather | solution.py:436
  34.7 3.6 %collective-permute-start.2 = (f32[4,8,128]{2,1,0:T(8,128)S(1)}, f32[4,8,128]{2,1,0:T(8,128)S(1)}, u32[]{:S(2)}, u32[]{:S(2)}) collective-permute-start(f32[4,8,128]{2,1,0:T(8,128)S(1)} %get-tuple-element.30.c0_ref), channel_id=1, source_target_pairs={{0,0},{1,2},{2,1},{3,4},{4,3},{5,6},{6,5},{7,8},{8,7},{9,10},{10,9... | collective-permute-start | bytes 49160 | tf_op jit(solution)/shard_map/ppermute | solution.py:375
  38.3 0.1 collective-permute-start.3
  38.4 0.0 copy-done.2
  38.4 0.0 copy-done.3
  38.4 0.0 copy-done.4
  38.4 0.0 copy-done.5
  38.4 0.8 shard_map.86
  39.3 5.2 %collective-permute-done.2.far_ref = f32[4,8,128]{2,1,0:T(8,128)S(1)} collective-permute-done((f32[4,8,128]{2,1,0:T(8,128)S(1)}, f32[4,8,128]{2,1,0:T(8,128)S(1)}, u32[]{:S(2)}, u32[]{:S(2)}) %collective-permute-start.2) | collective-permute-done | bytes 16416 | tf_op jit(solution)/shard_map/ppermute | solution.py:375
  44.5 0.0 collective-permute-done.3.near_ref
  44.5 0.0 copy-done.1
  44.5 1.5 %shard_map.87 = (f32[8,8,128]{2,1,0:T(8,128)S(1)}, f32[8,8,128]{2,1,0:T(8,128)S(1)}) custom-call(f32[4,8,128]{2,1,0:T(8,128)S(1)} %collective-permute-done.2.far_ref, f32[4,8,128]{2,1,0:T(8,128)S(1)} %get-tuple-element.30.c0_ref, f32[4,8,128]{2,1,0:T(8,128)S(1)} %get-tuple-element.31.c1_ref, f32[4,8,128]{2,1,0:T(8,128)S(1)} %collective-permute-done.3.near_ref, ...), custom_call_target="tpu_custom_call" | custom-call | flops 1000000 | bytes 1000000 | tf_op jit(solution)/shard_map/pallas_call | solution.py:28
  46.1 4.0 %collective-permute-start.4 = (f32[8,8,128]{2,1,0:T(8,128)S(1)}, f32[8,8,128]{2,1,0:T(8,128)S(1)}, u32[]{:S(2)}, u32[]{:S(2)}) collective-permute-start(f32[8,8,128]{2,1,0:T(8,128)S(1)} %get-tuple-element.35.lf_ref), channel_id=1, source_target_pairs={{0,0},{1,2},{2,1},{3,4},{4,3},{5,6},{6,5},{7,8},{8,7},{9,10},{10,9... | collective-permute-start | bytes 98312 | tf_op jit(solution)/shard_map/ppermute | solution.py:375
  50.1 0.1 collective-permute-start.5
  50.2 0.0 collective-permute-done.6.refs_0_
  50.2 5.9 %collective-permute-done.4.rf_ref = f32[8,8,128]{2,1,0:T(8,128)S(1)} collective-permute-done((f32[8,8,128]{2,1,0:T(8,128)S(1)}, f32[8,8,128]{2,1,0:T(8,128)S(1)}, u32[]{:S(2)}, u32[]{:S(2)}) %collective-permute-start.4) | collective-permute-done | bytes 32800 | tf_op jit(solution)/shard_map/ppermute | solution.py:375
  56.1 0.0 collective-permute-done.5.rn_ref
  56.1 0.0 collective-permute-done.7.refs_1_
  56.1 0.0 collective-permute-done.8.refs_5_
  56.1 1.5 %shard_map.88 = (f32[2,32,8,128]{3,2,1,0:T(8,128)S(1)}, f32[16,8,128]{2,1,0:T(8,128)S(1)}) custom-call(s32[4]{0:T(128)S(1)} %pad_add_fusion.place_ref, f32[8,8,128]{2,1,0:T(8,128)S(1)} %get-tuple-element.35.lf_ref, f32[8,8,128]{2,1,0:T(8,128)S(1)} %get-tuple-element.36.ln_ref, f32[8,8,128]{2,1,0:T(8,128)S(1)} %collective-permute-done.4.rf_ref, ...), custom_call_target="tpu_custom_call" | custom-call | flops 1000000 | bytes 1000000 | tf_op jit(solution)/shard_map/pallas_call | solution.py:28
  57.6 10.1 %all-gather.1 = f32[64,8,128]{2,1,0:T(8,128)S(1)} all-gather(f32[16,8,128]{2,1,0:T(8,128)S(1)} %get-tuple-element.39), channel_id=3, replica_groups=mesh['mem'=4,'lat'=64] {'mem'}, dimensions={0}, use_global_device_ids=true | all-gather | bytes 327680 | tf_op jit(solution)/shard_map/all_gather | solution.py:450
  67.7 4.8 %collective-permute-start.9 = (f32[8,8,128]{2,1,0:T(8,128)S(1)}, f32[8,8,128]{2,1,0:T(8,128)S(1)}, u32[]{:S(2)}, u32[]{:S(2)}) collective-permute-start(f32[8,8,128]{2,1,0:T(8,128)S(1)} %get-tuple-element.40.refs_0_), channel_id=1, source_target_pairs={{0,0},{1,2},{2,1},{3,4},{4,3},{5,6},{6,5},{7,8},{8,7},{9,10},{10,9... | collective-permute-start | bytes 98312 | tf_op jit(solution)/shard_map/ppermute | solution.py:375
  72.5 0.1 collective-permute-start.10
  72.6 5.2 %collective-permute-done.9.refs_2_ = f32[8,8,128]{2,1,0:T(8,128)S(1)} collective-permute-done((f32[8,8,128]{2,1,0:T(8,128)S(1)}, f32[8,8,128]{2,1,0:T(8,128)S(1)}, u32[]{:S(2)}, u32[]{:S(2)}) %collective-permute-start.9) | collective-permute-done | bytes 32800 | tf_op jit(solution)/shard_map/ppermute | solution.py:375
  77.7 0.0 collective-permute-done.10.refs_3_
  77.7 1.5 %shard_map.90 = (f32[8,8,128]{2,1,0:T(8,128)S(1)}, f32[8,8,128]{2,1,0:T(8,128)S(1)}) custom-call(f32[8,8,128]{2,1,0:T(8,128)S(1)} %get-tuple-element.40.refs_0_, f32[8,8,128]{2,1,0:T(8,128)S(1)} %get-tuple-element.41.refs_1_, f32[8,8,128]{2,1,0:T(8,128)S(1)} %collective-permute-done.9.refs_2_, f32[8,8,128]{2,1,0:T(8,128)S(1)} %collective-permute-done.10.refs_3_, ...), custom_call_target="tpu_custom_call" | custom-call | flops 1000000 | bytes 1000000 | tf_op jit(solution)/shard_map/pallas_call | solution.py:28
  79.3 4.8 %collective-permute-start.11 = (f32[8,8,128]{2,1,0:T(8,128)S(1)}, f32[8,8,128]{2,1,0:T(8,128)S(1)}, u32[]{:S(2)}, u32[]{:S(2)}) collective-permute-start(f32[8,8,128]{2,1,0:T(8,128)S(1)} %get-tuple-element.42.lf_ref), channel_id=1, source_target_pairs={{0,0},{1,2},{2,1},{3,4},{4,3},{5,6},{6,5},{7,8},{8,7},{9,10},{10,9... | collective-permute-start | bytes 98312 | tf_op jit(solution)/shard_map/ppermute | solution.py:375
  84.0 0.1 collective-permute-start.12
  84.1 5.2 %collective-permute-done.11.rf_ref = f32[8,8,128]{2,1,0:T(8,128)S(1)} collective-permute-done((f32[8,8,128]{2,1,0:T(8,128)S(1)}, f32[8,8,128]{2,1,0:T(8,128)S(1)}, u32[]{:S(2)}, u32[]{:S(2)}) %collective-permute-start.11) | collective-permute-done | bytes 32800 | tf_op jit(solution)/shard_map/ppermute | solution.py:375
  89.3 0.0 collective-permute-done.12.rn_ref
  89.3 1.8 %shard_map.91 = f32[32,16,128]{2,1,0:T(8,128)} custom-call(s32[4]{0:T(128)S(1)} %pad_add_fusion.place_ref, f32[8,8,128]{2,1,0:T(8,128)S(1)} %get-tuple-element.42.lf_ref, f32[8,8,128]{2,1,0:T(8,128)S(1)} %get-tuple-element.43.ln_ref, f32[8,8,128]{2,1,0:T(8,128)S(1)} %collective-permute-done.11.rf_ref, f32[8,8,128]{2,1,0:T(8,128)S(1)} %collective-permute-done.12.rn_ref, ...), custom_call_target="tpu_custom_call" | custom-call | flops 1000000 | bytes 1000000 | tf_op jit(solution)/shard_map/pallas_call | solution.py:28
  (8 shorter events, 0.0 us)
Async XLA Ops:
  0.0 0.7 copy-start.6
  2.6 53.4 %collective-permute-start.8 = (f32[128,8,128]{2,1,0:T(8,128)S(1)}, f32[128,8,128]{2,1,0:T(8,128)S(1)}, u32[]{:S(2)}, u32[]{:S(2)}) collective-permute-start(f32[128,8,128]{2,1,0:T(8,128)S(1)} %get-tuple-element.29.refs_2_.refs_4_), channel_id=1, source_target_pairs={{0,1},{1,0},{2,3},{3,2},{4,5},{5,4},{6,7},{7,6},{8,9},{9,8},{10,11... | collective-permute-start | bytes 1572872 | tf_op jit(solution)/shard_map/ppermute | solution.py:379
  3.5 52.6 %collective-permute-start.7 = (f32[96,8,128]{2,1,0:T(8,128)S(1)}, f32[96,8,128]{2,1,0:T(8,128)S(1)}, u32[]{:S(2)}, u32[]{:S(2)}) collective-permute-start(f32[96,8,128]{2,1,0:T(8,128)S(1)} %get-tuple-element.28.refs_1_.refs_3_), channel_id=1, source_target_pairs={{0,0},{1,2},{2,1},{3,4},{4,3},{5,6},{6,5},{7,8},{8,7},{9,10},{10,9... | collective-permute-start | bytes 1179656 | tf_op jit(solution)/shard_map/ppermute | solution.py:375
  9.8 13.2 %collective-permute-start = (f32[32,8,128]{2,1,0:T(8,128)S(1)}, f32[32,8,128]{2,1,0:T(8,128)S(1)}, u32[]{:S(2)}, u32[]{:S(2)}) collective-permute-start(f32[32,8,128]{2,1,0:T(8,128)S(1)} %get-tuple-element.25.w0_ref), channel_id=1, source_target_pairs={{0,0},{1,2},{2,1},{3,4},{4,3},{5,6},{6,5},{7,8},{8,7},{9,10},{10,9... | collective-permute-start | bytes 393224 | tf_op jit(solution)/shard_map/ppermute | solution.py:375
  15.6 7.3 %collective-permute-start.1 = (f32[32,8,128]{2,1,0:T(8,128)S(1)}, f32[32,8,128]{2,1,0:T(8,128)S(1)}, u32[]{:S(2)}, u32[]{:S(2)}) collective-permute-start(f32[32,8,128]{2,1,0:T(8,128)S(1)} %get-tuple-element.26.w1_ref), channel_id=1, source_target_pairs={{0,1},{1,0},{2,3},{3,2},{4,5},{5,4},{6,7},{7,6},{8,9},{9,8},{10,11... | collective-permute-start | bytes 393224 | tf_op jit(solution)/shard_map/ppermute | solution.py:379
  15.7 34.5 %collective-permute-start.6 = (f32[32,8,128]{2,1,0:T(8,128)S(1)}, f32[32,8,128]{2,1,0:T(8,128)S(1)}, u32[]{:S(2)}, u32[]{:S(2)}) collective-permute-start(f32[32,8,128]{2,1,0:T(8,128)S(1)} %get-tuple-element.27.refs_0_.refs_2_), channel_id=1, source_target_pairs={{0,0},{1,2},{2,1},{3,4},{4,3},{5,6},{6,5},{7,8},{8,7},{9,10},{10,9... | collective-permute-start | bytes 393224 | tf_op jit(solution)/shard_map/ppermute | solution.py:375
  23.0 15.4 %copy-start.2 = (s32[4,4,2048]{2,1,0:T(4,128)S(1)}, s32[4,4,2048]{2,1,0:T(4,128)}, u32[]{:S(2)}) copy-start(s32[4,4,2048]{2,1,0:T(4,128)} %param.11) | copy-start | bytes 393220
  23.0 15.5 %copy-start.3 = (f32[4,4,2048]{2,1,0:T(4,128)S(1)}, f32[4,4,2048]{2,1,0:T(4,128)}, u32[]{:S(2)}) copy-start(f32[4,4,2048]{2,1,0:T(4,128)} %param.12) | copy-start | bytes 393220
  23.0 15.5 %copy-start.4 = (s32[4,4,2048]{2,1,0:T(4,128)S(1)}, s32[4,4,2048]{2,1,0:T(4,128)}, u32[]{:S(2)}) copy-start(s32[4,4,2048]{2,1,0:T(4,128)} %param.13) | copy-start | bytes 393220
  23.0 15.5 %copy-start.5 = (f32[4,4,2048]{2,1,0:T(4,128)S(1)}, f32[4,4,2048]{2,1,0:T(4,128)}, u32[]{:S(2)}) copy-start(f32[4,4,2048]{2,1,0:T(4,128)} %param.14) | copy-start | bytes 393220
  23.0 21.5 %copy-start.1 = (bf16[256,1280]{1,0:T(8,128)(2,1)S(1)}, bf16[256,1280]{1,0:T(8,128)(2,1)}, u32[]{:S(2)}) copy-start(bf16[256,1280]{1,0:T(8,128)(2,1)} %constant.22.clone.refs_3_.refs_7_) | copy-start | bytes 1966084
  23.7 20.8 %copy-start = (bf16[1280,256]{1,0:T(8,128)(2,1)S(1)}, bf16[1280,256]{1,0:T(8,128)(2,1)}, u32[]{:S(2)}) copy-start(bf16[1280,256]{1,0:T(8,128)(2,1)} %constant.30.refs_4_.refs_8_) | copy-start | bytes 1966084
  34.7 9.9 %collective-permute-start.2 = (f32[4,8,128]{2,1,0:T(8,128)S(1)}, f32[4,8,128]{2,1,0:T(8,128)S(1)}, u32[]{:S(2)}, u32[]{:S(2)}) collective-permute-start(f32[4,8,128]{2,1,0:T(8,128)S(1)} %get-tuple-element.30.c0_ref), channel_id=1, source_target_pairs={{0,0},{1,2},{2,1},{3,4},{4,3},{5,6},{6,5},{7,8},{8,7},{9,10},{10,9... | collective-permute-start | bytes 49160 | tf_op jit(solution)/shard_map/ppermute | solution.py:375
  38.3 6.2 %collective-permute-start.3 = (f32[4,8,128]{2,1,0:T(8,128)S(1)}, f32[4,8,128]{2,1,0:T(8,128)S(1)}, u32[]{:S(2)}, u32[]{:S(2)}) collective-permute-start(f32[4,8,128]{2,1,0:T(8,128)S(1)} %get-tuple-element.31.c1_ref), channel_id=1, source_target_pairs={{0,1},{1,0},{2,3},{3,2},{4,5},{5,4},{6,7},{7,6},{8,9},{9,8},{10,11... | collective-permute-start | bytes 49160 | tf_op jit(solution)/shard_map/ppermute | solution.py:379
  46.1 10.0 %collective-permute-start.4 = (f32[8,8,128]{2,1,0:T(8,128)S(1)}, f32[8,8,128]{2,1,0:T(8,128)S(1)}, u32[]{:S(2)}, u32[]{:S(2)}) collective-permute-start(f32[8,8,128]{2,1,0:T(8,128)S(1)} %get-tuple-element.35.lf_ref), channel_id=1, source_target_pairs={{0,0},{1,2},{2,1},{3,4},{4,3},{5,6},{6,5},{7,8},{8,7},{9,10},{10,9... | collective-permute-start | bytes 98312 | tf_op jit(solution)/shard_map/ppermute | solution.py:375
  50.1 6.0 %collective-permute-start.5 = (f32[8,8,128]{2,1,0:T(8,128)S(1)}, f32[8,8,128]{2,1,0:T(8,128)S(1)}, u32[]{:S(2)}, u32[]{:S(2)}) collective-permute-start(f32[8,8,128]{2,1,0:T(8,128)S(1)} %get-tuple-element.36.ln_ref), channel_id=1, source_target_pairs={{0,1},{1,0},{2,3},{3,2},{4,5},{5,4},{6,7},{7,6},{8,9},{9,8},{10,11... | collective-permute-start | bytes 98312 | tf_op jit(solution)/shard_map/ppermute | solution.py:379
  67.7 10.0 %collective-permute-start.9 = (f32[8,8,128]{2,1,0:T(8,128)S(1)}, f32[8,8,128]{2,1,0:T(8,128)S(1)}, u32[]{:S(2)}, u32[]{:S(2)}) collective-permute-start(f32[8,8,128]{2,1,0:T(8,128)S(1)} %get-tuple-element.40.refs_0_), channel_id=1, source_target_pairs={{0,0},{1,2},{2,1},{3,4},{4,3},{5,6},{6,5},{7,8},{8,7},{9,10},{10,9... | collective-permute-start | bytes 98312 | tf_op jit(solution)/shard_map/ppermute | solution.py:375
  72.5 5.3 %collective-permute-start.10 = (f32[8,8,128]{2,1,0:T(8,128)S(1)}, f32[8,8,128]{2,1,0:T(8,128)S(1)}, u32[]{:S(2)}, u32[]{:S(2)}) collective-permute-start(f32[8,8,128]{2,1,0:T(8,128)S(1)} %get-tuple-element.41.refs_1_), channel_id=1, source_target_pairs={{0,1},{1,0},{2,3},{3,2},{4,5},{5,4},{6,7},{7,6},{8,9},{9,8},{10,11... | collective-permute-start | bytes 98312 | tf_op jit(solution)/shard_map/ppermute | solution.py:379
  79.3 10.0 %collective-permute-start.11 = (f32[8,8,128]{2,1,0:T(8,128)S(1)}, f32[8,8,128]{2,1,0:T(8,128)S(1)}, u32[]{:S(2)}, u32[]{:S(2)}) collective-permute-start(f32[8,8,128]{2,1,0:T(8,128)S(1)} %get-tuple-element.42.lf_ref), channel_id=1, source_target_pairs={{0,0},{1,2},{2,1},{3,4},{4,3},{5,6},{6,5},{7,8},{8,7},{9,10},{10,9... | collective-permute-start | bytes 98312 | tf_op jit(solution)/shard_map/ppermute | solution.py:375
  84.0 5.3 %collective-permute-start.12 = (f32[8,8,128]{2,1,0:T(8,128)S(1)}, f32[8,8,128]{2,1,0:T(8,128)S(1)}, u32[]{:S(2)}, u32[]{:S(2)}) collective-permute-start(f32[8,8,128]{2,1,0:T(8,128)S(1)} %get-tuple-element.43.ln_ref), channel_id=1, source_target_pairs={{0,1},{1,0},{2,3},{3,2},{4,5},{5,4},{6,7},{7,6},{8,9},{9,8},{10,11... | collective-permute-start | bytes 98312 | tf_op jit(solution)/shard_map/ppermute | solution.py:379

commit v7 on v6

--- a/solution.py
+++ b/solution.py
@@ -19,7 +19,7 @@
     return jax.ShapeDtypeStruct(dims, F32)
 
 
-def call(kernel, outs, args, scalars=(), scratch=(), far_args=()):
+def call(kernel, outs, args, scalars=(), scratch=(), far_args=(), out_space=pltpu.VMEM):
     in_specs = [pl.BlockSpec(memory_space=pltpu.SMEM)] * len(scalars)
     in_specs += [pl.BlockSpec(memory_space=pltpu.HBM)] * len(far_args)
     in_specs += [pl.BlockSpec(memory_space=pltpu.VMEM)] * len(args)
@@ -29,7 +29,7 @@
         kernel,
         out_shape=outs,
         in_specs=in_specs,
-        out_specs=jax.tree.map(lambda _: pl.BlockSpec(memory_space=pltpu.VMEM), outs),
+        out_specs=jax.tree.map(lambda _: pl.BlockSpec(memory_space=out_space), outs),
         scratch_shapes=list(scratch),
         compiler_params=pltpu.CompilerParams(vmem_limit_bytes=LIMIT),
         cost_estimate=pl.CostEstimate(flops=1_000_000, transcendentals=0, bytes_accessed=1_000_000),
@@ -84,13 +84,18 @@
     return jnp.where(jnp.full((8, 128), place_ref[0], jnp.int32) > 0, odd, even)
 
 
-def filter_kernel(
-    place_ref, widths_hbm, v_hbm, w0_ref, w1_ref, old_ref, band_ref, widths_ref, v_ref, sems
+def opening_kernel(
+    place_ref, widths_hbm, v_hbm, e_hbm,
+    w0_ref, w1_ref, old_ref, band_ref, scale_ref, far_ref, far_late_ref, near_ref,
+    widths_ref, v_ref, e_ref, sems,
 ):
     fetch = [pltpu.make_async_copy(widths_hbm, widths_ref, sems.at[0])]
     for b in range(2):
         at = pl.ds(b * 16, 16)
         fetch.append(pltpu.make_async_copy(v_hbm.at[at], v_ref.at[at], sems.at[1 + b]))
+    for part in range(4):
+        at = pl.ds(part * 32, 32)
+        fetch.append(pltpu.make_async_copy(e_hbm.at[at], e_ref.at[at], sems.at[3 + part]))
     for copy in fetch:
         copy.start()
     away = jnp.abs(position(iota((256, 128), 0)) - iota((256, 128), 1))
@@ -101,6 +106,7 @@
         inside = away <= jnp.full((256, 128), width, jnp.int32)
         band_ref[r] = jnp.where(inside, 1.0, 0.0).astype(jnp.bfloat16)
         scales.append(scale_of(width))
+        scale_ref[r] = scales[r]
     for b in range(2):
         at = pl.ds(b * 16, 16)
         fetch[1 + b].wait()
@@ -109,27 +115,19 @@
             x = if_odd(place_ref, top, bottom) if r else if_odd(place_ref, bottom, top)
             old_ref[r, at] = x
             out[at] = filtered(x, band_ref[r], scales[r])
-
-
-def split_kernel(place_ref, e_hbm, far_ref, far_late_ref, near_ref, e_ref, sems):
-    fetch = []
     for part in range(4):
-        at = pl.ds(part * 32, 32)
-        fetch.append(pltpu.make_async_copy(e_hbm.at[at], e_ref.at[at], sems.at[part]))
-        fetch[-1].start()
-    for part in range(4):
-        fetch[part].wait()
+        fetch[3 + part].wait()
         out = far_late_ref if part else far_ref
         first = max(part - 1, 0) * 32
 
         def body(b, carry, part=part, out=out, first=first):
-            at = pl.ds(part * 32 + b * 8, 8)
+            at = pl.ds(part * 32 + b * 16, 16)
             top, bottom = (e_ref[at, pl.ds(n, 8, stride=2), :] for n in range(2))
-            out[pl.ds(first + b * 8, 8)] = if_odd(place_ref, bottom, top)
+            out[pl.ds(first + b * 16, 16)] = if_odd(place_ref, bottom, top)
             near_ref[at] = if_odd(place_ref, top, bottom)
             return carry
 
-        lax.fori_loop(0, 4, body, 0)
+        lax.fori_loop(0, 2, body, 0)
 
 
 def planes_kernel(place_ref, src_ref, wgt_ref, msk_ref, inn_ref, planes_ref, mask_ref, target_ref):
@@ -137,10 +135,10 @@
     odd = jnp.full((8, 128), place_ref[0], jnp.int32)
     for j in range(8):
         half, fr = j // 4, j % 4
-        at, mirrored = pl.ds(j, 8, stride=8), pl.ds(half * 4 + 3 - fr, 8, stride=8)
-
-        def row(ref, n, at=at, mirrored=mirrored):
-            return jnp.where(odd > 0, ref[n, mirrored, :], ref[n, at, :])
+        at = pl.ds(j + place_ref[0] * (3 - 2 * fr), 8, stride=8)
+
+        def row(ref, n, at=at):
+            return ref[n, at, :]
 
         own_row = jnp.where(odd > 0, 1 - fr // 2, fr // 2)
         codes, weights = [], []
@@ -313,11 +311,11 @@
 
 
 def middle_kernel(place_ref, lf_ref, ln_ref, rf_ref, rn_ref, *refs):
-    *e_refs, band_ref, v_ref, new_ref, part_ref, s_ref, w_ref = refs
+    *e_refs, band_ref, scale_ref, v_ref, new_ref, part_ref, s_ref, w_ref = refs
     rows = adjoint_rows(place_ref, (lf_ref, ln_ref, rf_ref, rn_ref))
     smoothed_back(e_refs, rows, s_ref)
     chunks = [(r, pl.ds(b * 16, 16)) for b in range(2) for r in range(2)]
-    scales = [scale_of(place_ref[2 + r]) for r in range(2)]
+    scales = [scale_ref[r] for r in range(2)]
     fresh = []
     for r, at in chunks:
         old = v_ref[r, at]
@@ -354,10 +352,11 @@
 
 
 def last_kernel(place_ref, lf_ref, ln_ref, rf_ref, rn_ref, *refs):
-    *e_refs, band_ref, v_ref, out_ref, s_ref = refs
+    *e_refs, band_ref, scale_ref, v_ref, out_hbm, s_ref, out_ref, sems = refs
     rows = adjoint_rows(place_ref, (lf_ref, ln_ref, rf_ref, rn_ref))
     smoothed_back(e_refs, rows, s_ref)
-    scales = [scale_of(place_ref[2 + r]) for r in range(2)]
+    scales = [scale_ref[r] for r in range(2)]
+    store = []
     for b in range(2):
         at = pl.ds(b * 16, 16)
         new = []
@@ -367,6 +366,10 @@
             new.append(old - STEP_SIZE * gradient)
         out_ref[at, pl.ds(0, 8, stride=2), :] = if_odd(place_ref, new[1], new[0])
         out_ref[at, pl.ds(1, 8, stride=2), :] = if_odd(place_ref, new[0], new[1])
+        store.append(pltpu.make_async_copy(out_ref.at[at], out_hbm.at[at], sems.at[b]))
+        store[b].start()
+    for copy in store:
+        copy.wait()
 
 
 def from_far(x):
@@ -393,34 +396,28 @@
     v = tiles(control)
     e = tiles(ensemble)
     lat, last = lax.axis_index("lat"), lax.axis_size("lat") - 1
-    odd = lat % 2
-    ends = jnp.stack([odd, (lat != 0) & (lat != last)]).astype(jnp.int32)
-    place = jnp.concatenate([ends, jnp.where(odd > 0, widths[::-1], widths)])
-    scalars = (place,)
+    scalars = (jnp.stack([lat % 2, (lat != 0) & (lat != last)]).astype(jnp.int32),)
     row, rows = shape(32, 8, 128), shape(2, 32, 8, 128)
-    band = jax.ShapeDtypeStruct((2, 256, 128), jnp.bfloat16)
-    w0, w1, old, band = call(
-        filter_kernel,
-        (row, row, rows, band),
+    w0, w1, old, band, scale, e0, e0_late, e1 = call(
+        opening_kernel,
+        (
+            *(row, row, rows, jax.ShapeDtypeStruct((2, 256, 128), jnp.bfloat16)),
+            *(shape(2, 8, 128), shape(32, 8, 128), shape(96, 8, 128), shape(128, 8, 128)),
+        ),
         (),
-        (ends,),
+        scalars,
         (
             pltpu.SMEM((2,), jnp.int32),
             pltpu.VMEM((32, 16, 128), F32),
-            pltpu.SemaphoreType.DMA((3,)),
+            pltpu.VMEM((128, 16, 128), F32),
+            pltpu.SemaphoreType.DMA((7,)),
         ),
-        (widths, v),
+        (widths, v, e),
     )
     far, near = swapped(w0, w1)
-    e0, e0_late, e1 = call(
-        split_kernel,
-        (shape(32, 8, 128), shape(96, 8, 128), shape(128, 8, 128)),
-        (),
-        scalars,
-        (pltpu.VMEM((128, 16, 128), F32), pltpu.SemaphoreType.DMA((4,))),
-        (e,),
-    )
-    ensembles = (*(from_far(e0), from_far(e0_late)), *(e0, e0_late, e1, from_near(e1)), band)
+    ensembles = (
+        *(from_far(e0), from_far(e0_late)), *(e0, e0_late, e1, from_near(e1)), *(band, scale)
+    )
     fields = call(
         planes_kernel,
         (shape(15, 8, 8, 128), shape(4, 8, 8, 128), shape(4, 8, 8, 128)),
@@ -459,7 +456,8 @@
         shape(32, 16, 128),
         tuple(sent) + swapped(*sent) + ensembles + (new,),
         scalars,
-        smoothed,
+        smoothed + (pltpu.VMEM((32, 16, 128), F32), pltpu.SemaphoreType.DMA((2,))),
+        out_space=pltpu.HBM,
     )
     return out.reshape(32, 8, 2, 128).transpose(0, 2, 1, 3).reshape(control.shape)
 

time: 92.8 us -> 93.7 us (level)
  waiting for transfers between devices: 24.4 us -> 28.4 us
  Pallas kernels: 11.6 us -> 9.9 us
    ppermute x7, waiting for transfers between devices: 24.4 us -> 28.3 us  [from_far(): return lax.ppermute(x, 'lat', pairs)]
    pallas_call x10 -> x9, Pallas kernels: 11.6 us -> 9.9 us  [call(): pl.pallas_call(kernel, out_shape=outs, in_specs=in_specs, out_specs=jax.t...]
  transfers between devices with their start and end apart: 13 -> 13, of which waited for: 5 -> 5; matrix products, arithmetic and copies ran while one was open for 0% -> 0% of each run, Pallas kernels for 6% -> 3%
where the time goes in v7:
time: 93.7 us; the launch traced here: 92 us
  starting transfers between devices  32.3 us (34%)
  waiting for transfers between devices  28.4 us (30%)
  blocking collectives  21.1 us (23%)
  Pallas kernels  9.9 us (11%)
    ppermute x7, starting transfers between devices, from_far(): return lax.ppermute(x, 'lat', pairs)  31 us
    ppermute x7, waiting for transfers between devices, from_far(): return lax.ppermute(x, 'lat', pairs)  28.3 us
    all_gather x1, blocking collectives, descent(): c0, c1 = call(sum_kernel, (four, four), (lax.all_gather(part, 'mem'),))  11 us
    all_gather x1, blocking collectives, descent(): sent = call(sum_kernel, (eight, eight), (lax.all_gather(part, 'mem'),))  10.1 us
    pallas_call x9, Pallas kernels, call(): pl.pallas_call(kernel, out_shape=outs, in_specs=in_specs, out_specs=jax.t...  9.9 us
  transfers between devices with their start and end apart: 13, of which 5 were waited for; matrix products, arithmetic and copies ran while one was open for 0% of the time, Pallas kernels for 3%

profile of v7, /device:TPU:30, one launch (start us, length us, event | category | flops | bytes accessed | tf_op | source)
XLA Modules:
  0.0 92.0 jit_solution(5586466216527612804)
XLA Ops:
  0.0 0.1 pad_add_fusion.place_ref
  0.1 2.1 %shard_map.82 = (f32[32,8,128]{2,1,0:T(8,128)S(1)}, f32[32,8,128]{2,1,0:T(8,128)S(1)}, f32[2,32,8,128]{3,2,1,0:T(8,128)S(1)}, bf16[2,256,128]{2,1,0:T(8,128)(2,1...) custom-call(s32[2]{0:T(128)S(1)} %pad_add_fusion.place_ref, ...), custom_call_target="tpu_custom_call" | custom-call | flops 1000000 | bytes 1000000 | tf_op jit(solution)/shard_map/pallas_call | solution.py:28
  2.2 0.8 collective-permute-start.8
  3.0 4.2 %collective-permute-start.7 = (f32[96,8,128]{2,1,0:T(8,128)S(1)}, f32[96,8,128]{2,1,0:T(8,128)S(1)}, u32[]{:S(2)}, u32[]{:S(2)}) collective-permute-start(f32[96,8,128]{2,1,0:T(8,128)S(1)} %get-tuple-element.29.refs_1_.refs_3_), channel_id=1, source_target_pairs={{0,0},{1,2},{2,1},{3,4},{4,3},{5,6},{6,5},{7,8},{8,7},{9,10},{10,9... | collective-permute-start | bytes 1179656 | tf_op jit(solution)/shard_map/ppermute | solution.py:378
  7.3 5.8 %collective-permute-start = (f32[32,8,128]{2,1,0:T(8,128)S(1)}, f32[32,8,128]{2,1,0:T(8,128)S(1)}, u32[]{:S(2)}, u32[]{:S(2)}) collective-permute-start(f32[32,8,128]{2,1,0:T(8,128)S(1)} %get-tuple-element.26.w0_ref), channel_id=1, source_target_pairs={{0,0},{1,2},{2,1},{3,4},{4,3},{5,6},{6,5},{7,8},{8,7},{9,10},{10,9... | collective-permute-start | bytes 393224 | tf_op jit(solution)/shard_map/ppermute | solution.py:378
  13.1 0.1 collective-permute-start.1
  13.2 4.2 %collective-permute-start.6 = (f32[32,8,128]{2,1,0:T(8,128)S(1)}, f32[32,8,128]{2,1,0:T(8,128)S(1)}, u32[]{:S(2)}, u32[]{:S(2)}) collective-permute-start(f32[32,8,128]{2,1,0:T(8,128)S(1)} %get-tuple-element.28.refs_0_.refs_2_), channel_id=1, source_target_pairs={{0,0},{1,2},{2,1},{3,4},{4,3},{5,6},{6,5},{7,8},{8,7},{9,10},{10,9... | collective-permute-start | bytes 393224 | tf_op jit(solution)/shard_map/ppermute | solution.py:378
  17.4 6.5 %collective-permute-done.far_ref = f32[32,8,128]{2,1,0:T(8,128)S(1)} collective-permute-done((f32[32,8,128]{2,1,0:T(8,128)S(1)}, f32[32,8,128]{2,1,0:T(8,128)S(1)}, u32[]{:S(2)}, u32[]{:S(2)}) %collective-permute-start) | collective-permute-done | bytes 131104 | tf_op jit(solution)/shard_map/ppermute | solution.py:378
  23.9 0.0 collective-permute-done.1.near_ref
  23.9 0.0 copy-start.2
  23.9 0.0 copy-start.3
  23.9 0.0 copy-start.4
  23.9 0.0 copy-start.5
  24.0 0.0 copy-start.1
  24.0 0.7 shard_map.83
  24.6 0.0 copy-start
  24.7 11.0 %all-gather = f32[32,8,128]{2,1,0:T(8,128)S(1)} all-gather(f32[8,8,128]{2,1,0:T(8,128)S(1)} %shard_map.83), channel_id=2, replica_groups=mesh['mem'=4,'lat'=64] {'mem'}, dimensions={0}, use_global_device_ids=true | all-gather | bytes 163840 | tf_op jit(solution)/shard_map/all_gather | solution.py:433
  35.6 3.2 %collective-permute-start.2 = (f32[4,8,128]{2,1,0:T(8,128)S(1)}, f32[4,8,128]{2,1,0:T(8,128)S(1)}, u32[]{:S(2)}, u32[]{:S(2)}) collective-permute-start(f32[4,8,128]{2,1,0:T(8,128)S(1)} %get-tuple-element.31.c0_ref), channel_id=1, source_target_pairs={{0,0},{1,2},{2,1},{3,4},{4,3},{5,6},{6,5},{7,8},{8,7},{9,10},{10,9... | collective-permute-start | bytes 49160 | tf_op jit(solution)/shard_map/ppermute | solution.py:378
  38.9 0.1 collective-permute-start.3
  39.0 0.0 copy-done.2
  39.0 0.0 copy-done.3
  39.0 0.0 copy-done.4
  39.0 0.0 copy-done.5
  39.0 0.8 shard_map.85
  39.8 5.7 %collective-permute-done.2.far_ref = f32[4,8,128]{2,1,0:T(8,128)S(1)} collective-permute-done((f32[4,8,128]{2,1,0:T(8,128)S(1)}, f32[4,8,128]{2,1,0:T(8,128)S(1)}, u32[]{:S(2)}, u32[]{:S(2)}) %collective-permute-start.2) | collective-permute-done | bytes 16416 | tf_op jit(solution)/shard_map/ppermute | solution.py:378
  45.5 0.0 collective-permute-done.3.near_ref
  45.5 0.0 copy-done.1
  45.5 0.0 copy-done
  45.5 1.5 %shard_map.86 = (f32[8,8,128]{2,1,0:T(8,128)S(1)}, f32[8,8,128]{2,1,0:T(8,128)S(1)}) custom-call(f32[4,8,128]{2,1,0:T(8,128)S(1)} %collective-permute-done.2.far_ref, f32[4,8,128]{2,1,0:T(8,128)S(1)} %get-tuple-element.31.c0_ref, f32[4,8,128]{2,1,0:T(8,128)S(1)} %get-tuple-element.32.c1_ref, f32[4,8,128]{2,1,0:T(8,128)S(1)} %collective-permute-done.3.near_ref, ...), custom_call_target="tpu_custom_call" | custom-call | flops 1000000 | bytes 1000000 | tf_op jit(solution)/shard_map/pallas_call | solution.py:28
  47.0 4.0 %collective-permute-start.4 = (f32[8,8,128]{2,1,0:T(8,128)S(1)}, f32[8,8,128]{2,1,0:T(8,128)S(1)}, u32[]{:S(2)}, u32[]{:S(2)}) collective-permute-start(f32[8,8,128]{2,1,0:T(8,128)S(1)} %get-tuple-element.36.lf_ref), channel_id=1, source_target_pairs={{0,0},{1,2},{2,1},{3,4},{4,3},{5,6},{6,5},{7,8},{8,7},{9,10},{10,9... | collective-permute-start | bytes 98312 | tf_op jit(solution)/shard_map/ppermute | solution.py:378
  51.1 0.1 collective-permute-start.5
  51.2 0.0 collective-permute-done.6.refs_0_
  51.2 5.9 %collective-permute-done.4.rf_ref = f32[8,8,128]{2,1,0:T(8,128)S(1)} collective-permute-done((f32[8,8,128]{2,1,0:T(8,128)S(1)}, f32[8,8,128]{2,1,0:T(8,128)S(1)}, u32[]{:S(2)}, u32[]{:S(2)}) %collective-permute-start.4) | collective-permute-done | bytes 32800 | tf_op jit(solution)/shard_map/ppermute | solution.py:378
  57.1 0.0 collective-permute-done.5.rn_ref
  57.1 0.0 collective-permute-done.7.refs_1_
  57.1 0.0 collective-permute-done.8.refs_5_
  57.1 1.5 %shard_map.87 = (f32[2,32,8,128]{3,2,1,0:T(8,128)S(1)}, f32[16,8,128]{2,1,0:T(8,128)S(1)}) custom-call(s32[2]{0:T(128)S(1)} %pad_add_fusion.place_ref, f32[8,8,128]{2,1,0:T(8,128)S(1)} %get-tuple-element.36.lf_ref, f32[8,8,128]{2,1,0:T(8,128)S(1)} %get-tuple-element.37.ln_ref, f32[8,8,128]{2,1,0:T(8,128)S(1)} %collective-permute-done.4.rf_ref, ...), custom_call_target="tpu_custom_call" | custom-call | flops 1000000 | bytes 1000000 | tf_op jit(solution)/shard_map/pallas_call | solution.py:28
  58.5 10.1 %all-gather.1 = f32[64,8,128]{2,1,0:T(8,128)S(1)} all-gather(f32[16,8,128]{2,1,0:T(8,128)S(1)} %get-tuple-element.41), channel_id=3, replica_groups=mesh['mem'=4,'lat'=64] {'mem'}, dimensions={0}, use_global_device_ids=true | all-gather | bytes 327680 | tf_op jit(solution)/shard_map/all_gather | solution.py:447
  68.7 4.7 %collective-permute-start.9 = (f32[8,8,128]{2,1,0:T(8,128)S(1)}, f32[8,8,128]{2,1,0:T(8,128)S(1)}, u32[]{:S(2)}, u32[]{:S(2)}) collective-permute-start(f32[8,8,128]{2,1,0:T(8,128)S(1)} %get-tuple-element.42.refs_0_), channel_id=1, source_target_pairs={{0,0},{1,2},{2,1},{3,4},{4,3},{5,6},{6,5},{7,8},{8,7},{9,10},{10,9... | collective-permute-start | bytes 98312 | tf_op jit(solution)/shard_map/ppermute | solution.py:378
  73.5 0.1 collective-permute-start.10
  73.6 5.2 %collective-permute-done.9.refs_2_ = f32[8,8,128]{2,1,0:T(8,128)S(1)} collective-permute-done((f32[8,8,128]{2,1,0:T(8,128)S(1)}, f32[8,8,128]{2,1,0:T(8,128)S(1)}, u32[]{:S(2)}, u32[]{:S(2)}) %collective-permute-start.9) | collective-permute-done | bytes 32800 | tf_op jit(solution)/shard_map/ppermute | solution.py:378
  78.7 0.0 collective-permute-done.10.refs_3_
  78.7 1.5 %shard_map.89 = (f32[8,8,128]{2,1,0:T(8,128)S(1)}, f32[8,8,128]{2,1,0:T(8,128)S(1)}) custom-call(f32[8,8,128]{2,1,0:T(8,128)S(1)} %get-tuple-element.42.refs_0_, f32[8,8,128]{2,1,0:T(8,128)S(1)} %get-tuple-element.43.refs_1_, f32[8,8,128]{2,1,0:T(8,128)S(1)} %collective-permute-done.9.refs_2_, f32[8,8,128]{2,1,0:T(8,128)S(1)} %collective-permute-done.10.refs_3_, ...), custom_call_target="tpu_custom_call" | custom-call | flops 1000000 | bytes 1000000 | tf_op jit(solution)/shard_map/pallas_call | solution.py:28
  80.3 4.7 %collective-permute-start.11 = (f32[8,8,128]{2,1,0:T(8,128)S(1)}, f32[8,8,128]{2,1,0:T(8,128)S(1)}, u32[]{:S(2)}, u32[]{:S(2)}) collective-permute-start(f32[8,8,128]{2,1,0:T(8,128)S(1)} %get-tuple-element.44.lf_ref), channel_id=1, source_target_pairs={{0,0},{1,2},{2,1},{3,4},{4,3},{5,6},{6,5},{7,8},{8,7},{9,10},{10,9... | collective-permute-start | bytes 98312 | tf_op jit(solution)/shard_map/ppermute | solution.py:378
  85.0 0.1 collective-permute-start.12
  85.1 5.2 %collective-permute-done.11.rf_ref = f32[8,8,128]{2,1,0:T(8,128)S(1)} collective-permute-done((f32[8,8,128]{2,1,0:T(8,128)S(1)}, f32[8,8,128]{2,1,0:T(8,128)S(1)}, u32[]{:S(2)}, u32[]{:S(2)}) %collective-permute-start.11) | collective-permute-done | bytes 32800 | tf_op jit(solution)/shard_map/ppermute | solution.py:378
  90.3 0.0 collective-permute-done.12.rn_ref
  90.3 1.8 %shard_map.90 = f32[32,16,128]{2,1,0:T(8,128)} custom-call(s32[2]{0:T(128)S(1)} %pad_add_fusion.place_ref, f32[8,8,128]{2,1,0:T(8,128)S(1)} %get-tuple-element.44.lf_ref, f32[8,8,128]{2,1,0:T(8,128)S(1)} %get-tuple-element.45.ln_ref, f32[8,8,128]{2,1,0:T(8,128)S(1)} %collective-permute-done.11.rf_ref, f32[8,8,128]{2,1,0:T(8,128)S(1)} %collective-permute-done.12.rn_ref, ...), custom_call_target="tpu_custom_call" | custom-call | flops 1000000 | bytes 1000000 | tf_op jit(solution)/shard_map/pallas_call | solution.py:28
  (2 shorter events, 0.0 us)
Async XLA Ops:
  2.2 54.9 %collective-permute-start.8 = (f32[128,8,128]{2,1,0:T(8,128)S(1)}, f32[128,8,128]{2,1,0:T(8,128)S(1)}, u32[]{:S(2)}, u32[]{:S(2)}) collective-permute-start(f32[128,8,128]{2,1,0:T(8,128)S(1)} %get-tuple-element.30.refs_2_.refs_4_), channel_id=1, source_target_pairs={{0,1},{1,0},{2,3},{3,2},{4,5},{5,4},{6,7},{7,6},{8,9},{9,8},{10,11... | collective-permute-start | bytes 1572872 | tf_op jit(solution)/shard_map/ppermute | solution.py:382
  3.0 54.0 %collective-permute-start.7 = (f32[96,8,128]{2,1,0:T(8,128)S(1)}, f32[96,8,128]{2,1,0:T(8,128)S(1)}, u32[]{:S(2)}, u32[]{:S(2)}) collective-permute-start(f32[96,8,128]{2,1,0:T(8,128)S(1)} %get-tuple-element.29.refs_1_.refs_3_), channel_id=1, source_target_pairs={{0,0},{1,2},{2,1},{3,4},{4,3},{5,6},{6,5},{7,8},{8,7},{9,10},{10,9... | collective-permute-start | bytes 1179656 | tf_op jit(solution)/shard_map/ppermute | solution.py:378
  7.3 16.7 %collective-permute-start = (f32[32,8,128]{2,1,0:T(8,128)S(1)}, f32[32,8,128]{2,1,0:T(8,128)S(1)}, u32[]{:S(2)}, u32[]{:S(2)}) collective-permute-start(f32[32,8,128]{2,1,0:T(8,128)S(1)} %get-tuple-element.26.w0_ref), channel_id=1, source_target_pairs={{0,0},{1,2},{2,1},{3,4},{4,3},{5,6},{6,5},{7,8},{8,7},{9,10},{10,9... | collective-permute-start | bytes 393224 | tf_op jit(solution)/shard_map/ppermute | solution.py:378
  13.1 10.8 %collective-permute-start.1 = (f32[32,8,128]{2,1,0:T(8,128)S(1)}, f32[32,8,128]{2,1,0:T(8,128)S(1)}, u32[]{:S(2)}, u32[]{:S(2)}) collective-permute-start(f32[32,8,128]{2,1,0:T(8,128)S(1)} %get-tuple-element.27.w1_ref), channel_id=1, source_target_pairs={{0,1},{1,0},{2,3},{3,2},{4,5},{5,4},{6,7},{7,6},{8,9},{9,8},{10,11... | collective-permute-start | bytes 393224 | tf_op jit(solution)/shard_map/ppermute | solution.py:382
  13.2 38.0 %collective-permute-start.6 = (f32[32,8,128]{2,1,0:T(8,128)S(1)}, f32[32,8,128]{2,1,0:T(8,128)S(1)}, u32[]{:S(2)}, u32[]{:S(2)}) collective-permute-start(f32[32,8,128]{2,1,0:T(8,128)S(1)} %get-tuple-element.28.refs_0_.refs_2_), channel_id=1, source_target_pairs={{0,0},{1,2},{2,1},{3,4},{4,3},{5,6},{6,5},{7,8},{8,7},{9,10},{10,9... | collective-permute-start | bytes 393224 | tf_op jit(solution)/shard_map/ppermute | solution.py:378
  23.9 15.1 %copy-start.2 = (s32[4,4,2048]{2,1,0:T(4,128)S(1)}, s32[4,4,2048]{2,1,0:T(4,128)}, u32[]{:S(2)}) copy-start(s32[4,4,2048]{2,1,0:T(4,128)} %param.11) | copy-start | bytes 393220
  23.9 15.1 %copy-start.3 = (f32[4,4,2048]{2,1,0:T(4,128)S(1)}, f32[4,4,2048]{2,1,0:T(4,128)}, u32[]{:S(2)}) copy-start(f32[4,4,2048]{2,1,0:T(4,128)} %param.12) | copy-start | bytes 393220
  23.9 15.1 %copy-start.4 = (s32[4,4,2048]{2,1,0:T(4,128)S(1)}, s32[4,4,2048]{2,1,0:T(4,128)}, u32[]{:S(2)}) copy-start(s32[4,4,2048]{2,1,0:T(4,128)} %param.13) | copy-start | bytes 393220
  23.9 15.1 %copy-start.5 = (f32[4,4,2048]{2,1,0:T(4,128)S(1)}, f32[4,4,2048]{2,1,0:T(4,128)}, u32[]{:S(2)}) copy-start(f32[4,4,2048]{2,1,0:T(4,128)} %param.14) | copy-start | bytes 393220
  24.0 21.5 %copy-start.1 = (bf16[256,1280]{1,0:T(8,128)(2,1)S(1)}, bf16[256,1280]{1,0:T(8,128)(2,1)}, u32[]{:S(2)}) copy-start(bf16[256,1280]{1,0:T(8,128)(2,1)} %constant.22.clone.refs_3_.refs_7_) | copy-start | bytes 1966084
  24.6 20.9 %copy-start = (bf16[1280,256]{1,0:T(8,128)(2,1)S(1)}, bf16[1280,256]{1,0:T(8,128)(2,1)}, u32[]{:S(2)}) copy-start(bf16[1280,256]{1,0:T(8,128)(2,1)} %constant.30.refs_4_.refs_8_) | copy-start | bytes 1966084
  35.6 9.9 %collective-permute-start.2 = (f32[4,8,128]{2,1,0:T(8,128)S(1)}, f32[4,8,128]{2,1,0:T(8,128)S(1)}, u32[]{:S(2)}, u32[]{:S(2)}) collective-permute-start(f32[4,8,128]{2,1,0:T(8,128)S(1)} %get-tuple-element.31.c0_ref), channel_id=1, source_target_pairs={{0,0},{1,2},{2,1},{3,4},{4,3},{5,6},{6,5},{7,8},{8,7},{9,10},{10,9... | collective-permute-start | bytes 49160 | tf_op jit(solution)/shard_map/ppermute | solution.py:378
  38.9 6.6 %collective-permute-start.3 = (f32[4,8,128]{2,1,0:T(8,128)S(1)}, f32[4,8,128]{2,1,0:T(8,128)S(1)}, u32[]{:S(2)}, u32[]{:S(2)}) collective-permute-start(f32[4,8,128]{2,1,0:T(8,128)S(1)} %get-tuple-element.32.c1_ref), channel_id=1, source_target_pairs={{0,1},{1,0},{2,3},{3,2},{4,5},{5,4},{6,7},{7,6},{8,9},{9,8},{10,11... | collective-permute-start | bytes 49160 | tf_op jit(solution)/shard_map/ppermute | solution.py:382
  47.0 10.0 %collective-permute-start.4 = (f32[8,8,128]{2,1,0:T(8,128)S(1)}, f32[8,8,128]{2,1,0:T(8,128)S(1)}, u32[]{:S(2)}, u32[]{:S(2)}) collective-permute-start(f32[8,8,128]{2,1,0:T(8,128)S(1)} %get-tuple-element.36.lf_ref), channel_id=1, source_target_pairs={{0,0},{1,2},{2,1},{3,4},{4,3},{5,6},{6,5},{7,8},{8,7},{9,10},{10,9... | collective-permute-start | bytes 98312 | tf_op jit(solution)/shard_map/ppermute | solution.py:378
  51.1 6.0 %collective-permute-start.5 = (f32[8,8,128]{2,1,0:T(8,128)S(1)}, f32[8,8,128]{2,1,0:T(8,128)S(1)}, u32[]{:S(2)}, u32[]{:S(2)}) collective-permute-start(f32[8,8,128]{2,1,0:T(8,128)S(1)} %get-tuple-element.37.ln_ref), channel_id=1, source_target_pairs={{0,1},{1,0},{2,3},{3,2},{4,5},{5,4},{6,7},{7,6},{8,9},{9,8},{10,11... | collective-permute-start | bytes 98312 | tf_op jit(solution)/shard_map/ppermute | solution.py:382
  68.7 10.0 %collective-permute-start.9 = (f32[8,8,128]{2,1,0:T(8,128)S(1)}, f32[8,8,128]{2,1,0:T(8,128)S(1)}, u32[]{:S(2)}, u32[]{:S(2)}) collective-permute-start(f32[8,8,128]{2,1,0:T(8,128)S(1)} %get-tuple-element.42.refs_0_), channel_id=1, source_target_pairs={{0,0},{1,2},{2,1},{3,4},{4,3},{5,6},{6,5},{7,8},{8,7},{9,10},{10,9... | collective-permute-start | bytes 98312 | tf_op jit(solution)/shard_map/ppermute | solution.py:378
  73.5 5.3 %collective-permute-start.10 = (f32[8,8,128]{2,1,0:T(8,128)S(1)}, f32[8,8,128]{2,1,0:T(8,128)S(1)}, u32[]{:S(2)}, u32[]{:S(2)}) collective-permute-start(f32[8,8,128]{2,1,0:T(8,128)S(1)} %get-tuple-element.43.refs_1_), channel_id=1, source_target_pairs={{0,1},{1,0},{2,3},{3,2},{4,5},{5,4},{6,7},{7,6},{8,9},{9,8},{10,11... | collective-permute-start | bytes 98312 | tf_op jit(solution)/shard_map/ppermute | solution.py:382
  80.3 10.0 %collective-permute-start.11 = (f32[8,8,128]{2,1,0:T(8,128)S(1)}, f32[8,8,128]{2,1,0:T(8,128)S(1)}, u32[]{:S(2)}, u32[]{:S(2)}) collective-permute-start(f32[8,8,128]{2,1,0:T(8,128)S(1)} %get-tuple-element.44.lf_ref), channel_id=1, source_target_pairs={{0,0},{1,2},{2,1},{3,4},{4,3},{5,6},{6,5},{7,8},{8,7},{9,10},{10,9... | collective-permute-start | bytes 98312 | tf_op jit(solution)/shard_map/ppermute | solution.py:378
  85.0 5.3 %collective-permute-start.12 = (f32[8,8,128]{2,1,0:T(8,128)S(1)}, f32[8,8,128]{2,1,0:T(8,128)S(1)}, u32[]{:S(2)}, u32[]{:S(2)}) collective-permute-start(f32[8,8,128]{2,1,0:T(8,128)S(1)} %get-tuple-element.45.ln_ref), channel_id=1, source_target_pairs={{0,1},{1,0},{2,3},{3,2},{4,5},{5,4},{6,7},{7,6},{8,9},{9,8},{10,11... | collective-permute-start | bytes 98312 | tf_op jit(solution)/shard_map/ppermute | solution.py:382

commit v8 on v7

--- a/solution.py
+++ b/solution.py
@@ -187,14 +187,11 @@
         part_ref[n] = sums[n]
 
 
-def sum_kernel(parts_ref, a_ref, b_ref):
+def sum_kernel(mine_ref, theirs_ref, a_ref, b_ref):
     count = a_ref.shape[0]
-    for n in range(2 * count):
-        total = (parts_ref[0, n] + parts_ref[1, n]) + (parts_ref[2, n] + parts_ref[3, n])
-        if n < count:
-            a_ref[n] = total
-        else:
-            b_ref[n - count] = total
+    for n in range(count):
+        a_ref[n] = mine_ref[n] + theirs_ref[n]
+        b_ref[n] = mine_ref[count + n] + theirs_ref[count + n]
 
 
 def stencil(a, b):
@@ -382,6 +379,14 @@
     return lax.ppermute(x, "lat", [(i, i ^ 1) for i in range(lax.axis_size("lat"))])
 
 
+def member_sum(part):
+    groups = lax.axis_size("mem")
+    pair = part + lax.ppermute(part, "mem", [(i, i ^ 1) for i in range(groups)])
+    other = lax.ppermute(pair, "mem", [(i, (i + groups // 2) % groups) for i in range(groups)])
+    half = shape(part.shape[0] // 2, 8, 128)
+    return call(sum_kernel, (half, half), (pair, other))
+
+
 def swapped(far, near):
     return from_far(far), from_near(near)
 
@@ -429,8 +434,8 @@
     part = call(
         first_kernel, shape(8, 8, 128), (w0, w1, far, near, e0, e0_late, e1), scalars
     )
-    four, eight = shape(4, 8, 128), shape(8, 8, 128)
-    c0, c1 = call(sum_kernel, (four, four), (lax.all_gather(part, "mem"),))
+    eight = shape(8, 8, 128)
+    c0, c1 = member_sum(part)
     far, near = swapped(c0, c1)
     refined = (pltpu.VMEM((128, 1280), F32),)
     sent = call(
@@ -444,7 +449,7 @@
         scalars,
         smoothed * 2,
     )
-    sent = call(sum_kernel, (eight, eight), (lax.all_gather(part, "mem"),))
+    sent = member_sum(part)
     sent = call(
         second_observe_kernel,
         (eight, eight),

time: 93.7 us -> 92.9 us (level)
  blocking collectives: 21.1 us -> 0 us
  starting transfers between devices: 32.3 us -> 43.8 us
  waiting for transfers between devices: 28.4 us -> 37.6 us
    all_gather x2 -> x0, blocking collectives: 21.1 us -> none  [the longest x1 11 us: descent(): c0, c1 = call(sum_kernel, (four, four), (lax.all_gather(part, 'mem'),))]
    ppermute x0 -> x4, starting transfers between devices: none -> 13.4 us  [the longest x2 13.2 us: member_sum(): lax.ppermute(pair, 'mem', [(i, (i + groups // 2) % groups) for i in range...]
    ppermute x0 -> x4, waiting for transfers between devices: none -> 7.34 us  [the longest x2 4.91 us: member_sum(): lax.ppermute(pair, 'mem', [(i, (i + groups // 2) % groups) for i in range...]
    ppermute x7, starting transfers between devices: 31 us -> 29.1 us  [from_far(): return lax.ppermute(x, 'lat', pairs)]
    ppermute x7, waiting for transfers between devices: 28.3 us -> 30.3 us  [from_far(): return lax.ppermute(x, 'lat', pairs)]
  transfers between devices with their start and end apart: 13 -> 17, of which waited for: 5 -> 9; matrix products, arithmetic and copies ran while one was open for 0% -> 0% of each run, Pallas kernels for 3% -> 3%
where the time goes in v8:
time: 92.9 us; the launch traced here: 91.7 us
  starting transfers between devices  43.8 us (47%)
  waiting for transfers between devices  37.6 us (40%)
  Pallas kernels  9.9 us (11%)
    ppermute x7, waiting for transfers between devices, from_far(): return lax.ppermute(x, 'lat', pairs)  30.3 us
    ppermute x7, starting transfers between devices, from_far(): return lax.ppermute(x, 'lat', pairs)  29.1 us
    ppermute x2, starting transfers between devices, member_sum(): lax.ppermute(pair, 'mem', [(i, (i + groups // 2) % groups) for i in range...  13.2 us
    pallas_call x9, Pallas kernels, call(): pl.pallas_call(kernel, out_shape=outs, in_specs=in_specs, out_specs=jax.t...  9.9 us
    ppermute x2, waiting for transfers between devices, member_sum(): lax.ppermute(pair, 'mem', [(i, (i + groups // 2) % groups) for i in range...  4.91 us
    ppermute x2, waiting for transfers between devices, member_sum(): pair = part + lax.ppermute(part, 'mem', [(i, i ^ 1) for i in range(groups)])  2.44 us
  transfers between devices with their start and end apart: 17, of which 9 were waited for; matrix products, arithmetic and copies ran while one was open for 0% of the time, Pallas kernels for 3%

profile of v8, /device:TPU:30, one launch (start us, length us, event | category | flops | bytes accessed | tf_op | source)
XLA Modules:
  0.0 91.7 jit_solution(8921285060553398829)
XLA Ops:
  0.0 0.1 pad_add_fusion.place_ref
  0.1 2.1 %shard_map.82 = (f32[32,8,128]{2,1,0:T(8,128)S(1)}, f32[32,8,128]{2,1,0:T(8,128)S(1)}, f32[2,32,8,128]{3,2,1,0:T(8,128)S(1)}, bf16[2,256,128]{2,1,0:T(8,128)(2,1...) custom-call(s32[2]{0:T(128)S(1)} %pad_add_fusion.place_ref, ...), custom_call_target="tpu_custom_call" | custom-call | flops 1000000 | bytes 1000000 | tf_op jit(solution)/shard_map/pallas_call | solution.py:28
  2.2 0.8 collective-permute-start.10
  3.0 4.2 %collective-permute-start.9 = (f32[96,8,128]{2,1,0:T(8,128)S(1)}, f32[96,8,128]{2,1,0:T(8,128)S(1)}, u32[]{:S(2)}, u32[]{:S(2)}) collective-permute-start(f32[96,8,128]{2,1,0:T(8,128)S(1)} %get-tuple-element.29.refs_1_.refs_3_), channel_id=1, source_target_pairs={{0,0},{1,2},{2,1},{3,4},{4,3},{5,6},{6,5},{7,8},{8,7},{9,10},{10,9... | collective-permute-start | bytes 1179656 | tf_op jit(solution)/shard_map/ppermute | solution.py:375
  7.3 5.8 %collective-permute-start = (f32[32,8,128]{2,1,0:T(8,128)S(1)}, f32[32,8,128]{2,1,0:T(8,128)S(1)}, u32[]{:S(2)}, u32[]{:S(2)}) collective-permute-start(f32[32,8,128]{2,1,0:T(8,128)S(1)} %get-tuple-element.26.w0_ref), channel_id=1, source_target_pairs={{0,0},{1,2},{2,1},{3,4},{4,3},{5,6},{6,5},{7,8},{8,7},{9,10},{10,9... | collective-permute-start | bytes 393224 | tf_op jit(solution)/shard_map/ppermute | solution.py:375
  13.1 0.1 collective-permute-start.1
  13.2 4.2 %collective-permute-start.8 = (f32[32,8,128]{2,1,0:T(8,128)S(1)}, f32[32,8,128]{2,1,0:T(8,128)S(1)}, u32[]{:S(2)}, u32[]{:S(2)}) collective-permute-start(f32[32,8,128]{2,1,0:T(8,128)S(1)} %get-tuple-element.28.refs_0_.refs_2_), channel_id=1, source_target_pairs={{0,0},{1,2},{2,1},{3,4},{4,3},{5,6},{6,5},{7,8},{8,7},{9,10},{10,9... | collective-permute-start | bytes 393224 | tf_op jit(solution)/shard_map/ppermute | solution.py:375
  17.4 6.5 %collective-permute-done.far_ref = f32[32,8,128]{2,1,0:T(8,128)S(1)} collective-permute-done((f32[32,8,128]{2,1,0:T(8,128)S(1)}, f32[32,8,128]{2,1,0:T(8,128)S(1)}, u32[]{:S(2)}, u32[]{:S(2)}) %collective-permute-start) | collective-permute-done | bytes 131104 | tf_op jit(solution)/shard_map/ppermute | solution.py:375
  23.9 0.0 collective-permute-done.1.near_ref
  23.9 0.0 copy-start.5
  24.0 0.0 copy-start.1
  24.0 0.7 shard_map.83
  24.6 0.0 copy-start
  24.7 0.1 collective-permute-start.2
  24.8 1.2 %collective-permute-done.2 = f32[8,8,128]{2,1,0:T(8,128)S(1)} collective-permute-done((f32[8,8,128]{2,1,0:T(8,128)S(1)}, f32[8,8,128]{2,1,0:T(8,128)S(1)}, u32[]{:S(2)}, u32[]{:S(2)}) %collective-permute-start.2) | collective-permute-done | bytes 32800 | tf_op jit(solution)/shard_map/ppermute | solution.py:384
  26.0 7.2 %collective-permute-start.3 = (f32[8,8,128]{2,1,0:T(8,128)S(1)}, f32[8,8,128]{2,1,0:T(8,128)S(1)}, u32[]{:S(2)}, u32[]{:S(2)}) collective-permute-start(f32[8,8,128]{2,1,0:T(8,128)S(1)} %add.11.mine_ref), channel_id=1, source_target_pairs={{0,128},{64,192},{128,0},{192,64},{1,129},{65,193},{129,1},{193,65... | collective-permute-start | bytes 98312 | tf_op jit(solution)/shard_map/ppermute | solution.py:385
  33.2 1.9 %collective-permute-done.3.theirs_ref = f32[8,8,128]{2,1,0:T(8,128)S(1)} collective-permute-done((f32[8,8,128]{2,1,0:T(8,128)S(1)}, f32[8,8,128]{2,1,0:T(8,128)S(1)}, u32[]{:S(2)}, u32[]{:S(2)}) %collective-permute-start.3) | collective-permute-done | bytes 32800 | tf_op jit(solution)/shard_map/ppermute | solution.py:385
  35.1 3.3 %collective-permute-start.4 = (f32[4,8,128]{2,1,0:T(8,128)S(1)}, f32[4,8,128]{2,1,0:T(8,128)S(1)}, u32[]{:S(2)}, u32[]{:S(2)}) collective-permute-start(f32[4,8,128]{2,1,0:T(8,128)S(1)} %get-tuple-element.31.c0_ref), channel_id=1, source_target_pairs={{0,0},{1,2},{2,1},{3,4},{4,3},{5,6},{6,5},{7,8},{8,7},{9,10},{10,9... | collective-permute-start | bytes 49160 | tf_op jit(solution)/shard_map/ppermute | solution.py:375
  38.4 0.1 collective-permute-start.5
  38.5 0.0 copy-done.2
  38.5 0.0 copy-done.3
  38.5 0.8 shard_map.85
  39.3 5.6 %collective-permute-done.4.far_ref = f32[4,8,128]{2,1,0:T(8,128)S(1)} collective-permute-done((f32[4,8,128]{2,1,0:T(8,128)S(1)}, f32[4,8,128]{2,1,0:T(8,128)S(1)}, u32[]{:S(2)}, u32[]{:S(2)}) %collective-permute-start.4) | collective-permute-done | bytes 16416 | tf_op jit(solution)/shard_map/ppermute | solution.py:375
  44.9 0.0 collective-permute-done.5.near_ref
  44.9 0.0 copy-done
  44.9 1.5 %shard_map.86 = (f32[8,8,128]{2,1,0:T(8,128)S(1)}, f32[8,8,128]{2,1,0:T(8,128)S(1)}) custom-call(f32[4,8,128]{2,1,0:T(8,128)S(1)} %collective-permute-done.4.far_ref, f32[4,8,128]{2,1,0:T(8,128)S(1)} %get-tuple-element.31.c0_ref, f32[4,8,128]{2,1,0:T(8,128)S(1)} %get-tuple-element.32.c1_ref, f32[4,8,128]{2,1,0:T(8,128)S(1)} %collective-permute-done.5.near_ref, ...), custom_call_target="tpu_custom_call" | custom-call | flops 1000000 | bytes 1000000 | tf_op jit(solution)/shard_map/pallas_call | solution.py:28
  46.4 4.0 %collective-permute-start.6 = (f32[8,8,128]{2,1,0:T(8,128)S(1)}, f32[8,8,128]{2,1,0:T(8,128)S(1)}, u32[]{:S(2)}, u32[]{:S(2)}) collective-permute-start(f32[8,8,128]{2,1,0:T(8,128)S(1)} %get-tuple-element.36.lf_ref), channel_id=1, source_target_pairs={{0,0},{1,2},{2,1},{3,4},{4,3},{5,6},{6,5},{7,8},{8,7},{9,10},{10,9... | collective-permute-start | bytes 98312 | tf_op jit(solution)/shard_map/ppermute | solution.py:375
  50.5 0.1 collective-permute-start.7
  50.6 0.0 collective-permute-done.8.refs_0_
  50.6 5.9 %collective-permute-done.6.rf_ref = f32[8,8,128]{2,1,0:T(8,128)S(1)} collective-permute-done((f32[8,8,128]{2,1,0:T(8,128)S(1)}, f32[8,8,128]{2,1,0:T(8,128)S(1)}, u32[]{:S(2)}, u32[]{:S(2)}) %collective-permute-start.6) | collective-permute-done | bytes 32800 | tf_op jit(solution)/shard_map/ppermute | solution.py:375
  56.5 0.0 collective-permute-done.7.rn_ref
  56.5 0.0 collective-permute-done.9.refs_1_
  56.5 0.0 collective-permute-done.10.refs_5_
  56.5 1.5 %shard_map.87 = (f32[2,32,8,128]{3,2,1,0:T(8,128)S(1)}, f32[16,8,128]{2,1,0:T(8,128)S(1)}) custom-call(s32[2]{0:T(128)S(1)} %pad_add_fusion.place_ref, f32[8,8,128]{2,1,0:T(8,128)S(1)} %get-tuple-element.36.lf_ref, f32[8,8,128]{2,1,0:T(8,128)S(1)} %get-tuple-element.37.ln_ref, f32[8,8,128]{2,1,0:T(8,128)S(1)} %collective-permute-done.6.rf_ref, ...), custom_call_target="tpu_custom_call" | custom-call | flops 1000000 | bytes 1000000 | tf_op jit(solution)/shard_map/pallas_call | solution.py:28
  58.0 0.1 collective-permute-start.11
  58.1 1.2 %collective-permute-done.11 = f32[16,8,128]{2,1,0:T(8,128)S(1)} collective-permute-done((f32[16,8,128]{2,1,0:T(8,128)S(1)}, f32[16,8,128]{2,1,0:T(8,128)S(1)}, u32[]{:S(2)}, u32[]{:S(2)}) %collective-permute-start.11) | collective-permute-done | bytes 65568 | tf_op jit(solution)/shard_map/ppermute | solution.py:384
  59.3 6.0 %collective-permute-start.12 = (f32[16,8,128]{2,1,0:T(8,128)S(1)}, f32[16,8,128]{2,1,0:T(8,128)S(1)}, u32[]{:S(2)}, u32[]{:S(2)}) collective-permute-start(f32[16,8,128]{2,1,0:T(8,128)S(1)} %add.12.mine_ref), channel_id=1, source_target_pairs={{0,128},{64,192},{128,0},{192,64},{1,129},{65,193},{129,1},{193,65... | collective-permute-start | bytes 196616 | tf_op jit(solution)/shard_map/ppermute | solution.py:385
  65.3 3.0 %collective-permute-done.12.theirs_ref = f32[16,8,128]{2,1,0:T(8,128)S(1)} collective-permute-done((f32[16,8,128]{2,1,0:T(8,128)S(1)}, f32[16,8,128]{2,1,0:T(8,128)S(1)}, u32[]{:S(2)}, u32[]{:S(2)}) %collective-permute-start.12) | collective-permute-done | bytes 65568 | tf_op jit(solution)/shard_map/ppermute | solution.py:385
  68.3 3.4 %collective-permute-start.13 = (f32[8,8,128]{2,1,0:T(8,128)S(1)}, f32[8,8,128]{2,1,0:T(8,128)S(1)}, u32[]{:S(2)}, u32[]{:S(2)}) collective-permute-start(f32[8,8,128]{2,1,0:T(8,128)S(1)} %get-tuple-element.42.refs_0_), channel_id=1, source_target_pairs={{0,0},{1,2},{2,1},{3,4},{4,3},{5,6},{6,5},{7,8},{8,7},{9,10},{10,9... | collective-permute-start | bytes 98312 | tf_op jit(solution)/shard_map/ppermute | solution.py:375
  71.8 0.1 collective-permute-start.14
  71.9 6.5 %collective-permute-done.13.refs_2_ = f32[8,8,128]{2,1,0:T(8,128)S(1)} collective-permute-done((f32[8,8,128]{2,1,0:T(8,128)S(1)}, f32[8,8,128]{2,1,0:T(8,128)S(1)}, u32[]{:S(2)}, u32[]{:S(2)}) %collective-permute-start.13) | collective-permute-done | bytes 32800 | tf_op jit(solution)/shard_map/ppermute | solution.py:375
  78.4 0.0 collective-permute-done.14.refs_3_
  78.4 1.5 %shard_map.89 = (f32[8,8,128]{2,1,0:T(8,128)S(1)}, f32[8,8,128]{2,1,0:T(8,128)S(1)}) custom-call(f32[8,8,128]{2,1,0:T(8,128)S(1)} %get-tuple-element.42.refs_0_, f32[8,8,128]{2,1,0:T(8,128)S(1)} %get-tuple-element.43.refs_1_, f32[8,8,128]{2,1,0:T(8,128)S(1)} %collective-permute-done.13.refs_2_, f32[8,8,128]{2,1,0:T(8,128)S(1)} %collective-permute-done.14.refs_3_, ...), custom_call_target="tpu_custom_call" | custom-call | flops 1000000 | bytes 1000000 | tf_op jit(solution)/shard_map/pallas_call | solution.py:28
  79.9 4.0 %collective-permute-start.15 = (f32[8,8,128]{2,1,0:T(8,128)S(1)}, f32[8,8,128]{2,1,0:T(8,128)S(1)}, u32[]{:S(2)}, u32[]{:S(2)}) collective-permute-start(f32[8,8,128]{2,1,0:T(8,128)S(1)} %get-tuple-element.44.lf_ref), channel_id=1, source_target_pairs={{0,0},{1,2},{2,1},{3,4},{4,3},{5,6},{6,5},{7,8},{8,7},{9,10},{10,9... | collective-permute-start | bytes 98312 | tf_op jit(solution)/shard_map/ppermute | solution.py:375
  83.9 0.1 collective-permute-start.16
  84.0 5.9 %collective-permute-done.15.rf_ref = f32[8,8,128]{2,1,0:T(8,128)S(1)} collective-permute-done((f32[8,8,128]{2,1,0:T(8,128)S(1)}, f32[8,8,128]{2,1,0:T(8,128)S(1)}, u32[]{:S(2)}, u32[]{:S(2)}) %collective-permute-start.15) | collective-permute-done | bytes 32800 | tf_op jit(solution)/shard_map/ppermute | solution.py:375
  89.9 0.0 collective-permute-done.16.rn_ref
  89.9 1.8 %shard_map.90 = f32[32,16,128]{2,1,0:T(8,128)} custom-call(s32[2]{0:T(128)S(1)} %pad_add_fusion.place_ref, f32[8,8,128]{2,1,0:T(8,128)S(1)} %get-tuple-element.44.lf_ref, f32[8,8,128]{2,1,0:T(8,128)S(1)} %get-tuple-element.45.ln_ref, f32[8,8,128]{2,1,0:T(8,128)S(1)} %collective-permute-done.15.rf_ref, f32[8,8,128]{2,1,0:T(8,128)S(1)} %collective-permute-done.16.rn_ref, ...), custom_call_target="tpu_custom_call" | custom-call | flops 1000000 | bytes 1000000 | tf_op jit(solution)/shard_map/pallas_call | solution.py:28
  (10 shorter events, 0.0 us)
Async XLA Ops:
  2.2 54.3 %collective-permute-start.10 = (f32[128,8,128]{2,1,0:T(8,128)S(1)}, f32[128,8,128]{2,1,0:T(8,128)S(1)}, u32[]{:S(2)}, u32[]{:S(2)}) collective-permute-start(f32[128,8,128]{2,1,0:T(8,128)S(1)} %get-tuple-element.30.refs_2_.refs_4_), channel_id=1, source_target_pairs={{0,1},{1,0},{2,3},{3,2},{4,5},{5,4},{6,7},{7,6},{8,9},{9,8},{10,11... | collective-permute-start | bytes 1572872 | tf_op jit(solution)/shard_map/ppermute | solution.py:379
  3.0 53.4 %collective-permute-start.9 = (f32[96,8,128]{2,1,0:T(8,128)S(1)}, f32[96,8,128]{2,1,0:T(8,128)S(1)}, u32[]{:S(2)}, u32[]{:S(2)}) collective-permute-start(f32[96,8,128]{2,1,0:T(8,128)S(1)} %get-tuple-element.29.refs_1_.refs_3_), channel_id=1, source_target_pairs={{0,0},{1,2},{2,1},{3,4},{4,3},{5,6},{6,5},{7,8},{8,7},{9,10},{10,9... | collective-permute-start | bytes 1179656 | tf_op jit(solution)/shard_map/ppermute | solution.py:375
  7.3 16.7 %collective-permute-start = (f32[32,8,128]{2,1,0:T(8,128)S(1)}, f32[32,8,128]{2,1,0:T(8,128)S(1)}, u32[]{:S(2)}, u32[]{:S(2)}) collective-permute-start(f32[32,8,128]{2,1,0:T(8,128)S(1)} %get-tuple-element.26.w0_ref), channel_id=1, source_target_pairs={{0,0},{1,2},{2,1},{3,4},{4,3},{5,6},{6,5},{7,8},{8,7},{9,10},{10,9... | collective-permute-start | bytes 393224 | tf_op jit(solution)/shard_map/ppermute | solution.py:375
  13.1 10.8 %collective-permute-start.1 = (f32[32,8,128]{2,1,0:T(8,128)S(1)}, f32[32,8,128]{2,1,0:T(8,128)S(1)}, u32[]{:S(2)}, u32[]{:S(2)}) collective-permute-start(f32[32,8,128]{2,1,0:T(8,128)S(1)} %get-tuple-element.27.w1_ref), channel_id=1, source_target_pairs={{0,1},{1,0},{2,3},{3,2},{4,5},{5,4},{6,7},{7,6},{8,9},{9,8},{10,11... | collective-permute-start | bytes 393224 | tf_op jit(solution)/shard_map/ppermute | solution.py:379
  13.2 37.4 %collective-permute-start.8 = (f32[32,8,128]{2,1,0:T(8,128)S(1)}, f32[32,8,128]{2,1,0:T(8,128)S(1)}, u32[]{:S(2)}, u32[]{:S(2)}) collective-permute-start(f32[32,8,128]{2,1,0:T(8,128)S(1)} %get-tuple-element.28.refs_0_.refs_2_), channel_id=1, source_target_pairs={{0,0},{1,2},{2,1},{3,4},{4,3},{5,6},{6,5},{7,8},{8,7},{9,10},{10,9... | collective-permute-start | bytes 393224 | tf_op jit(solution)/shard_map/ppermute | solution.py:375
  23.9 14.6 %copy-start.2 = (s32[4,4,2048]{2,1,0:T(4,128)S(1)}, s32[4,4,2048]{2,1,0:T(4,128)}, u32[]{:S(2)}) copy-start(s32[4,4,2048]{2,1,0:T(4,128)} %param.11) | copy-start | bytes 393220
  23.9 14.6 %copy-start.3 = (f32[4,4,2048]{2,1,0:T(4,128)S(1)}, f32[4,4,2048]{2,1,0:T(4,128)}, u32[]{:S(2)}) copy-start(f32[4,4,2048]{2,1,0:T(4,128)} %param.12) | copy-start | bytes 393220
  23.9 14.6 %copy-start.4 = (s32[4,4,2048]{2,1,0:T(4,128)S(1)}, s32[4,4,2048]{2,1,0:T(4,128)}, u32[]{:S(2)}) copy-start(s32[4,4,2048]{2,1,0:T(4,128)} %param.13) | copy-start | bytes 393220
  23.9 14.6 %copy-start.5 = (f32[4,4,2048]{2,1,0:T(4,128)S(1)}, f32[4,4,2048]{2,1,0:T(4,128)}, u32[]{:S(2)}) copy-start(f32[4,4,2048]{2,1,0:T(4,128)} %param.14) | copy-start | bytes 393220
  24.0 21.0 %copy-start.1 = (bf16[256,1280]{1,0:T(8,128)(2,1)S(1)}, bf16[256,1280]{1,0:T(8,128)(2,1)}, u32[]{:S(2)}) copy-start(bf16[256,1280]{1,0:T(8,128)(2,1)} %constant.22.clone.refs_3_.refs_7_) | copy-start | bytes 1966084
  24.6 20.3 %copy-start = (bf16[1280,256]{1,0:T(8,128)(2,1)S(1)}, bf16[1280,256]{1,0:T(8,128)(2,1)}, u32[]{:S(2)}) copy-start(bf16[1280,256]{1,0:T(8,128)(2,1)} %constant.30.refs_4_.refs_8_) | copy-start | bytes 1966084
  24.7 1.3 %collective-permute-start.2 = (f32[8,8,128]{2,1,0:T(8,128)S(1)}, f32[8,8,128]{2,1,0:T(8,128)S(1)}, u32[]{:S(2)}, u32[]{:S(2)}) collective-permute-start(f32[8,8,128]{2,1,0:T(8,128)S(1)} %shard_map.83), channel_id=1, source_target_pairs={{0,64},{64,0},{128,192},{192,128},{1,65},{65,1},{129,193},{193,129... | collective-permute-start | bytes 98312 | tf_op jit(solution)/shard_map/ppermute | solution.py:384
  26.0 9.1 %collective-permute-start.3 = (f32[8,8,128]{2,1,0:T(8,128)S(1)}, f32[8,8,128]{2,1,0:T(8,128)S(1)}, u32[]{:S(2)}, u32[]{:S(2)}) collective-permute-start(f32[8,8,128]{2,1,0:T(8,128)S(1)} %add.11.mine_ref), channel_id=1, source_target_pairs={{0,128},{64,192},{128,0},{192,64},{1,129},{65,193},{129,1},{193,65... | collective-permute-start | bytes 98312 | tf_op jit(solution)/shard_map/ppermute | solution.py:385
  35.1 9.8 %collective-permute-start.4 = (f32[4,8,128]{2,1,0:T(8,128)S(1)}, f32[4,8,128]{2,1,0:T(8,128)S(1)}, u32[]{:S(2)}, u32[]{:S(2)}) collective-permute-start(f32[4,8,128]{2,1,0:T(8,128)S(1)} %get-tuple-element.31.c0_ref), channel_id=1, source_target_pairs={{0,0},{1,2},{2,1},{3,4},{4,3},{5,6},{6,5},{7,8},{8,7},{9,10},{10,9... | collective-permute-start | bytes 49160 | tf_op jit(solution)/shard_map/ppermute | solution.py:375
  38.4 6.5 %collective-permute-start.5 = (f32[4,8,128]{2,1,0:T(8,128)S(1)}, f32[4,8,128]{2,1,0:T(8,128)S(1)}, u32[]{:S(2)}, u32[]{:S(2)}) collective-permute-start(f32[4,8,128]{2,1,0:T(8,128)S(1)} %get-tuple-element.32.c1_ref), channel_id=1, source_target_pairs={{0,1},{1,0},{2,3},{3,2},{4,5},{5,4},{6,7},{7,6},{8,9},{9,8},{10,11... | collective-permute-start | bytes 49160 | tf_op jit(solution)/shard_map/ppermute | solution.py:379
  46.4 10.0 %collective-permute-start.6 = (f32[8,8,128]{2,1,0:T(8,128)S(1)}, f32[8,8,128]{2,1,0:T(8,128)S(1)}, u32[]{:S(2)}, u32[]{:S(2)}) collective-permute-start(f32[8,8,128]{2,1,0:T(8,128)S(1)} %get-tuple-element.36.lf_ref), channel_id=1, source_target_pairs={{0,0},{1,2},{2,1},{3,4},{4,3},{5,6},{6,5},{7,8},{8,7},{9,10},{10,9... | collective-permute-start | bytes 98312 | tf_op jit(solution)/shard_map/ppermute | solution.py:375
  50.5 6.0 %collective-permute-start.7 = (f32[8,8,128]{2,1,0:T(8,128)S(1)}, f32[8,8,128]{2,1,0:T(8,128)S(1)}, u32[]{:S(2)}, u32[]{:S(2)}) collective-permute-start(f32[8,8,128]{2,1,0:T(8,128)S(1)} %get-tuple-element.37.ln_ref), channel_id=1, source_target_pairs={{0,1},{1,0},{2,3},{3,2},{4,5},{5,4},{6,7},{7,6},{8,9},{9,8},{10,11... | collective-permute-start | bytes 98312 | tf_op jit(solution)/shard_map/ppermute | solution.py:379
  58.0 1.3 %collective-permute-start.11 = (f32[16,8,128]{2,1,0:T(8,128)S(1)}, f32[16,8,128]{2,1,0:T(8,128)S(1)}, u32[]{:S(2)}, u32[]{:S(2)}) collective-permute-start(f32[16,8,128]{2,1,0:T(8,128)S(1)} %get-tuple-element.41), channel_id=1, source_target_pairs={{0,64},{64,0},{128,192},{192,128},{1,65},{65,1},{129,193},{193,129... | collective-permute-start | bytes 196616 | tf_op jit(solution)/shard_map/ppermute | solution.py:384
  59.3 9.0 %collective-permute-start.12 = (f32[16,8,128]{2,1,0:T(8,128)S(1)}, f32[16,8,128]{2,1,0:T(8,128)S(1)}, u32[]{:S(2)}, u32[]{:S(2)}) collective-permute-start(f32[16,8,128]{2,1,0:T(8,128)S(1)} %add.12.mine_ref), channel_id=1, source_target_pairs={{0,128},{64,192},{128,0},{192,64},{1,129},{65,193},{129,1},{193,65... | collective-permute-start | bytes 196616 | tf_op jit(solution)/shard_map/ppermute | solution.py:385
  68.3 10.0 %collective-permute-start.13 = (f32[8,8,128]{2,1,0:T(8,128)S(1)}, f32[8,8,128]{2,1,0:T(8,128)S(1)}, u32[]{:S(2)}, u32[]{:S(2)}) collective-permute-start(f32[8,8,128]{2,1,0:T(8,128)S(1)} %get-tuple-element.42.refs_0_), channel_id=1, source_target_pairs={{0,0},{1,2},{2,1},{3,4},{4,3},{5,6},{6,5},{7,8},{8,7},{9,10},{10,9... | collective-permute-start | bytes 98312 | tf_op jit(solution)/shard_map/ppermute | solution.py:375
  71.8 6.6 %collective-permute-start.14 = (f32[8,8,128]{2,1,0:T(8,128)S(1)}, f32[8,8,128]{2,1,0:T(8,128)S(1)}, u32[]{:S(2)}, u32[]{:S(2)}) collective-permute-start(f32[8,8,128]{2,1,0:T(8,128)S(1)} %get-tuple-element.43.refs_1_), channel_id=1, source_target_pairs={{0,1},{1,0},{2,3},{3,2},{4,5},{5,4},{6,7},{7,6},{8,9},{9,8},{10,11... | collective-permute-start | bytes 98312 | tf_op jit(solution)/shard_map/ppermute | solution.py:379
  79.9 10.0 %collective-permute-start.15 = (f32[8,8,128]{2,1,0:T(8,128)S(1)}, f32[8,8,128]{2,1,0:T(8,128)S(1)}, u32[]{:S(2)}, u32[]{:S(2)}) collective-permute-start(f32[8,8,128]{2,1,0:T(8,128)S(1)} %get-tuple-element.44.lf_ref), channel_id=1, source_target_pairs={{0,0},{1,2},{2,1},{3,4},{4,3},{5,6},{6,5},{7,8},{8,7},{9,10},{10,9... | collective-permute-start | bytes 98312 | tf_op jit(solution)/shard_map/ppermute | solution.py:375
  83.9 6.0 %collective-permute-start.16 = (f32[8,8,128]{2,1,0:T(8,128)S(1)}, f32[8,8,128]{2,1,0:T(8,128)S(1)}, u32[]{:S(2)}, u32[]{:S(2)}) collective-permute-start(f32[8,8,128]{2,1,0:T(8,128)S(1)} %get-tuple-element.45.ln_ref), channel_id=1, source_target_pairs={{0,1},{1,0},{2,3},{3,2},{4,5},{5,4},{6,7},{7,6},{8,9},{9,8},{10,11... | collective-permute-start | bytes 98312 | tf_op jit(solution)/shard_map/ppermute | solution.py:379
